TPU v7x, 256 devices: a whole 4x4x8 slice. The times are simulated.
256 devices in a mesh: view: 8 (over x, core), gauss: 32 (over y, z).
Axes of the slice: x: 4, y: 4, z: 8, core: 2. Of those that a mesh axis runs over, the one named last changes fastest.
Arguments:
- means: float32 [3, 524288], P(None, 'gauss'), may hold values from -1 to 1
- scales: float32 [3, 524288], P(None, 'gauss'), may hold values from 0.05 to 0.6
- quats: float32 [4, 524288], P(None, 'gauss'), may hold values from -6 to 6
- attrs: float32 [49, 524288], P(None, 'gauss'), may hold values from -6 to 6
- grad_screen: float32 [32, 2, 524288], P('view', None, 'gauss'), may hold values from -6 to 6
- visible: int32 [32, 524288], P('view', 'gauss'), may hold values 0 or 1
- clone_mask: int32 [524288], P('gauss'), may hold values from 0 to 1, as said below
- rotation: float32 [32, 3, 3], P('view'), may hold values from -3.5 to 3.5
- shift: float32 [32, 3], P('view'), may hold values from 2 to 5
- focal: float32 [32], P('view'), may hold values from 1 to 4
Outputs:
- peak_stats: float32 [2, 524288], P(None, 'gauss')
- clones: float32 [61, 524288], P(None, 'gauss')
- clone_total: int32 [], replicated
Inputs may be any that keep to these rules, and one draw needn't show every extreme that they name: `clone_mask`: in every draw some shard of 16384 consecutive Gaussians has all of them marked.
All inputs are finite; a program needn't handle non-finite values. No bound on the sum of `visible` on one device may be relied on, other than what follows from the above.
Results may differ from a plain program's by a relative error of at most 0.0003.
Values sent between devices are 32-bit elements; how exact they have to be, the bound alone decides.
No kernel may reach another device: no remote copies, remote signals or barrier semaphores. Data moves between devices by JAX's collectives and lax.ppermute only.
A program may use at most 128 MiB of HBM per device.

v0:
```python
import jax
import jax.numpy as jnp
from jax import lax
from jax.sharding import PartitionSpec as P

G_DEV = 16384


def copy_for_each(x, axis):
    count = lax.axis_size(axis)
    return lax.all_to_all(jnp.broadcast_to(x[None], (count, *x.shape)), axis, 0, 0, tiled=True)


def of_everyone(x, axis):
    return copy_for_each(x, axis).max(axis=0)


def together(arrays, axis):
    vector, at, done = (jnp.concatenate([a.reshape(-1) for a in arrays]), 0, [])
    running = of_everyone(vector, axis)
    for a in arrays:
        done.append(running[at : at + a.size].reshape(a.shape))
        at += a.size
    return tuple(done)


def folded_in_pairs(pieces, combine):
    while len(jax.tree.leaves(pieces)[0]) > 1:
        pieces = jax.vmap(combine)(*(pieces[side::2] for side in (0, 1)))
    return pieces[0]


def prefix(x, axis, combine, identity):
    count, mine = (lax.axis_size(axis), lax.axis_index(axis))
    passed = jnp.arange(count) < mine

    def kept(part, zero, own):
        part = jnp.where(
            passed.reshape(-1, *(1 for _ in own.shape)), part, jnp.asarray(zero, own.dtype)
        )
        return part

    pieces = copy_for_each(x, axis)
    return folded_in_pairs(kept(pieces, identity, x), combine)


def of_everyone_2(x, axis):
    everything = copy_for_each(x, axis)
    return jnp.sum(everything, axis=0)


def quat_factor(scales, quats):
    inv = 1.0 / jnp.sqrt(jnp.sum(quats * quats, axis=0) + 0.25)
    w, x, y, z = (quats[0] * inv, quats[1] * inv, quats[2] * inv, quats[3] * inv)
    rq = [
        [1 - 2 * (y * y + z * z), 2 * (x * y - w * z), 2 * (x * z + w * y)],
        [2 * (x * y + w * z), 1 - 2 * (x * x + z * z), 2 * (y * z - w * x)],
        [2 * (x * z - w * y), 2 * (y * z + w * x), 1 - 2 * (x * x + y * y)],
    ]
    return [[rq[i][j] * scales[j] for j in range(3)] for i in range(3)]


def view_stats(means, factor, grad, seen, rot, trans, focal_v):
    point = [
        rot[i, 0] * means[0] + rot[i, 1] * means[1] + rot[i, 2] * means[2] + trans[i]
        for i in range(3)
    ]
    depth = jnp.maximum(point[2], 1.0)
    j00 = focal_v / depth
    j02 = -focal_v * point[0] / (depth * depth)
    j12 = -focal_v * point[1] / (depth * depth)
    first = [j00 * rot[0, j] + j02 * rot[2, j] for j in range(3)]
    second = [j00 * rot[1, j] + j12 * rot[2, j] for j in range(3)]
    prow = [sum((first[j] * factor[j][k] for j in range(3))) for k in range(3)]
    qrow = [sum((second[j] * factor[j][k] for j in range(3))) for k in range(3)]
    a_val = prow[0] ** 2 + prow[1] ** 2 + prow[2] ** 2 + 0.3
    c_val = qrow[0] ** 2 + qrow[1] ** 2 + qrow[2] ** 2 + 0.3
    b_val = prow[0] * qrow[0] + prow[1] * qrow[1] + prow[2] * qrow[2]
    half = 0.5 * (a_val - c_val)
    lam = 0.5 * (a_val + c_val) + jnp.sqrt(half * half + b_val * b_val + 0.01)
    seenf = seen.astype(jnp.float32)
    radius = 3.0 * jnp.sqrt(lam) * seenf
    gnorm = jnp.sqrt(grad[0] * grad[0] + grad[1] * grad[1]) * seenf
    return (gnorm, radius)


def add_ints(earlier, later):
    return earlier + later


def body(means, scales, quats, attrs, grad_screen, visible, clone_mask, rotation, shift, focal):
    factor = quat_factor(scales, quats)
    gmax = jnp.zeros(means.shape[1], jnp.float32)
    rmax = jnp.zeros(means.shape[1], jnp.float32)
    for v in range(grad_screen.shape[0]):
        gnorm, radius = view_stats(
            means, factor, grad_screen[v], visible[v], rotation[v], shift[v], focal[v]
        )
        gmax = jnp.maximum(gmax, gnorm)
        rmax = jnp.maximum(rmax, radius)
    gmax, rmax = together((gmax, rmax), "view")
    peak = jnp.stack([gmax, rmax])
    rows = jnp.concatenate([means, scales, quats, attrs, peak], axis=0)
    feat_rows = rows.shape[0]
    shards = lax.axis_size("gauss")
    cap_blk = G_DEV // 128
    count = jnp.sum(clone_mask)
    blocks = (count + 127) // 128
    offset = prefix(blocks, "gauss", add_ints, jnp.int32(0))
    summed = of_everyone_2(count.astype(jnp.float32), "gauss")
    total = summed.astype(jnp.int32)
    rank = jnp.cumsum(clone_mask) - 1
    where_to = jnp.where(clone_mask == 1, rank, cap_blk * 128)
    packed = (
        jnp.zeros((feat_rows, cap_blk * 128), jnp.float32).at[:, where_to].set(rows, mode="drop")
    )
    packed = packed.reshape(feat_rows, cap_blk, 128)
    per = (cap_blk + shards - 1) // shards
    target = jnp.arange(shards, dtype=jnp.int32)[:, None]
    within = jnp.arange(per, dtype=jnp.int32)[None, :]
    local_blk = (target - offset) % shards + within * shards
    valid = local_blk < blocks
    picked = jnp.minimum(local_blk, cap_blk - 1).reshape(-1)
    outgoing = packed[:, picked, :] * valid.reshape(1, -1, 1).astype(jnp.float32)
    outgoing = outgoing.reshape(feat_rows, shards, per, 128)
    slot_ids = (
        jnp.where(valid, (offset + local_blk) // shards, cap_blk)
        .astype(jnp.int32)
        .reshape(1, shards, per)
    )
    width = 128 // lax.axis_size("view")
    start = lax.axis_index("view") * width
    portion = lax.dynamic_slice_in_dim(outgoing, start, width, 3)
    arrived, slots_in = (
        lax.all_to_all(portion, "gauss", split_axis=1, concat_axis=1, tiled=True),
        lax.all_to_all(slot_ids, "gauss", split_axis=1, concat_axis=1, tiled=True),
    )
    arrived = arrived.reshape(feat_rows, shards * per, width)
    partial_place = (
        jnp.zeros((feat_rows, cap_blk, width), jnp.float32)
        .at[:, slots_in.reshape(-1)]
        .set(arrived, mode="drop")
    )
    placed = lax.all_gather(partial_place, "view", axis=2, tiled=True)
    clones = placed.reshape(feat_rows, cap_blk * 128)
    return (peak, clones, total)


def solution(mesh):
    return jax.shard_map(
        body,
        mesh=mesh,
        in_specs=(
            P(None, "gauss"),
            P(None, "gauss"),
            P(None, "gauss"),
            P(None, "gauss"),
            P("view", None, "gauss"),
            P("view", "gauss"),
            P("gauss"),
            P("view", None, None),
            P("view", None),
            P("view"),
        ),
        out_specs=(P(None, "gauss"), P(None, "gauss"), P()),
        check_vma=False,
    )
```

profile of v0, /device:TPU:1, one launch (start us, length us, event | category | flops | bytes accessed | tf_op | source)
XLA Modules:
  0.0 326.7 jit_solution(10295088173397887772)
XLA Ops:
  8.9 2.1 compare_select_fusion
  12.2 12.0 %all-to-all-start.1 = ((s32[32,1,1]{2,1,0:T(1,128)}), s32[32,1,1]{2,1,0:T(1,128)S(1)}, u32[]{:S(2)}, u32[]{:S(2)}) async-start(s32[32,1,1]{2,1,0:T(1,128)} %broadcast_in_dim.45), calls=%async_computation.1 | async-start | bytes 32768 | tf_op jit(solution)/shard_map/all_to_all | solution.py:11
  24.2 2.4 fusion.6
  29.9 1.8 fusion.11
  33.8 7.2 %multiply_add_fusion.23 = (f32[1,16384]{1,0:T(1,128)S(1)}, f32[1,16384]{1,0:T(1,128)S(1)}, f32[1,16384]{1,0:T(1,128)S(1)}, f32[1,16384]{1,0:T(1,128)S(1)}) fusion(f32[]{:T(128)} %bitcast.13, f32[]{:T(128)} %bitcast.9, f32[]{:T(128)} %bitcast.16, f32[3,16384]{1,0:T(4,128)} %param.10, f32[]{:T(128)} %bitcast.15, f32[]{:T(128)} %bitcast.14, f32[]{:T(128)S(6)} %neg.16, ...), kind=kLoop, calls=%fused_computation.35 | loop fusion | flops 327680 | bytes 458792 | tf_op jit(solution)/shard_map/add | solution.py:72
  41.1 7.3 %multiply_add_fusion.22 = (f32[1,16384]{1,0:T(1,128)S(1)}, f32[1,16384]{1,0:T(1,128)S(1)}, f32[1,16384]{1,0:T(1,128)S(1)}, f32[1,16384]{1,0:T(1,128)S(1)}) fusion(f32[1,16384]{1,0:T(1,128)S(1)} %get-tuple-element.22, f32[1,16384]{1,0:T(1,128)S(1)} %get-tuple-element.23, f32[]{:T(128)} %bitcast.14, f32[]{:T(128)} %bitcast.10, f32[]{:T(128)} %bitcast.11, ...), kind=kLoop, calls=%fused_computation.34 | loop fusion | flops 294912 | bytes 655400 | tf_op jit(solution)/shard_map/add | solution.py:72
  48.3 2.5 multiply_add_fusion.19
  52.2 7.4 %multiply_add_fusion.17 = (f32[1,16384]{1,0:T(1,128)S(1)}, f32[1,16384]{1,0:T(1,128)S(1)}, f32[1,16384]{1,0:T(1,128)S(1)}, f32[1,16384]{1,0:T(1,128)S(1)}) fusion(f32[]{:T(128)} %bitcast.39, f32[]{:T(128)} %bitcast.35, f32[]{:T(128)} %bitcast.42, f32[3,16384]{1,0:T(4,128)} %param.10, f32[]{:T(128)} %bitcast.41, f32[]{:T(128)} %bitcast.40, f32[]{:T(128)S(6)} %neg.17, ...), kind=kLoop, calls=%fused_computation.29 | loop fusion | flops 327680 | bytes 458792 | tf_op jit(solution)/shard_map/add | solution.py:72
  59.6 7.2 %multiply_add_fusion.16 = (f32[1,16384]{1,0:T(1,128)S(1)}, f32[1,16384]{1,0:T(1,128)S(1)}, f32[1,16384]{1,0:T(1,128)S(1)}, f32[1,16384]{1,0:T(1,128)S(1)}) fusion(f32[1,16384]{1,0:T(1,128)S(1)} %get-tuple-element.28, f32[1,16384]{1,0:T(1,128)S(1)} %get-tuple-element.29, f32[]{:T(128)} %bitcast.40, f32[]{:T(128)} %bitcast.36, f32[]{:T(128)} %bitcast.37, ...), kind=kLoop, calls=%fused_computation.28 | loop fusion | flops 294912 | bytes 655400 | tf_op jit(solution)/shard_map/add | solution.py:72
  66.8 2.5 multiply_add_fusion.13
  70.7 7.4 %multiply_add_fusion.11 = (f32[1,16384]{1,0:T(1,128)S(1)}, f32[1,16384]{1,0:T(1,128)S(1)}, f32[1,16384]{1,0:T(1,128)S(1)}, f32[1,16384]{1,0:T(1,128)S(1)}) fusion(f32[]{:T(128)} %bitcast.58, f32[]{:T(128)} %bitcast.54, f32[]{:T(128)} %bitcast.61, f32[3,16384]{1,0:T(4,128)} %param.10, f32[]{:T(128)} %bitcast.60, f32[]{:T(128)} %bitcast.59, f32[]{:T(128)S(6)} %neg.18, ...), kind=kLoop, calls=%fused_computation.23 | loop fusion | flops 327680 | bytes 458792 | tf_op jit(solution)/shard_map/add | solution.py:72
  78.1 7.4 %multiply_add_fusion.10 = (f32[1,16384]{1,0:T(1,128)S(1)}, f32[1,16384]{1,0:T(1,128)S(1)}, f32[1,16384]{1,0:T(1,128)S(1)}, f32[1,16384]{1,0:T(1,128)S(1)}) fusion(f32[1,16384]{1,0:T(1,128)S(1)} %get-tuple-element.34, f32[1,16384]{1,0:T(1,128)S(1)} %get-tuple-element.35, f32[]{:T(128)} %bitcast.59, f32[]{:T(128)} %bitcast.55, f32[]{:T(128)} %bitcast.56, ...), kind=kLoop, calls=%fused_computation.22 | loop fusion | flops 294912 | bytes 655400 | tf_op jit(solution)/shard_map/add | solution.py:72
  85.4 2.6 multiply_add_fusion.7
  89.4 7.4 %multiply_add_fusion.5 = (f32[1,16384]{1,0:T(1,128)S(1)}, f32[1,16384]{1,0:T(1,128)S(1)}, f32[1,16384]{1,0:T(1,128)S(1)}, f32[1,16384]{1,0:T(1,128)S(1)}) fusion(f32[]{:T(128)} %bitcast.77, f32[]{:T(128)} %bitcast.73, f32[]{:T(128)} %bitcast.80, f32[3,16384]{1,0:T(4,128)} %param.10, f32[]{:T(128)} %bitcast.79, f32[]{:T(128)} %bitcast.78, f32[]{:T(128)S(6)} %neg.19, ...), kind=kLoop, calls=%fused_computation.17 | loop fusion | flops 327680 | bytes 458792 | tf_op jit(solution)/shard_map/add | solution.py:72
  96.8 7.4 %multiply_add_fusion.4 = (f32[1,16384]{1,0:T(1,128)S(1)}, f32[1,16384]{1,0:T(1,128)S(1)}, f32[1,16384]{1,0:T(1,128)S(1)}, f32[1,16384]{1,0:T(1,128)S(1)}) fusion(f32[1,16384]{1,0:T(1,128)S(1)} %get-tuple-element.40, f32[1,16384]{1,0:T(1,128)S(1)} %get-tuple-element.41, f32[]{:T(128)} %bitcast.78, f32[]{:T(128)} %bitcast.74, f32[]{:T(128)} %bitcast.75, ...), kind=kLoop, calls=%fused_computation.16 | loop fusion | flops 294912 | bytes 655400 | tf_op jit(solution)/shard_map/add | solution.py:72
  104.2 2.6 multiply_add_fusion.1
  110.2 1.8 multiply_maximum_fusion
  113.5 5.3 %all-to-all-start = ((f32[8,1,32768]{2,1,0:T(1,128)}), f32[8,1,32768]{2,1,0:T(1,128)S(1)}, u32[]{:S(2)}, u32[]{:S(2)}) async-start(f32[8,1,32768]{2,1,0:T(1,128)} %broadcast_in_dim.24), calls=%async_computation | async-start | bytes 2097152 | tf_op jit(solution)/shard_map/all_to_all | solution.py:11
  125.2 8.5 %all-to-all-done = f32[8,1,32768]{2,1,0:T(1,128)S(1)} async-done(((f32[8,1,32768]{2,1,0:T(1,128)}), f32[8,1,32768]{2,1,0:T(1,128)S(1)}, u32[]{:S(2)}, u32[]{:S(2)}) %all-to-all-start) | async-done | bytes 1048608 | tf_op jit(solution)/shard_map/all_to_all | solution.py:11
  133.7 9.7 %all-to-all-start.2 = ((s32[1,32,4]{2,0,1:T(1,128)}), s32[1,32,4]{2,0,1:T(1,128)S(1)}, u32[]{:S(2)}, u32[]{:S(2)}) async-start(s32[1,32,4]{2,0,1:T(1,128)} %compare_select_fusion.1), calls=%async_computation.2 | async-start | bytes 32768 | tf_op jit(solution)/shard_map/all_to_all | solution.py:136
  144.2 21.5 %concatenate.8 = f32[61,16384]{1,0:T(8,128)} concatenate(f32[3,16384]{1,0:T(4,128)S(1)} %copy-done.1, f32[3,16384]{1,0:T(4,128)S(1)} %copy-done.3, f32[4,16384]{1,0:T(4,128)S(1)} %copy-done.2, f32[49,16384]{1,0:T(8,128)} %param.13, f32[1,16384]{1,0:T(1,128)S(1)} %bitcast.129, f32[1,16384]{1,0:T(1,128)S(1)} %bitcast.131), dimensions={0} | concatenate | bytes 7995392 | tf_op jit(solution)/shard_map/concatenate | solution.py:103
  165.8 6.9 %copy.40 = f32[16384,61]{1,0:T(8,128)} copy(f32[16384,61]{0,1:T(8,128)} %bitcast.126) | data formatting | bytes 7995392 | tf_op jit(solution)/shard_map/concatenate | solution.py:103
  172.7 44.3 %scatter_custom_fusion = f32[61,16384]{0,1:T(8,128)} fusion(s32[16384]{0:T(1024)} %get-tuple-element.78, f32[16384,61]{1,0:T(8,128)} %copy.40, f32[]{:T(128)} %constant.32.clone.1), kind=kCustom, calls=%fused_computation.3 | custom fusion | bytes 3998208 | tf_op jit(solution)/shard_map/scatter | solution.py:115
  217.0 7.7 %gather_fusion = f32[128,61,128]{1,2,0:T(8,128)} fusion(f32[61,128,128]{0,2,1:T(8,128)} %bitcast.125, s32[1024]{0:T(1024)S(1)} %pad_clamp_fusion), kind=kCustom, calls=%fused_computation | custom fusion | bytes 7995904 | tf_op jit(solution)/shard_map/gather | solution.py:124
  226.2 2.3 reshape.640
  228.5 9.1 %all-to-all-start.3 = ((f32[32,1,3904]{2,1,0:T(1,128)}), f32[32,1,3904]{2,1,0:T(1,128)S(1)}, u32[]{:S(2)}, u32[]{:S(2)}) async-start(f32[32,1,3904]{2,1,0:T(1,128)} %reshape.640), calls=%async_computation.3 | async-start | bytes 1015808 | tf_op jit(solution)/shard_map/all_to_all | solution.py:135
  238.9 11.3 %all-to-all-done.3 = f32[32,1,3904]{2,1,0:T(1,128)S(1)} async-done(((f32[32,1,3904]{2,1,0:T(1,128)}), f32[32,1,3904]{2,1,0:T(1,128)S(1)}, u32[]{:S(2)}, u32[]{:S(2)}) %all-to-all-start.3) | async-done | bytes 499744 | tf_op jit(solution)/shard_map/all_to_all | solution.py:135
  250.8 1.8 reduce.9
  254.2 4.5 %scatter_fusion = f32[61,128,16]{0,2,1:T(8,128)S(1)} fusion(f32[61,128,16]{0,2,1:T(8,128)S(1)} %broadcast_in_dim.44, s32[128]{0:T(128)S(1)} %fusion.4, f32[128,61,16]{1,2,0:T(8,128)S(1)} %bitcast.124), kind=kCustom, calls=%fused_computation.2 | custom fusion | bytes 1499648 | tf_op jit(solution)/shard_map/scatter | solution.py:142
  260.3 16.9 %all_to_all.31 = f32[32,1,1]{2,1,0:T(1,128)S(1)} all-to-all(f32[32,1,1]{2,1,0:T(1,128)S(1)} %broadcast_in_dim.51), channel_id=1, replica_groups=mesh['view'=8,'gauss'=32] {'gauss'}, dimensions={0} | all-to-all | bytes 256 | tf_op jit(solution)/shard_map/all_to_all | solution.py:11
  279.3 32.5 %all-gather.2.cloned.1.call-done = f32[61,128,128]{0,2,1:T(8,128)} async-done(((f32[61,128,16]{0,2,1:T(8,128)}), f32[61,128,128]{0,2,1:T(8,128)}) %all-gather.2.cloned.1.call-update) | async-done | bytes 3997712 | tf_op jit(solution)/shard_map/all_gather | solution.py:144
  311.8 6.8 %copy.42 = f32[61,16384]{1,0:T(8,128)} copy(f32[61,16384]{0,1:T(8,128)} %bitcast.127) | data formatting | bytes 7995392
  (74 shorter events, 27.1 us)
Async XLA Ops:
  7.2 101.4 %copy-start.3 = (f32[3,16384]{1,0:T(4,128)S(1)}, f32[3,16384]{1,0:T(4,128)}, u32[]{:S(2)}) copy-start(f32[3,16384]{1,0:T(4,128)} %param.11) | copy-start | bytes 589828
  7.2 102.1 %copy-start.4 = (f32[4,2,16384]{2,1,0:T(2,128)S(1)}, f32[4,2,16384]{2,1,0:T(2,128)}, u32[]{:S(2)}) copy-start(f32[4,2,16384]{2,1,0:T(2,128)} %param.14) | copy-start | bytes 1572868
  12.2 99.8 %all-to-all-start.1 = ((s32[32,1,1]{2,1,0:T(1,128)}), s32[32,1,1]{2,1,0:T(1,128)S(1)}, u32[]{:S(2)}, u32[]{:S(2)}) async-start(s32[32,1,1]{2,1,0:T(1,128)} %broadcast_in_dim.45), calls=%async_computation.1 | async-start | bytes 32768 | tf_op jit(solution)/shard_map/all_to_all | solution.py:11
  24.2 120.0 %copy-start.1 = (f32[3,16384]{1,0:T(4,128)S(1)}, f32[3,16384]{1,0:T(4,128)}, u32[]{:S(2)}) copy-start(f32[3,16384]{1,0:T(4,128)} %param.10) | copy-start | bytes 589828
  24.2 120.0 %copy-start.2 = (f32[4,16384]{1,0:T(4,128)S(1)}, f32[4,16384]{1,0:T(4,128)}, u32[]{:S(2)}) copy-start(f32[4,16384]{1,0:T(4,128)} %param.12) | copy-start | bytes 786436
  113.5 20.2 %all-to-all-start = ((f32[8,1,32768]{2,1,0:T(1,128)}), f32[8,1,32768]{2,1,0:T(1,128)S(1)}, u32[]{:S(2)}, u32[]{:S(2)}) async-start(f32[8,1,32768]{2,1,0:T(1,128)} %broadcast_in_dim.24), calls=%async_computation | async-start | bytes 2097152 | tf_op jit(solution)/shard_map/all_to_all | solution.py:11
  133.7 94.8 %all-to-all-start.2 = ((s32[1,32,4]{2,0,1:T(1,128)}), s32[1,32,4]{2,0,1:T(1,128)S(1)}, u32[]{:S(2)}, u32[]{:S(2)}) async-start(s32[1,32,4]{2,0,1:T(1,128)} %compare_select_fusion.1), calls=%async_computation.2 | async-start | bytes 32768 | tf_op jit(solution)/shard_map/all_to_all | solution.py:136
  228.5 21.8 %all-to-all-start.3 = ((f32[32,1,3904]{2,1,0:T(1,128)}), f32[32,1,3904]{2,1,0:T(1,128)S(1)}, u32[]{:S(2)}, u32[]{:S(2)}) async-start(f32[32,1,3904]{2,1,0:T(1,128)} %reshape.640), calls=%async_computation.3 | async-start | bytes 1015808 | tf_op jit(solution)/shard_map/all_to_all | solution.py:135
  237.6 74.3 %all-gather.2.cloned.1.call-start = ((), (), s32[]{:S(2)}) async-start(), calls=%async_computation.5 | async-start | bytes 9437184 | tf_op jit(solution)/shard_map/all_gather | solution.py:144
  258.8 1.0 copy-start
Sparse Core Ops, SparseCore 0:
  259.9 51.9 all-gather.1
where the time goes:
time: 329 us; the launch traced here: 327 us
  local copies, waits for them, and re-layouts  113 us (34%)
  other arithmetic  87.1 us (26%)
  waiting for transfers between devices  52.4 us (16%)
  starting transfers between devices  36.1 us (11%)
  between operations  21.3 us (6%)
  blocking collectives  16.9 us (5%)
    add x8, other arithmetic, view_stats(): first = [j00 * rot[0, j] + j02 * rot[2, j] for j in range(3)]  58.6 us
    scatter x1, local copies, waits for them, and re-layouts, body(): jnp.zeros((feat_rows, cap_blk * 128), jnp.float32).at[:, where_to]  44.3 us
    all_gather x1, waiting for transfers between devices, body(): placed = lax.all_gather(partial_place, 'view', axis=2, tiled=True)  32.5 us
    concatenate x2, local copies, waits for them, and re-layouts, body(): rows = jnp.concatenate([means, scales, quats, attrs, peak], axis=0)  28.5 us
    all_to_all x2, starting transfers between devices, copy_for_each(): lax.all_to_all(jnp.broadcast_to(x[None], (count, *x.shape)), axis, 0, 0,...  17.3 us
    all_to_all x1, blocking collectives, copy_for_each(): lax.all_to_all(jnp.broadcast_to(x[None], (count, *x.shape)), axis, 0, 0,...  16.9 us
    unnamed x15, local copies, waits for them, and re-layouts  11.7 us
    all_to_all x1, waiting for transfers between devices, body(): lax.all_to_all(portion, 'gauss', split_axis=1, concat_axis=1, tiled=True)  11.3 us
  transfers between devices with their start and end apart: 5, of which 3 were waited for; matrix products, arithmetic and copies ran while one was open for 54% of the time, Pallas kernels for 0%

commit v1 on v0

v1 whole, which is shorter than its diff:
```python
import jax
import jax.numpy as jnp
from jax import lax
from jax.experimental import pallas as pl
from jax.experimental.pallas import tpu as pltpu
from jax.sharding import PartitionSpec as P

G_DEV = 16384
LANES = 128
BLOCKS = G_DEV // LANES
SHARDS = 32
PER = BLOCKS // SHARDS
VIEWS_DEV = 4
ROWS = 61
SMEM = pltpu.MemorySpace.SMEM
VMEM = pltpu.MemorySpace.VMEM


def dot(a, b, dims=((1,), (0,))):
    return lax.dot_general(a, b, (dims, ((), ())), preferred_element_type=jnp.float32)


def index_kernel(mask_ref, count_ref, start_ref, index_ref):
    marked = mask_ref[...]
    ones = marked.astype(jnp.float32).astype(jnp.bfloat16)
    row = lax.broadcasted_iota(jnp.int32, (LANES, LANES), 0)
    lane = lax.broadcasted_iota(jnp.int32, (LANES, LANES), 1)
    full = jnp.ones((LANES, LANES), jnp.bfloat16)

    def where_1(cond):
        return jnp.where(cond, 1.0, 0.0).astype(jnp.bfloat16)

    inclusive = dot(ones, where_1(row <= lane)).astype(jnp.int32)
    in_row = dot(ones, full)
    start = dot(where_1(row > lane), in_row.astype(jnp.bfloat16)).astype(jnp.int32)
    in_row_t = dot(jnp.ones((8, LANES), jnp.bfloat16), ones, ((1,), (1,)))
    in_row_tb = in_row_t.astype(jnp.bfloat16)
    start_ref[...] = dot(in_row_tb, where_1(row < lane)).astype(jnp.int32)
    total = dot(in_row_tb, full).astype(jnp.int32)
    for i in range(SHARDS // 8):
        count_ref[8 * i : 8 * i + 8, :] = total

    moves = lane - inclusive + 1
    code = jnp.where(marked == 1, moves * 256 + lane, 0)
    for bit in range(7):
        moved = pltpu.roll(code, LANES - (1 << bit), 1)
        take = ((moved >> (8 + bit)) & 1) == 1
        leave = ((code >> (8 + bit)) & 1) == 1
        code = jnp.where(take, moved, jnp.where(leave, 0, code))
    first = start & (LANES - 1)
    nth = (lane - first) & (LANES - 1)
    source = jnp.take_along_axis(
        code & (LANES - 1), nth, axis=1, mode="promise_in_bounds"
    )
    valid = nth < in_row.astype(jnp.int32)
    here = jnp.where(valid, jnp.where(lane >= first, 256, 512), 0)
    index_ref[...] = source + here


def view_kernel(rot, trans, focal, means, scales, quats, grad, seen, out_ref, scr):
    width = 23

    def group(g, carry):
        for j in range(8):
            col = pl.ds(pl.multiple_of(g * 1024 + j * LANES, LANES), LANES)
            base = j * width
            scr[base : base + 3, :] = means[:, col]
            scr[base + 3 : base + 6, :] = scales[:, col]
            scr[base + 6 : base + 10, :] = quats[:, col]
            for v in range(VIEWS_DEV):
                scr[base + 10 + 2 * v : base + 12 + 2 * v, :] = grad[v, :, col]
            scr[base + 18 : base + 22, :] = seen[:, col].astype(jnp.float32)

        def comp(r):
            return scr[pl.ds(r, 8, stride=width), :]

        m = [comp(i) for i in range(3)]
        sc = [comp(3 + i) for i in range(3)]
        q = [comp(6 + i) for i in range(4)]
        norm = q[0] * q[0] + q[1] * q[1] + q[2] * q[2] + q[3] * q[3]
        inv = 1.0 / jnp.sqrt(norm + 0.25)
        w, x, y, z = (c * inv for c in q)
        rq = [
            [1 - 2 * (y * y + z * z), 2 * (x * y - w * z), 2 * (x * z + w * y)],
            [2 * (x * y + w * z), 1 - 2 * (x * x + z * z), 2 * (y * z - w * x)],
            [2 * (x * z - w * y), 2 * (y * z + w * x), 1 - 2 * (x * x + y * y)],
        ]
        factor = [[rq[i][j] * sc[j] for j in range(3)] for i in range(3)]
        gmax = jnp.zeros((8, LANES), jnp.float32)
        lmax = jnp.zeros((8, LANES), jnp.float32)
        for v in range(VIEWS_DEV):
            r = [[rot[v, 3 * i + j] for j in range(3)] for i in range(3)]
            f = focal[0, v]
            p = [r[i][0] * m[0] + r[i][1] * m[1] + r[i][2] * m[2] + trans[v, i] for i in range(3)]
            over = 1.0 / jnp.maximum(p[2], 1.0)
            j00 = f * over
            j02 = -(j00 * p[0]) * over
            j12 = -(j00 * p[1]) * over
            first = [j00 * r[0][j] + j02 * r[2][j] for j in range(3)]
            second = [j00 * r[1][j] + j12 * r[2][j] for j in range(3)]
            pr = [sum(first[j] * factor[j][k] for j in range(3)) for k in range(3)]
            qr = [sum(second[j] * factor[j][k] for j in range(3)) for k in range(3)]
            a = pr[0] * pr[0] + pr[1] * pr[1] + pr[2] * pr[2] + 0.3
            c = qr[0] * qr[0] + qr[1] * qr[1] + qr[2] * qr[2] + 0.3
            b = pr[0] * qr[0] + pr[1] * qr[1] + pr[2] * qr[2]
            half = 0.5 * (a - c)
            lam = 0.5 * (a + c) + jnp.sqrt(half * half + b * b + 0.01)
            vis = comp(18 + v)
            g0 = comp(10 + 2 * v)
            g1 = comp(11 + 2 * v)
            gmax = jnp.maximum(gmax, (g0 * g0 + g1 * g1) * vis)
            lmax = jnp.maximum(lmax, lam * vis)
        rows = pl.ds(pl.multiple_of(g * 8, 8), 8)
        out_ref[0, rows, :] = gmax
        out_ref[1, rows, :] = lmax
        return carry

    lax.fori_loop(0, G_DEV // 1024, group, 0)


def blocks_before(counts, upto):
    total = jnp.int32(0)
    for t in range(SHARDS):
        total = total + jnp.where(t < upto, (counts[t, 0] + LANES - 1) // LANES, 0)
    return total


def pack_kernel(
    where, counts, start, index, squares, means, scales, quats, low, high, out_ref, peak_ref, rows
):
    view = where[0]
    g_of = lax.broadcasted_iota(jnp.int32, (8, LANES), 0)
    for g in range(BLOCKS // 8):
        norm = jnp.sqrt(squares[0, 8 * g : 8 * g + 8, :])
        radius = 3.0 * jnp.sqrt(squares[1, 8 * g : 8 * g + 8, :])
        for j in range(8):
            col = slice((8 * g + j) * LANES, (8 * g + j + 1) * LANES)
            peak_ref[0:1, col] = norm[j : j + 1, :]
            peak_ref[1:2, col] = radius[j : j + 1, :]

    @pl.when(view == 0)
    def _():
        rows[0:3, :] = means[...]
        rows[3:6, :] = scales[...]
        rows[6:8, :] = quats[0:2, :]

    @pl.when(view == 1)
    def _():
        rows[0:2, :] = quats[2:4, :]

    @pl.when(view > 1)
    def _():
        rows[0:2, :] = low[6:8, :]

    @pl.when((view > 0) & (view < 7))
    def _():
        rows[2:8, :] = high[0:6, :]

    @pl.when(view == 7)
    def _():
        rows[2:3, :] = high[0:1, :]
        rows[3:5, :] = peak_ref[...]
        rows[5:8, :] = jnp.zeros((3, G_DEV), jnp.float32)

    offset = blocks_before(counts, where[1])
    zero = jnp.zeros((8, LANES), jnp.float32)
    for i in range(BLOCKS):
        out_ref[i] = zero

    def place_of(block):
        return ((offset + block) & (SHARDS - 1)) * PER + (block >> 5)

    def eight(i, carry):
        for j in range(8):
            b = i * 8 + j
            block = start[0, b] >> 7
            code = jnp.broadcast_to(index[pl.ds(b, 1), :], (8, LANES))
            tile = rows[:, pl.ds(pl.multiple_of(b * LANES, LANES), LANES)]
            packed = jnp.take_along_axis(
                tile, code & (LANES - 1), axis=1, mode="promise_in_bounds"
            )
            pltpu.store(out_ref.at[place_of(block)], packed, mask=(code & 256) != 0)
            after = jnp.minimum(block + 1, BLOCKS - 1)
            pltpu.store(out_ref.at[place_of(after)], packed, mask=(code & 512) != 0)
        return carry

    lax.fori_loop(0, BLOCKS // 8, eight, 0)


def place_kernel(where, counts, arrived, out_ref, slots):
    cap = out_ref.shape[1]
    mine = where[1]
    zero = jnp.zeros((8, LANES), jnp.float32)
    for i in range(cap):
        slots[i] = zero
    before = jnp.int32(0)
    for s in range(SHARDS):
        local = (mine - before) & (SHARDS - 1)
        first = (before + local) >> 5
        for w in range(PER):
            slots[jnp.minimum(first + w, cap)] = arrived[s * PER + w]
        before = before + (counts[s, 0] + LANES - 1) // LANES
    for i in range(cap):
        tile = slots[i]
        for x in range(4):
            out_ref[x, i] = tile


def join_kernel(where, own, other, out_ref):
    cap = own.shape[1]
    core = where[0] & 1
    mine = pl.ds(pl.multiple_of(8 * core, 8), 8)
    theirs = pl.ds(pl.multiple_of(8 - 8 * core, 8), 8)
    for i in range(BLOCKS):
        col = slice(i * LANES, (i + 1) * LANES)
        if i < cap:
            out_ref[mine, col] = own[0, i]
            out_ref[theirs, col] = other[0, i]
        else:
            out_ref[:, col] = jnp.zeros((16, LANES), jnp.float32)


def smem():
    return pl.BlockSpec(memory_space=SMEM)


def vmem():
    return pl.BlockSpec(memory_space=VMEM)


def body(means, scales, quats, attrs, grad_screen, visible, clone_mask, rotation, shift, focal):
    f32, i32 = jnp.float32, jnp.int32
    view = lax.axis_index("view")
    where = jnp.stack([view, lax.axis_index("gauss")]).astype(i32)

    count, start, index = pl.pallas_call(
        index_kernel,
        in_specs=[vmem()],
        out_specs=[vmem()] * 3,
        out_shape=[
            jax.ShapeDtypeStruct((SHARDS, LANES), i32),
            jax.ShapeDtypeStruct((8, LANES), i32),
            jax.ShapeDtypeStruct((BLOCKS, LANES), i32),
        ],
        name="index",
    )(clone_mask.reshape(BLOCKS, LANES))
    counts = lax.all_to_all(count, "gauss", 0, 0, tiled=True)

    squares = pl.pallas_call(
        view_kernel,
        in_specs=[smem()] * 3 + [vmem()] * 5,
        out_specs=vmem(),
        out_shape=jax.ShapeDtypeStruct((2, BLOCKS, LANES), f32),
        scratch_shapes=[pltpu.VMEM((192, LANES), f32)],
        name="views",
    )(
        rotation.reshape(VIEWS_DEV, 9),
        shift,
        focal.reshape(1, VIEWS_DEV),
        means,
        scales,
        quats,
        grad_screen,
        visible,
    )
    for k in (1, 2, 4):
        pairs = [(v, v ^ k) for v in range(8)]
        squares = jnp.maximum(squares, lax.ppermute(squares, "view", pairs))

    def whole(*shape):
        return pl.BlockSpec(shape, lambda i, w: (0,) * len(shape))

    outgoing, peak = pl.pallas_call(
        pack_kernel,
        grid_spec=pltpu.PrefetchScalarGridSpec(
            num_scalar_prefetch=1,
            grid=(1,),
            in_specs=[
                smem(),
                smem(),
                whole(BLOCKS, LANES),
                whole(2, BLOCKS, LANES),
                whole(3, G_DEV),
                whole(3, G_DEV),
                whole(4, G_DEV),
                pl.BlockSpec((8, G_DEV), lambda i, w: (jnp.maximum(w[0] - 2, 0), 0)),
                pl.BlockSpec((8, G_DEV), lambda i, w: (jnp.maximum(w[0] - 1, 0), 0)),
            ],
            out_specs=[whole(BLOCKS, 8, LANES), whole(2, G_DEV)],
            scratch_shapes=[pltpu.VMEM((8, G_DEV), f32)],
        ),
        out_shape=[
            jax.ShapeDtypeStruct((BLOCKS, 8, LANES), f32),
            jax.ShapeDtypeStruct((2, G_DEV), f32),
        ],
        name="pack",
    )(where, counts, start, index, squares, means, scales, quats, attrs, attrs)

    arrived = lax.all_to_all(
        outgoing.reshape(SHARDS, PER, 8, LANES), "gauss", 0, 0, tiled=True
    ).reshape(BLOCKS, 8, LANES)

    cap = BLOCKS
    piece = pl.pallas_call(
        place_kernel,
        in_specs=[smem(), smem(), vmem()],
        out_specs=vmem(),
        out_shape=jax.ShapeDtypeStruct((4, cap, 8, LANES), f32),
        scratch_shapes=[pltpu.VMEM((cap + 1, 8, LANES), f32)],
        name="place",
    )(where, counts, arrived)
    cores = [[0, 2, 4, 6], [1, 3, 5, 7]]
    own = lax.all_to_all(piece, "view", 0, 0, axis_index_groups=cores, tiled=True)
    other = lax.ppermute(own, "view", [(v, v ^ 1) for v in range(8)])
    clones = pl.pallas_call(
        join_kernel,
        grid_spec=pltpu.PrefetchScalarGridSpec(
            num_scalar_prefetch=1,
            grid=(4,),
            in_specs=[
                pl.BlockSpec((1, cap, 8, LANES), lambda i, w: (i, 0, 0, 0)),
                pl.BlockSpec((1, cap, 8, LANES), lambda i, w: (i, 0, 0, 0)),
            ],
            out_specs=pl.BlockSpec((16, G_DEV), lambda i, w: (i, 0)),
        ),
        out_shape=jax.ShapeDtypeStruct((ROWS, G_DEV), f32),
        name="join",
    )(where, own, other)
    return (peak, clones, jnp.sum(counts[:, 0]))


def solution(mesh):
    return jax.shard_map(
        body,
        mesh=mesh,
        in_specs=(
            P(None, "gauss"),
            P(None, "gauss"),
            P(None, "gauss"),
            P(None, "gauss"),
            P("view", None, "gauss"),
            P("view", "gauss"),
            P("gauss"),
            P("view", None, None),
            P("view", None),
            P("view"),
        ),
        out_specs=(P(None, "gauss"), P(None, "gauss"), P()),
        check_vma=False,
    )
```

time: 329 us -> 107 us (0.33)
  local copies, waits for them, and re-layouts: 113 us -> 1.96 us
  other arithmetic: 87.1 us -> 2.82 us
  waiting for transfers between devices: 52.4 us -> 16.5 us
  blocking collectives: 16.9 us -> 41.7 us
  between operations: 21.3 us -> 0.67 us
  Pallas kernels: 0 us -> 19.5 us
  starting transfers between devices: 36.1 us -> 21.8 us
    add x16 -> x0, other arithmetic: 68.8 us -> none  [the longest x8 58.6 us: view_stats(): first = [j00 * rot[0, j] + j02 * rot[2, j] for j in range(3)]]
    scatter x2 -> x0, local copies, waits for them, and re-layouts: 48.8 us -> none  [the longest x1 44.3 us: body(): jnp.zeros((feat_rows, cap_blk * 128), jnp.float32).at[:, where_to]]
    all_gather x1 -> x0, waiting for transfers between devices: 32.5 us -> none  [body(): placed = lax.all_gather(partial_place, 'view', axis=2, tiled=True)]
    concatenate x2 -> x0, local copies, waits for them, and re-layouts: 28.5 us -> none  [body(): rows = jnp.concatenate([means, scales, quats, attrs, peak], axis=0)]
    all_to_all x4 -> x1, starting transfers between devices: 36 us -> 11.2 us  [body(): counts = lax.all_to_all(count, 'gauss', 0, 0, tiled=True)]
    all_to_all x1 -> x2, blocking collectives: 16.9 us -> 41.7 us  [the longest x1 24.8 us: body(): lax.all_to_all(piece, 'view', 0, 0, axis_index_groups=cores, tiled=True)]
    pallas_call x0 -> x5, Pallas kernels: none -> 19.5 us  [the longest x1 5.36 us: body(): pl.pallas_call(join_kernel, grid_spec=pltpu.PrefetchScalarGridSpec(num_sc...]
    all_to_all x4 -> x1, waiting for transfers between devices: 19.8 us -> 7.34 us  [body(): counts = lax.all_to_all(count, 'gauss', 0, 0, tiled=True)]
  transfers between devices with their start and end apart: 5 -> 5, of which waited for: 3 -> 4; matrix products, arithmetic and copies ran while one was open for 54% -> 2% of each run, Pallas kernels for 0% -> 2%
where the time goes in v1:
time: 107 us; the launch traced here: 105 us
  blocking collectives  41.7 us (39%)
  starting transfers between devices  21.8 us (20%)
  Pallas kernels  19.5 us (18%)
  waiting for transfers between devices  16.5 us (15%)
  other arithmetic  2.82 us (3%)
  local copies, waits for them, and re-layouts  1.96 us (2%)
    all_to_all x1, blocking collectives, body(): lax.all_to_all(piece, 'view', 0, 0, axis_index_groups=cores, tiled=True)  24.8 us
    all_to_all x1, blocking collectives, body(): lax.all_to_all(outgoing.reshape(SHARDS, PER, 8, LANES), 'gauss', 0, 0, ti...  16.9 us
    all_to_all x1, starting transfers between devices, body(): counts = lax.all_to_all(count, 'gauss', 0, 0, tiled=True)  11.2 us
    all_to_all x1, waiting for transfers between devices, body(): counts = lax.all_to_all(count, 'gauss', 0, 0, tiled=True)  7.34 us
    ppermute x1, starting transfers between devices, body(): other = lax.ppermute(own, 'view', [(v, v ^ 1) for v in range(8)])  6.19 us
    ppermute x3, waiting for transfers between devices, body(): squares = jnp.maximum(squares, lax.ppermute(squares, 'view', pairs))  5.88 us
    pallas_call x1, Pallas kernels, body(): pl.pallas_call(join_kernel, grid_spec=pltpu.PrefetchScalarGridSpec(num_sc...  5.36 us
    pallas_call x1, Pallas kernels, body(): pl.pallas_call(pack_kernel, grid_spec=pltpu.PrefetchScalarGridSpec(num_sc...  4.89 us
  transfers between devices with their start and end apart: 5, of which 4 were waited for; matrix products, arithmetic and copies ran while one was open for 2% of the time, Pallas kernels for 2%

profile of v1, /device:TPU:1, one launch (start us, length us, event | category | flops | bytes accessed | tf_op | source)
XLA Modules:
  0.0 104.9 jit_solution(16192988414498482074)
XLA Ops:
  0.6 0.7 copy.16
  1.3 0.7 reshape.24.rot
  2.0 4.2 %views.1 = f32[2,128,128]{2,1,0:T(8,128)} custom-call(f32[4,9]{1,0:T(4,128)} %reshape.24.rot, f32[4,3]{1,0:T(4,128)} %trans.1, f32[1,4]{1,0:T(1,128)} %bitcast.17, f32[3,16384]{1,0:T(4,128)} %means.3, f32[3,16384]{1,0:T(4,128)} %scales.3, f32[4,16384]{1,0:T(4,128)} %quats.3, f32[4,2,16384]{2,1,0:T(2,128)} %grad.1, s32[4,16384]{1,0:T(4,128)} %seen.1), custom_call_target="tpu_custom_call" | custom-call | tf_op jit(solution)/shard_map/views/pallas_call | solution.py:249
  6.2 3.2 %collective-permute-start = (f32[2,128,128]{2,1,0:T(8,128)}, f32[2,128,128]{2,1,0:T(8,128)S(1)}, u32[]{:S(2)}, u32[]{:S(2)}) collective-permute-start(f32[2,128,128]{2,1,0:T(8,128)} %views.1), channel_id=1, source_target_pairs={{0,32},{32,0},{64,96},{96,64},{128,160},{160,128},{192,224},{224,1... | collective-permute-start | bytes 393224 | tf_op jit(solution)/shard_map/ppermute | solution.py:268
  9.4 1.2 %collective-permute-done = f32[2,128,128]{2,1,0:T(8,128)S(1)} collective-permute-done((f32[2,128,128]{2,1,0:T(8,128)}, f32[2,128,128]{2,1,0:T(8,128)S(1)}, u32[]{:S(2)}, u32[]{:S(2)}) %collective-permute-start) | collective-permute-done | bytes 131104 | tf_op jit(solution)/shard_map/ppermute | solution.py:268
  10.6 0.9 max.9
  11.5 0.1 collective-permute-start.1
  11.6 4.7 %collective-permute-done.1 = f32[2,128,128]{2,1,0:T(8,128)S(1)} collective-permute-done((f32[2,128,128]{2,1,0:T(8,128)S(1)}, f32[2,128,128]{2,1,0:T(8,128)S(1)}, u32[]{:S(2)}, u32[]{:S(2)}) %collective-permute-start.1) | collective-permute-done | bytes 131104 | tf_op jit(solution)/shard_map/ppermute | solution.py:268
  16.3 1.1 %collective-permute-start.2 = (f32[2,128,128]{2,1,0:T(8,128)S(1)}, f32[2,128,128]{2,1,0:T(8,128)S(1)}, u32[]{:S(2)}, u32[]{:S(2)}) collective-permute-start(f32[2,128,128]{2,1,0:T(8,128)S(1)} %max.10), channel_id=1, source_target_pairs={{0,128},{32,160},{64,192},{96,224},{128,0},{160,32},{192,64},{224,... | collective-permute-start | bytes 393224 | tf_op jit(solution)/shard_map/ppermute | solution.py:268
  17.4 2.2 %index.1 = (s32[32,128]{1,0:T(8,128)}, s32[8,128]{1,0:T(8,128)}, s32[128,128]{1,0:T(8,128)}) custom-call(s32[128,128]{1,0:T(8,128)} %bitcast.15), custom_call_target="tpu_custom_call" | custom-call | tf_op jit(solution)/shard_map/index/pallas_call | solution.py:236
  19.6 11.2 %all-to-all-start = ((s32[32,1,128]{2,1,0:T(1,128)}), s32[32,1,128]{2,1,0:T(1,128)S(1)}, u32[]{:S(2)}, u32[]{:S(2)}) async-start(s32[32,1,128]{2,1,0:T(1,128)} %bitcast.16), calls=%async_computation | async-start | bytes 32768 | tf_op jit(solution)/shard_map/all_to_all | solution.py:247
  30.9 0.6 pad_add_fusion.where
  31.4 0.0 collective-permute-done.2
  31.4 0.7 max.11.squares
  32.1 7.3 %all-to-all-done = s32[32,1,128]{2,1,0:T(1,128)S(1)} async-done(((s32[32,1,128]{2,1,0:T(1,128)}), s32[32,1,128]{2,1,0:T(1,128)S(1)}, u32[]{:S(2)}, u32[]{:S(2)}) %all-to-all-start) | async-done | bytes 16416 | tf_op jit(solution)/shard_map/all_to_all | solution.py:247
  39.4 0.0 copy-start.1
  39.4 0.6 copy-done.1
  40.0 4.9 %pack.1 = (f32[128,8,128]{2,1,0:T(8,128)}, f32[2,16384]{1,0:T(2,128)}) custom-call(s32[2]{0:T(128)} %pad_add_fusion.where, s32[32,128]{1,0:T(8,128)} %bitcast.12, s32[8,128]{1,0:T(8,128)} %get-tuple-element.9.start, s32[128,128]{1,0:T(8,128)} %get-tuple-element.10.index, f32[2,128,128]{2,1,0:T(8,128)} %max.11.squares, f32[3,16384]{1,0:T(4,128)} %means.3, ...), custom_call_target="tpu_custom_call" | custom-call | tf_op jit(solution)/shard_map/pack/pallas_call | solution.py:273
  44.9 16.9 %all_to_all.21 = f32[32,4,8,128]{3,2,1,0:T(8,128)} all-to-all(f32[32,4,8,128]{3,2,1,0:T(8,128)} %bitcast.11), channel_id=1, replica_groups=mesh['view'=8,'gauss'=32] {'gauss'}, dimensions={0} | all-to-all | bytes 1048576 | tf_op jit(solution)/shard_map/all_to_all | solution.py:299
  61.8 2.9 %place.1 = f32[4,128,8,128]{3,2,1,0:T(8,128)} custom-call(s32[2]{0:T(128)} %pad_add_fusion.where, s32[32,128]{1,0:T(8,128)} %bitcast.13, f32[128,8,128]{2,1,0:T(8,128)} %bitcast.10), custom_call_target="tpu_custom_call" | custom-call | tf_op jit(solution)/shard_map/place/pallas_call | solution.py:304
  64.7 0.0 copy-start.2
  64.7 24.8 %all_to_all.22.own = f32[4,128,8,128]{3,2,1,0:T(8,128)S(1)} all-to-all(f32[4,128,8,128]{3,2,1,0:T(8,128)} %place.1), channel_id=1, replica_groups={{0,64,128,192},{32,96,160,224},{1,65,129,193},{33,97,161,225},{2,66,130..., dimensions={0} | all-to-all | bytes 4194304 | tf_op jit(solution)/shard_map/all_to_all | solution.py:313
  89.5 0.0 copy-start
  89.5 6.2 %collective-permute-start.3 = (f32[4,128,8,128]{3,2,1,0:T(8,128)S(1)}, f32[4,128,8,128]{3,2,1,0:T(8,128)}, u32[]{:S(2)}, u32[]{:S(2)}) collective-permute-start(f32[4,128,8,128]{3,2,1,0:T(8,128)S(1)} %all_to_all.22.own), channel_id=1, source_target_pairs={{0,32},{32,0},{64,96},{96,64},{128,160},{160,128},{192,224},{224,1... | collective-permute-start | bytes 6291464 | tf_op jit(solution)/shard_map/ppermute | solution.py:314
  95.7 0.0 copy-done.2
  95.7 0.6 slice_reduce_fusion
  96.3 3.3 %collective-permute-done.3.other = f32[4,128,8,128]{3,2,1,0:T(8,128)} collective-permute-done((f32[4,128,8,128]{3,2,1,0:T(8,128)S(1)}, f32[4,128,8,128]{3,2,1,0:T(8,128)}, u32[]{:S(2)}, u32[]{:S(2)}) %collective-permute-start.3) | collective-permute-done | bytes 2097184 | tf_op jit(solution)/shard_map/ppermute | solution.py:314
  99.6 0.0 copy-done
  99.6 5.4 %join.1 = f32[61,16384]{1,0:T(8,128)} custom-call(s32[2]{0:T(128)} %pad_add_fusion.where, f32[4,128,8,128]{3,2,1,0:T(8,128)} %copy-done, f32[4,128,8,128]{3,2,1,0:T(8,128)} %collective-permute-done.3.other), custom_call_target="tpu_custom_call" | custom-call | tf_op jit(solution)/shard_map/join/pallas_call | solution.py:315
  (1 shorter events, 0.0 us)
Async XLA Ops:
  6.2 4.4 %collective-permute-start = (f32[2,128,128]{2,1,0:T(8,128)}, f32[2,128,128]{2,1,0:T(8,128)S(1)}, u32[]{:S(2)}, u32[]{:S(2)}) collective-permute-start(f32[2,128,128]{2,1,0:T(8,128)} %views.1), channel_id=1, source_target_pairs={{0,32},{32,0},{64,96},{96,64},{128,160},{160,128},{192,224},{224,1... | collective-permute-start | bytes 393224 | tf_op jit(solution)/shard_map/ppermute | solution.py:268
  11.5 4.8 %collective-permute-start.1 = (f32[2,128,128]{2,1,0:T(8,128)S(1)}, f32[2,128,128]{2,1,0:T(8,128)S(1)}, u32[]{:S(2)}, u32[]{:S(2)}) collective-permute-start(f32[2,128,128]{2,1,0:T(8,128)S(1)} %max.9), channel_id=1, source_target_pairs={{0,64},{32,96},{64,0},{96,32},{128,192},{160,224},{192,128},{224,1... | collective-permute-start | bytes 393224 | tf_op jit(solution)/shard_map/ppermute | solution.py:268
  16.3 15.1 %collective-permute-start.2 = (f32[2,128,128]{2,1,0:T(8,128)S(1)}, f32[2,128,128]{2,1,0:T(8,128)S(1)}, u32[]{:S(2)}, u32[]{:S(2)}) collective-permute-start(f32[2,128,128]{2,1,0:T(8,128)S(1)} %max.10), channel_id=1, source_target_pairs={{0,128},{32,160},{64,192},{96,224},{128,0},{160,32},{192,64},{224,... | collective-permute-start | bytes 393224 | tf_op jit(solution)/shard_map/ppermute | solution.py:268
  19.6 19.8 %all-to-all-start = ((s32[32,1,128]{2,1,0:T(1,128)}), s32[32,1,128]{2,1,0:T(1,128)S(1)}, u32[]{:S(2)}, u32[]{:S(2)}) async-start(s32[32,1,128]{2,1,0:T(1,128)} %bitcast.16), calls=%async_computation | async-start | bytes 32768 | tf_op jit(solution)/shard_map/all_to_all | solution.py:247
  39.4 0.6 copy-start.1
  64.7 31.0 %copy-start.2 = (s32[32,1,128]{2,1,0:T(1,128)S(1)}, s32[32,1,128]{2,1,0:T(1,128)}, u32[]{:S(2)}) copy-start(s32[32,1,128]{2,1,0:T(1,128)} %copy-done.1) | copy-start | bytes 49156
  89.5 10.1 %copy-start = (f32[4,128,8,128]{3,2,1,0:T(8,128)}, f32[4,128,8,128]{3,2,1,0:T(8,128)S(1)}, u32[]{:S(2)}) copy-start(f32[4,128,8,128]{3,2,1,0:T(8,128)S(1)} %all_to_all.22.own) | copy-start | bytes 6291460
  89.5 10.1 %collective-permute-start.3 = (f32[4,128,8,128]{3,2,1,0:T(8,128)S(1)}, f32[4,128,8,128]{3,2,1,0:T(8,128)}, u32[]{:S(2)}, u32[]{:S(2)}) collective-permute-start(f32[4,128,8,128]{3,2,1,0:T(8,128)S(1)} %all_to_all.22.own), channel_id=1, source_target_pairs={{0,32},{32,0},{64,96},{96,64},{128,160},{160,128},{192,224},{224,1... | collective-permute-start | bytes 6291464 | tf_op jit(solution)/shard_map/ppermute | solution.py:314

commit v2 on v1

--- a/solution.py
+++ b/solution.py
@@ -20,25 +20,27 @@
     return lax.dot_general(a, b, (dims, ((), ())), preferred_element_type=jnp.float32)
 
 
-def index_kernel(mask_ref, count_ref, start_ref, index_ref):
+def where_1(cond):
+    return jnp.where(cond, 1.0, 0.0).astype(jnp.bfloat16)
+
+
+def count_kernel(mask_ref, count_ref):
+    total = jnp.sum(jnp.sum(mask_ref[...], axis=0, keepdims=True), axis=1, keepdims=True)
+    count_ref[...] = jnp.broadcast_to(total, (SHARDS, LANES))
+
+
+def index_kernel(mask_ref, start_ref, index_ref):
     marked = mask_ref[...]
     ones = marked.astype(jnp.float32).astype(jnp.bfloat16)
     row = lax.broadcasted_iota(jnp.int32, (LANES, LANES), 0)
     lane = lax.broadcasted_iota(jnp.int32, (LANES, LANES), 1)
     full = jnp.ones((LANES, LANES), jnp.bfloat16)
 
-    def where_1(cond):
-        return jnp.where(cond, 1.0, 0.0).astype(jnp.bfloat16)
-
     inclusive = dot(ones, where_1(row <= lane)).astype(jnp.int32)
     in_row = dot(ones, full)
     start = dot(where_1(row > lane), in_row.astype(jnp.bfloat16)).astype(jnp.int32)
     in_row_t = dot(jnp.ones((8, LANES), jnp.bfloat16), ones, ((1,), (1,)))
-    in_row_tb = in_row_t.astype(jnp.bfloat16)
-    start_ref[...] = dot(in_row_tb, where_1(row < lane)).astype(jnp.int32)
-    total = dot(in_row_tb, full).astype(jnp.int32)
-    for i in range(SHARDS // 8):
-        count_ref[8 * i : 8 * i + 8, :] = total
+    start_ref[...] = dot(in_row_t.astype(jnp.bfloat16), where_1(row < lane)).astype(jnp.int32)
 
     moves = lane - inclusive + 1
     code = jnp.where(marked == 1, moves * 256 + lane, 0)
@@ -89,7 +91,7 @@
         gmax = jnp.zeros((8, LANES), jnp.float32)
         lmax = jnp.zeros((8, LANES), jnp.float32)
         for v in range(VIEWS_DEV):
-            r = [[rot[v, 3 * i + j] for j in range(3)] for i in range(3)]
+            r = [[rot[i, v, j] for j in range(3)] for i in range(3)]
             f = focal[0, v]
             p = [r[i][0] * m[0] + r[i][1] * m[1] + r[i][2] * m[2] + trans[v, i] for i in range(3)]
             over = 1.0 / jnp.maximum(p[2], 1.0)
@@ -125,47 +127,8 @@
     return total
 
 
-def pack_kernel(
-    where, counts, start, index, squares, means, scales, quats, low, high, out_ref, peak_ref, rows
-):
-    view = where[0]
-    g_of = lax.broadcasted_iota(jnp.int32, (8, LANES), 0)
-    for g in range(BLOCKS // 8):
-        norm = jnp.sqrt(squares[0, 8 * g : 8 * g + 8, :])
-        radius = 3.0 * jnp.sqrt(squares[1, 8 * g : 8 * g + 8, :])
-        for j in range(8):
-            col = slice((8 * g + j) * LANES, (8 * g + j + 1) * LANES)
-            peak_ref[0:1, col] = norm[j : j + 1, :]
-            peak_ref[1:2, col] = radius[j : j + 1, :]
-
-    @pl.when(view == 0)
-    def _():
-        rows[0:3, :] = means[...]
-        rows[3:6, :] = scales[...]
-        rows[6:8, :] = quats[0:2, :]
-
-    @pl.when(view == 1)
-    def _():
-        rows[0:2, :] = quats[2:4, :]
-
-    @pl.when(view > 1)
-    def _():
-        rows[0:2, :] = low[6:8, :]
-
-    @pl.when((view > 0) & (view < 7))
-    def _():
-        rows[2:8, :] = high[0:6, :]
-
-    @pl.when(view == 7)
-    def _():
-        rows[2:3, :] = high[0:1, :]
-        rows[3:5, :] = peak_ref[...]
-        rows[5:8, :] = jnp.zeros((3, G_DEV), jnp.float32)
-
+def each_block(where, counts, start, index, rows, store):
     offset = blocks_before(counts, where[1])
-    zero = jnp.zeros((8, LANES), jnp.float32)
-    for i in range(BLOCKS):
-        out_ref[i] = zero
 
     def place_of(block):
         return ((offset + block) & (SHARDS - 1)) * PER + (block >> 5)
@@ -179,12 +142,79 @@
             packed = jnp.take_along_axis(
                 tile, code & (LANES - 1), axis=1, mode="promise_in_bounds"
             )
-            pltpu.store(out_ref.at[place_of(block)], packed, mask=(code & 256) != 0)
+            store(place_of(block), packed, (code & 256) != 0)
             after = jnp.minimum(block + 1, BLOCKS - 1)
-            pltpu.store(out_ref.at[place_of(after)], packed, mask=(code & 512) != 0)
+            store(place_of(after), packed, (code & 512) != 0)
         return carry
 
     lax.fori_loop(0, BLOCKS // 8, eight, 0)
+
+
+def fill_kernel(where, counts, start, index, means, scales, quats, low, high, out_ref, rows):
+    view = where[0]
+
+    @pl.when(view == 0)
+    def _():
+        rows[0:3, :] = means[...]
+        rows[3:6, :] = scales[...]
+        rows[6:8, :] = quats[0:2, :]
+
+    @pl.when(view == 1)
+    def _():
+        rows[0:2, :] = quats[2:4, :]
+
+    @pl.when(view > 1)
+    def _():
+        rows[0:2, :] = low[6:8, :]
+
+    @pl.when((view > 0) & (view < 7))
+    def _():
+        rows[2:8, :] = high[0:6, :]
+
+    @pl.when(view == 7)
+    def _():
+        rows[2:3, :] = high[0:1, :]
+        rows[3:8, :] = jnp.zeros((5, G_DEV), jnp.float32)
+
+    zero = jnp.zeros((8, LANES), jnp.float32)
+    for i in range(BLOCKS):
+        out_ref[i] = zero
+
+    def store(at, packed, mask):
+        pltpu.store(out_ref.at[at], packed, mask=mask)
+
+    each_block(where, counts, start, index, rows, store)
+
+
+def peak_kernel(where, counts, start, index, sq0, sq1, sq2, sq3, filled, out_ref, peak_ref, rows):
+    for i in range(BLOCKS):
+        out_ref[i] = filled[i]
+
+    for g in range(BLOCKS // 8):
+        at = slice(8 * g, 8 * g + 8)
+
+        def top(k):
+            return jnp.maximum(
+                jnp.maximum(sq0[k, at, :], sq1[k, at, :]), jnp.maximum(sq2[k, at, :], sq3[k, at, :])
+            )
+
+        norm = jnp.sqrt(top(0))
+        radius = 3.0 * jnp.sqrt(top(1))
+        for j in range(8):
+            col = slice((8 * g + j) * LANES, (8 * g + j + 1) * LANES)
+            peak_ref[0:1, col] = norm[j : j + 1, :]
+            peak_ref[1:2, col] = radius[j : j + 1, :]
+
+    @pl.when(where[0] == 7)
+    def _():
+        rows[3:5, :] = peak_ref[...]
+        sub = lax.broadcasted_iota(jnp.int32, (8, LANES), 0)
+        ours = (sub == 3) | (sub == 4)
+
+        def store(at, packed, mask):
+            pltpu.store(out_ref.at[at], packed, mask=mask & ours)
+
+        each_block(where, counts, start, index, rows, store)
 
 
 def place_kernel(where, counts, arrived, out_ref, slots):
@@ -233,17 +263,17 @@
     view = lax.axis_index("view")
     where = jnp.stack([view, lax.axis_index("gauss")]).astype(i32)
 
-    count, start, index = pl.pallas_call(
-        index_kernel,
+    def whole(*shape):
+        return pl.BlockSpec(shape, lambda i, w: (0,) * len(shape))
+
+    mask = clone_mask.reshape(BLOCKS, LANES)
+    count = pl.pallas_call(
+        count_kernel,
         in_specs=[vmem()],
-        out_specs=[vmem()] * 3,
-        out_shape=[
-            jax.ShapeDtypeStruct((SHARDS, LANES), i32),
-            jax.ShapeDtypeStruct((8, LANES), i32),
-            jax.ShapeDtypeStruct((BLOCKS, LANES), i32),
-        ],
-        name="index",
-    )(clone_mask.reshape(BLOCKS, LANES))
+        out_specs=vmem(),
+        out_shape=jax.ShapeDtypeStruct((SHARDS, LANES), i32),
+        name="count",
+    )(mask)
     counts = lax.all_to_all(count, "gauss", 0, 0, tiled=True)
 
     squares = pl.pallas_call(
@@ -254,7 +284,7 @@
         scratch_shapes=[pltpu.VMEM((192, LANES), f32)],
         name="views",
     )(
-        rotation.reshape(VIEWS_DEV, 9),
+        rotation.transpose(1, 0, 2),
         shift,
         focal.reshape(1, VIEWS_DEV),
         means,
@@ -263,15 +293,24 @@
         grad_screen,
         visible,
     )
-    for k in (1, 2, 4):
-        pairs = [(v, v ^ k) for v in range(8)]
-        squares = jnp.maximum(squares, lax.ppermute(squares, "view", pairs))
-
-    def whole(*shape):
-        return pl.BlockSpec(shape, lambda i, w: (0,) * len(shape))
-
-    outgoing, peak = pl.pallas_call(
-        pack_kernel,
+    other = lax.ppermute(squares, "view", [(v, v ^ 1) for v in range(8)])
+    squares = [jnp.maximum(squares, other)]
+    for k in (1, 2, 3):
+        pairs = [(v, (v + 2 * k) % 8) for v in range(8)]
+        squares.append(lax.ppermute(squares[0], "view", pairs))
+
+    start, index = pl.pallas_call(
+        index_kernel,
+        in_specs=[vmem()],
+        out_specs=[vmem()] * 2,
+        out_shape=[
+            jax.ShapeDtypeStruct((8, LANES), i32),
+            jax.ShapeDtypeStruct((BLOCKS, LANES), i32),
+        ],
+        name="index",
+    )(mask)
+    filled = pl.pallas_call(
+        fill_kernel,
         grid_spec=pltpu.PrefetchScalarGridSpec(
             num_scalar_prefetch=1,
             grid=(1,),
@@ -279,22 +318,29 @@
                 smem(),
                 smem(),
                 whole(BLOCKS, LANES),
-                whole(2, BLOCKS, LANES),
                 whole(3, G_DEV),
                 whole(3, G_DEV),
                 whole(4, G_DEV),
                 pl.BlockSpec((8, G_DEV), lambda i, w: (jnp.maximum(w[0] - 2, 0), 0)),
                 pl.BlockSpec((8, G_DEV), lambda i, w: (jnp.maximum(w[0] - 1, 0), 0)),
             ],
-            out_specs=[whole(BLOCKS, 8, LANES), whole(2, G_DEV)],
+            out_specs=whole(BLOCKS, 8, LANES),
             scratch_shapes=[pltpu.VMEM((8, G_DEV), f32)],
         ),
+        out_shape=jax.ShapeDtypeStruct((BLOCKS, 8, LANES), f32),
+        name="fill",
+    )(where, counts, start, index, means, scales, quats, attrs, attrs)
+    outgoing, peak = pl.pallas_call(
+        peak_kernel,
+        in_specs=[smem()] * 3 + [vmem()] * 6,
+        out_specs=[vmem()] * 2,
         out_shape=[
             jax.ShapeDtypeStruct((BLOCKS, 8, LANES), f32),
             jax.ShapeDtypeStruct((2, G_DEV), f32),
         ],
-        name="pack",
-    )(where, counts, start, index, squares, means, scales, quats, attrs, attrs)
+        scratch_shapes=[pltpu.VMEM((8, G_DEV), f32)],
+        name="peaks",
+    )(where, counts, start, index, *squares, filled)
 
     arrived = lax.all_to_all(
         outgoing.reshape(SHARDS, PER, 8, LANES), "gauss", 0, 0, tiled=True

time: 107 us -> 107 us (level); the launches traced: 105 us -> 106 us
  waiting for transfers between devices: 16.5 us -> 10.3 us
  blocking collectives: 41.7 us -> 47.5 us
  Pallas kernels: 19.5 us -> 23.2 us
  starting transfers between devices: 21.8 us -> 20.5 us
    all_to_all x1, blocking collectives: 24.8 us -> 30.3 us  [body(): lax.all_to_all(piece, 'view', 0, 0, axis_index_groups=cores, tiled=True)]
    ppermute x3 -> x4, waiting for transfers between devices: 5.88 us -> 1.2 us  [the longest x1 1.2 us: body(): other = lax.ppermute(squares, 'view', [(v, v ^ 1) for v in range(8)])]
    pallas_call x2 -> x4, Pallas kernels: 7.09 us -> 10.7 us  [the longest x1 4.69 us: body(): pl.pallas_call(fill_kernel, grid_spec=pltpu.PrefetchScalarGridSpec(num_sc...]
    ppermute x1, starting transfers between devices: 6.19 us -> 4.14 us  [body(): other = lax.ppermute(own, 'view', [(v, v ^ 1) for v in range(8)])]
    all_to_all x1, waiting for transfers between devices: 7.34 us -> 5.81 us  [body(): counts = lax.all_to_all(count, 'gauss', 0, 0, tiled=True)]
    ppermute x3 -> x4, starting transfers between devices: 4.41 us -> 5.17 us  [the longest x1 3.2 us: body(): other = lax.ppermute(squares, 'view', [(v, v ^ 1) for v in range(8)])]
  transfers between devices with their start and end apart: 5 -> 6, of which waited for: 4 -> 3; matrix products, arithmetic and copies ran while one was open for 2% -> 1% of each run, Pallas kernels for 2% -> 8%
where the time goes in v2:
time: 107 us; the launch traced here: 106 us
  blocking collectives  47.5 us (44%)
  Pallas kernels  23.2 us (22%)
  starting transfers between devices  20.5 us (19%)
  waiting for transfers between devices  10.3 us (10%)
  other arithmetic  2.12 us (2%)
  local copies, waits for them, and re-layouts  1.94 us (2%)
    all_to_all x1, blocking collectives, body(): lax.all_to_all(piece, 'view', 0, 0, axis_index_groups=cores, tiled=True)  30.3 us
    all_to_all x1, blocking collectives, body(): lax.all_to_all(outgoing.reshape(SHARDS, PER, 8, LANES), 'gauss', 0, 0, ti...  17.2 us
    all_to_all x1, starting transfers between devices, body(): counts = lax.all_to_all(count, 'gauss', 0, 0, tiled=True)  11.2 us
    all_to_all x1, waiting for transfers between devices, body(): counts = lax.all_to_all(count, 'gauss', 0, 0, tiled=True)  5.81 us
    pallas_call x1, Pallas kernels, body(): pl.pallas_call(join_kernel, grid_spec=pltpu.PrefetchScalarGridSpec(num_sc...  5.36 us
    pallas_call x1, Pallas kernels, body(): pl.pallas_call(fill_kernel, grid_spec=pltpu.PrefetchScalarGridSpec(num_sc...  4.69 us
    pallas_call x1, Pallas kernels, body(): pl.pallas_call(view_kernel, in_specs=[smem()] * 3 + [vmem()] * 5, out_spe...  4.19 us
    ppermute x1, starting transfers between devices, body(): other = lax.ppermute(own, 'view', [(v, v ^ 1) for v in range(8)])  4.14 us
  transfers between devices with their start and end apart: 6, of which 3 were waited for; matrix products, arithmetic and copies ran while one was open for 1% of the time, Pallas kernels for 8%

profile of v2, /device:TPU:1, one launch (start us, length us, event | category | flops | bytes accessed | tf_op | source)
XLA Modules:
  0.0 106.2 jit_solution(13342427491949306273)
XLA Ops:
  0.6 4.2 %views.1 = f32[2,128,128]{2,1,0:T(8,128)} custom-call(f32[3,4,3]{2,1,0:T(4,128)} %bitcast.20, f32[4,3]{1,0:T(4,128)} %trans.1, f32[1,4]{1,0:T(1,128)} %bitcast.21, f32[3,16384]{1,0:T(4,128)} %means.3, f32[3,16384]{1,0:T(4,128)} %scales.3, f32[4,16384]{1,0:T(4,128)} %quats.3, f32[4,2,16384]{2,1,0:T(2,128)} %grad.1, s32[4,16384]{1,0:T(4,128)} %seen.1), custom_call_target="tpu_custom_call" | custom-call | tf_op jit(solution)/shard_map/views/pallas_call | solution.py:279
  4.8 3.2 %collective-permute-start = (f32[2,128,128]{2,1,0:T(8,128)}, f32[2,128,128]{2,1,0:T(8,128)S(1)}, u32[]{:S(2)}, u32[]{:S(2)}) collective-permute-start(f32[2,128,128]{2,1,0:T(8,128)} %views.1), channel_id=1, source_target_pairs={{0,32},{32,0},{64,96},{96,64},{128,160},{160,128},{192,224},{224,1... | collective-permute-start | bytes 393224 | tf_op jit(solution)/shard_map/ppermute | solution.py:296
  8.0 1.2 %collective-permute-done = f32[2,128,128]{2,1,0:T(8,128)S(1)} collective-permute-done((f32[2,128,128]{2,1,0:T(8,128)}, f32[2,128,128]{2,1,0:T(8,128)S(1)}, u32[]{:S(2)}, u32[]{:S(2)}) %collective-permute-start) | collective-permute-done | bytes 131104 | tf_op jit(solution)/shard_map/ppermute | solution.py:296
  9.2 0.9 max.3.sq0
  10.2 0.8 collective-permute-start.3
  11.0 0.5 collective-permute-start.2
  11.5 0.6 collective-permute-start.1
  12.1 1.5 %count.1 = s32[32,128]{1,0:T(8,128)} custom-call(s32[128,128]{1,0:T(8,128)} %bitcast.17), custom_call_target="tpu_custom_call" | custom-call | tf_op jit(solution)/shard_map/count/pallas_call | solution.py:270
  13.7 11.2 %all-to-all-start = ((s32[32,1,128]{2,1,0:T(1,128)}), s32[32,1,128]{2,1,0:T(1,128)S(1)}, u32[]{:S(2)}, u32[]{:S(2)}) async-start(s32[32,1,128]{2,1,0:T(1,128)} %bitcast.19), calls=%async_computation | async-start | bytes 32768 | tf_op jit(solution)/shard_map/all_to_all | solution.py:277
  24.9 0.6 pad_add_fusion.where
  25.4 2.2 %index.1 = (s32[8,128]{1,0:T(8,128)}, s32[128,128]{1,0:T(8,128)}) custom-call(s32[128,128]{1,0:T(8,128)} %bitcast.18), custom_call_target="tpu_custom_call" | custom-call | tf_op jit(solution)/shard_map/index/pallas_call | solution.py:302
  27.7 5.8 %all-to-all-done = s32[32,1,128]{2,1,0:T(1,128)S(1)} async-done(((s32[32,1,128]{2,1,0:T(1,128)}), s32[32,1,128]{2,1,0:T(1,128)S(1)}, u32[]{:S(2)}, u32[]{:S(2)}) %all-to-all-start) | async-done | bytes 16416 | tf_op jit(solution)/shard_map/all_to_all | solution.py:277
  33.5 0.6 copy-done.2
  34.1 4.7 %fill.1.filled = f32[128,8,128]{2,1,0:T(8,128)} custom-call(s32[2]{0:T(128)} %pad_add_fusion.where, s32[32,128]{1,0:T(8,128)} %bitcast.13, s32[8,128]{1,0:T(8,128)} %get-tuple-element.7.start, s32[128,128]{1,0:T(8,128)} %get-tuple-element.8.index, f32[3,16384]{1,0:T(4,128)} %means.3, f32[3,16384]{1,0:T(4,128)} %scales.3, f32[4,16384]{1,0:T(4,128)} %quats.3, ...), custom_call_target="tpu_custom_call" | custom-call | tf_op jit(solution)/shard_map/fill/pallas_call | solution.py:312
  38.8 0.0 copy-done.1
  38.8 0.0 collective-permute-done.3.sq3
  38.8 0.0 copy-start.4
  38.8 0.0 collective-permute-done.2.sq2
  38.8 0.0 copy-start.5
  38.8 0.0 collective-permute-done.1.sq1
  38.8 0.6 copy-done.4
  39.4 0.1 copy-done.5
  39.5 0.7 copy-done.6
  40.1 2.3 %peaks.1 = (f32[128,8,128]{2,1,0:T(8,128)}, f32[2,16384]{1,0:T(2,128)}) custom-call(s32[2]{0:T(128)} %pad_add_fusion.where, s32[32,128]{1,0:T(8,128)} %bitcast.14, s32[8,128]{1,0:T(8,128)} %get-tuple-element.7.start, s32[128,128]{1,0:T(8,128)} %get-tuple-element.8.index, f32[2,128,128]{2,1,0:T(8,128)} %copy-done.1, f32[2,128,128]{2,1,0:T(8,128)} %copy-done.6, ...), custom_call_target="tpu_custom_call" | custom-call | tf_op jit(solution)/shard_map/peaks/pallas_call | solution.py:333
  42.4 17.2 %all_to_all.21 = f32[32,4,8,128]{3,2,1,0:T(8,128)} all-to-all(f32[32,4,8,128]{3,2,1,0:T(8,128)} %bitcast.12), channel_id=1, replica_groups=mesh['view'=8,'gauss'=32] {'gauss'}, dimensions={0} | all-to-all | bytes 1048576 | tf_op jit(solution)/shard_map/all_to_all | solution.py:345
  59.6 2.9 %place.1 = f32[4,128,8,128]{3,2,1,0:T(8,128)} custom-call(s32[2]{0:T(128)} %pad_add_fusion.where, s32[32,128]{1,0:T(8,128)} %bitcast.15, f32[128,8,128]{2,1,0:T(8,128)} %bitcast.11), custom_call_target="tpu_custom_call" | custom-call | tf_op jit(solution)/shard_map/place/pallas_call | solution.py:350
  62.5 30.3 %all_to_all.22.own = f32[4,128,8,128]{3,2,1,0:T(8,128)S(1)} all-to-all(f32[4,128,8,128]{3,2,1,0:T(8,128)} %place.1), channel_id=1, replica_groups={{0,64,128,192},{32,96,160,224},{1,65,129,193},{33,97,161,225},{2,66,130..., dimensions={0} | all-to-all | bytes 4194304 | tf_op jit(solution)/shard_map/all_to_all | solution.py:359
  92.8 4.1 %collective-permute-start.4 = (f32[4,128,8,128]{3,2,1,0:T(8,128)S(1)}, f32[4,128,8,128]{3,2,1,0:T(8,128)}, u32[]{:S(2)}, u32[]{:S(2)}) collective-permute-start(f32[4,128,8,128]{3,2,1,0:T(8,128)S(1)} %all_to_all.22.own), channel_id=1, source_target_pairs={{0,32},{32,0},{64,96},{96,64},{128,160},{160,128},{192,224},{224,1... | collective-permute-start | bytes 6291464 | tf_op jit(solution)/shard_map/ppermute | solution.py:360
  97.0 0.0 copy-done.3
  97.0 0.6 slice_reduce_fusion
  97.6 3.3 %collective-permute-done.4.other = f32[4,128,8,128]{3,2,1,0:T(8,128)} collective-permute-done((f32[4,128,8,128]{3,2,1,0:T(8,128)S(1)}, f32[4,128,8,128]{3,2,1,0:T(8,128)}, u32[]{:S(2)}, u32[]{:S(2)}) %collective-permute-start.4) | collective-permute-done | bytes 2097184 | tf_op jit(solution)/shard_map/ppermute | solution.py:360
  100.9 5.4 %join.1 = f32[61,16384]{1,0:T(8,128)} custom-call(s32[2]{0:T(128)} %pad_add_fusion.where, f32[4,128,8,128]{3,2,1,0:T(8,128)} %copy-done, f32[4,128,8,128]{3,2,1,0:T(8,128)} %collective-permute-done.4.other), custom_call_target="tpu_custom_call" | custom-call | tf_op jit(solution)/shard_map/join/pallas_call | solution.py:361
  (6 shorter events, 0.0 us)
Async XLA Ops:
  4.8 4.4 %collective-permute-start = (f32[2,128,128]{2,1,0:T(8,128)}, f32[2,128,128]{2,1,0:T(8,128)S(1)}, u32[]{:S(2)}, u32[]{:S(2)}) collective-permute-start(f32[2,128,128]{2,1,0:T(8,128)} %views.1), channel_id=1, source_target_pairs={{0,32},{32,0},{64,96},{96,64},{128,160},{160,128},{192,224},{224,1... | collective-permute-start | bytes 393224 | tf_op jit(solution)/shard_map/ppermute | solution.py:296
  10.1 28.6 %copy-start.1 = (f32[2,128,128]{2,1,0:T(8,128)}, f32[2,128,128]{2,1,0:T(8,128)S(1)}, u32[]{:S(2)}) copy-start(f32[2,128,128]{2,1,0:T(8,128)S(1)} %max.3.sq0) | copy-start | bytes 393220
  10.2 28.6 %collective-permute-start.3 = (f32[2,128,128]{2,1,0:T(8,128)S(1)}, f32[2,128,128]{2,1,0:T(8,128)S(1)}, u32[]{:S(2)}, u32[]{:S(2)}) collective-permute-start(f32[2,128,128]{2,1,0:T(8,128)S(1)} %max.3.sq0), channel_id=1, source_target_pairs={{0,192},{32,224},{64,0},{96,32},{128,64},{160,96},{192,128},{224,1... | collective-permute-start | bytes 393224 | tf_op jit(solution)/shard_map/ppermute | solution.py:300
  11.0 27.8 %collective-permute-start.2 = (f32[2,128,128]{2,1,0:T(8,128)S(1)}, f32[2,128,128]{2,1,0:T(8,128)S(1)}, u32[]{:S(2)}, u32[]{:S(2)}) collective-permute-start(f32[2,128,128]{2,1,0:T(8,128)S(1)} %max.3.sq0), channel_id=1, source_target_pairs={{0,128},{32,160},{64,192},{96,224},{128,0},{160,32},{192,64},{224,... | collective-permute-start | bytes 393224 | tf_op jit(solution)/shard_map/ppermute | solution.py:300
  11.5 27.3 %collective-permute-start.1 = (f32[2,128,128]{2,1,0:T(8,128)S(1)}, f32[2,128,128]{2,1,0:T(8,128)S(1)}, u32[]{:S(2)}, u32[]{:S(2)}) collective-permute-start(f32[2,128,128]{2,1,0:T(8,128)S(1)} %max.3.sq0), channel_id=1, source_target_pairs={{0,64},{32,96},{64,128},{96,160},{128,192},{160,224},{192,0},{224,... | collective-permute-start | bytes 393224 | tf_op jit(solution)/shard_map/ppermute | solution.py:300
  13.7 19.8 %all-to-all-start = ((s32[32,1,128]{2,1,0:T(1,128)}), s32[32,1,128]{2,1,0:T(1,128)S(1)}, u32[]{:S(2)}, u32[]{:S(2)}) async-start(s32[32,1,128]{2,1,0:T(1,128)} %bitcast.19), calls=%async_computation | async-start | bytes 32768 | tf_op jit(solution)/shard_map/all_to_all | solution.py:277
  33.5 0.6 copy-start.2
  38.8 0.6 copy-start.4
  38.8 0.7 copy-start.5
  39.5 0.7 copy-start.6
  62.5 34.5 %copy-start.3 = (s32[32,1,128]{2,1,0:T(1,128)S(1)}, s32[32,1,128]{2,1,0:T(1,128)}, u32[]{:S(2)}) copy-start(s32[32,1,128]{2,1,0:T(1,128)} %copy-done.2) | copy-start | bytes 49156
  92.8 8.1 %copy-start = (f32[4,128,8,128]{3,2,1,0:T(8,128)}, f32[4,128,8,128]{3,2,1,0:T(8,128)S(1)}, u32[]{:S(2)}) copy-start(f32[4,128,8,128]{3,2,1,0:T(8,128)S(1)} %all_to_all.22.own) | copy-start | bytes 6291460
  92.8 8.1 %collective-permute-start.4 = (f32[4,128,8,128]{3,2,1,0:T(8,128)S(1)}, f32[4,128,8,128]{3,2,1,0:T(8,128)}, u32[]{:S(2)}, u32[]{:S(2)}) collective-permute-start(f32[4,128,8,128]{3,2,1,0:T(8,128)S(1)} %all_to_all.22.own), channel_id=1, source_target_pairs={{0,32},{32,0},{64,96},{96,64},{128,160},{160,128},{192,224},{224,1... | collective-permute-start | bytes 6291464 | tf_op jit(solution)/shard_map/ppermute | solution.py:360

commit v3 on v2

--- a/solution.py
+++ b/solution.py
@@ -11,6 +11,7 @@
 SHARDS = 32
 PER = BLOCKS // SHARDS
 VIEWS_DEV = 4
+STEP = 16
 ROWS = 61
 SMEM = pltpu.MemorySpace.SMEM
 VMEM = pltpu.MemorySpace.VMEM
@@ -346,32 +347,46 @@
         outgoing.reshape(SHARDS, PER, 8, LANES), "gauss", 0, 0, tiled=True
     ).reshape(BLOCKS, 8, LANES)
 
-    cap = BLOCKS
-    piece = pl.pallas_call(
-        place_kernel,
-        in_specs=[smem(), smem(), vmem()],
-        out_specs=vmem(),
-        out_shape=jax.ShapeDtypeStruct((4, cap, 8, LANES), f32),
-        scratch_shapes=[pltpu.VMEM((cap + 1, 8, LANES), f32)],
-        name="place",
-    )(where, counts, arrived)
-    cores = [[0, 2, 4, 6], [1, 3, 5, 7]]
-    own = lax.all_to_all(piece, "view", 0, 0, axis_index_groups=cores, tiled=True)
-    other = lax.ppermute(own, "view", [(v, v ^ 1) for v in range(8)])
-    clones = pl.pallas_call(
-        join_kernel,
-        grid_spec=pltpu.PrefetchScalarGridSpec(
-            num_scalar_prefetch=1,
-            grid=(4,),
-            in_specs=[
-                pl.BlockSpec((1, cap, 8, LANES), lambda i, w: (i, 0, 0, 0)),
-                pl.BlockSpec((1, cap, 8, LANES), lambda i, w: (i, 0, 0, 0)),
-            ],
-            out_specs=pl.BlockSpec((16, G_DEV), lambda i, w: (i, 0)),
-        ),
-        out_shape=jax.ShapeDtypeStruct((ROWS, G_DEV), f32),
-        name="join",
-    )(where, own, other)
+    used = jnp.sum((counts[:, 0] + LANES - 1) >> 7)
+    rounds = (used + SHARDS * STEP - 1) >> 9
+
+    def gather(cap):
+        def go(where, counts, arrived):
+            piece = pl.pallas_call(
+                place_kernel,
+                in_specs=[smem(), smem(), vmem()],
+                out_specs=vmem(),
+                out_shape=jax.ShapeDtypeStruct((4, cap, 8, LANES), f32),
+                scratch_shapes=[pltpu.VMEM((cap + 1, 8, LANES), f32)],
+                name="place",
+            )(where, counts, arrived)
+            cores = [[0, 2, 4, 6], [1, 3, 5, 7]]
+            own = lax.all_to_all(piece, "view", 0, 0, axis_index_groups=cores, tiled=True)
+            other = lax.ppermute(own, "view", [(v, v ^ 1) for v in range(8)])
+            return pl.pallas_call(
+                join_kernel,
+                grid_spec=pltpu.PrefetchScalarGridSpec(
+                    num_scalar_prefetch=1,
+                    grid=(4,),
+                    in_specs=[
+                        pl.BlockSpec((1, cap, 8, LANES), lambda i, w: (i, 0, 0, 0)),
+                        pl.BlockSpec((1, cap, 8, LANES), lambda i, w: (i, 0, 0, 0)),
+                    ],
+                    out_specs=pl.BlockSpec((16, G_DEV), lambda i, w: (i, 0)),
+                ),
+                out_shape=jax.ShapeDtypeStruct((ROWS, G_DEV), f32),
+                name="join",
+            )(where, own, other)
+
+        return go
+
+    clones = lax.switch(
+        jnp.clip(rounds - 1, 0, BLOCKS // STEP - 1),
+        [gather(cap) for cap in range(STEP, BLOCKS + 1, STEP)],
+        where,
+        counts,
+        arrived,
+    )
     return (peak, clones, jnp.sum(counts[:, 0]))
 
 

time: 107 us -> 92.2 us (0.86)
  blocking collectives: 47.5 us -> 19 us
  waiting for transfers between devices: 10.3 us -> 21.1 us
  starting transfers between devices: 20.5 us -> 24.4 us
  Pallas kernels: 23.2 us -> 21.7 us
    all_to_all x2 -> x1, blocking collectives: 47.5 us -> 19 us  [go(): lax.all_to_all(piece, 'view', 0, 0, axis_index_groups=cores, tiled=True)]
    all_to_all x0 -> x1, waiting for transfers between devices: none -> 11.3 us  [body(): lax.all_to_all(outgoing.reshape(SHARDS, PER, 8, LANES), 'gauss', 0, 0, ti...]
    all_to_all x0 -> x1, starting transfers between devices: none -> 3.89 us  [body(): lax.all_to_all(outgoing.reshape(SHARDS, PER, 8, LANES), 'gauss', 0, 0, ti...]
    pallas_call x2, Pallas kernels: 8.23 us -> 6.92 us  [the longest x1 4.72 us: go(): pl.pallas_call(join_kernel, grid_spec=pltpu.PrefetchScalarGridSpec(num_sc...]
  transfers between devices with their start and end apart: 6 -> 7, of which waited for: 3 -> 4; matrix products, arithmetic and copies ran while one was open for 1% -> 1% of each run, Pallas kernels for 8% -> 9%
where the time goes in v3:
time: 92.2 us; the launch traced here: 91.5 us
  starting transfers between devices  24.4 us (26%)
  Pallas kernels  21.7 us (24%)
  waiting for transfers between devices  21.1 us (23%)
  blocking collectives  19 us (21%)
  local copies, waits for them, and re-layouts  2.3 us (2%)
  other arithmetic  1.63 us (2%)
  between operations  1.37 us (1%)
    all_to_all x1, blocking collectives, go(): lax.all_to_all(piece, 'view', 0, 0, axis_index_groups=cores, tiled=True)  19 us
    all_to_all x1, waiting for transfers between devices, body(): lax.all_to_all(outgoing.reshape(SHARDS, PER, 8, LANES), 'gauss', 0, 0, ti...  11.3 us
    all_to_all x1, starting transfers between devices, body(): counts = lax.all_to_all(count, 'gauss', 0, 0, tiled=True)  11.2 us
    all_to_all x1, waiting for transfers between devices, body(): counts = lax.all_to_all(count, 'gauss', 0, 0, tiled=True)  6.31 us
    pallas_call x1, Pallas kernels, go(): pl.pallas_call(join_kernel, grid_spec=pltpu.PrefetchScalarGridSpec(num_sc...  4.72 us
    pallas_call x1, Pallas kernels, body(): pl.pallas_call(fill_kernel, grid_spec=pltpu.PrefetchScalarGridSpec(num_sc...  4.56 us
    pallas_call x1, Pallas kernels, body(): pl.pallas_call(view_kernel, in_specs=[smem()] * 3 + [vmem()] * 5, out_spe...  4.19 us
    ppermute x1, starting transfers between devices, go(): other = lax.ppermute(own, 'view', [(v, v ^ 1) for v in range(8)])  4.14 us
  transfers between devices with their start and end apart: 7, of which 4 were waited for; matrix products, arithmetic and copies ran while one was open for 1% of the time, Pallas kernels for 9%

profile of v3, /device:TPU:1, one launch (start us, length us, event | category | flops | bytes accessed | tf_op | source)
XLA Modules:
  0.0 91.5 jit_solution(8262058451064055131)
XLA Ops:
  0.6 4.2 %views.1 = f32[2,128,128]{2,1,0:T(8,128)} custom-call(f32[3,4,3]{2,1,0:T(4,128)} %bitcast.34, f32[4,3]{1,0:T(4,128)} %trans.1, f32[1,4]{1,0:T(1,128)} %bitcast.35, f32[3,16384]{1,0:T(4,128)} %means.3, f32[3,16384]{1,0:T(4,128)} %scales.3, f32[4,16384]{1,0:T(4,128)} %quats.3, f32[4,2,16384]{2,1,0:T(2,128)} %grad.1, s32[4,16384]{1,0:T(4,128)} %seen.1), custom_call_target="tpu_custom_call" | custom-call | tf_op jit(solution)/shard_map/views/pallas_call | solution.py:280
  4.8 3.2 %collective-permute-start.8 = (f32[2,128,128]{2,1,0:T(8,128)}, f32[2,128,128]{2,1,0:T(8,128)S(1)}, u32[]{:S(2)}, u32[]{:S(2)}) collective-permute-start(f32[2,128,128]{2,1,0:T(8,128)} %views.1), channel_id=1, source_target_pairs={{0,32},{32,0},{64,96},{96,64},{128,160},{160,128},{192,224},{224,1... | collective-permute-start | bytes 393224 | tf_op jit(solution)/shard_map/ppermute | solution.py:297
  8.0 1.2 %collective-permute-done.8 = f32[2,128,128]{2,1,0:T(8,128)S(1)} collective-permute-done((f32[2,128,128]{2,1,0:T(8,128)}, f32[2,128,128]{2,1,0:T(8,128)S(1)}, u32[]{:S(2)}, u32[]{:S(2)}) %collective-permute-start.8) | collective-permute-done | bytes 131104 | tf_op jit(solution)/shard_map/ppermute | solution.py:297
  9.2 0.9 %max.7.sq0 = f32[2,128,128]{2,1,0:T(8,128)S(1)} maximum(f32[2,128,128]{2,1,0:T(8,128)} %views.1, f32[2,128,128]{2,1,0:T(8,128)S(1)} %collective-permute-done.8) | non-fusion elementwise | flops 32768 | bytes 393216 | tf_op jit(solution)/shard_map/max | solution.py:298
  10.1 0.0 copy-start.11
  10.2 0.8 collective-permute-start.11
  11.0 0.5 collective-permute-start.10
  11.5 0.6 collective-permute-start.9
  12.1 1.5 %count.1 = s32[32,128]{1,0:T(8,128)} custom-call(s32[128,128]{1,0:T(8,128)} %bitcast.31), custom_call_target="tpu_custom_call" | custom-call | tf_op jit(solution)/shard_map/count/pallas_call | solution.py:271
  13.7 11.2 %all-to-all-start.8 = ((s32[32,1,128]{2,1,0:T(1,128)}), s32[32,1,128]{2,1,0:T(1,128)S(1)}, u32[]{:S(2)}, u32[]{:S(2)}) async-start(s32[32,1,128]{2,1,0:T(1,128)} %bitcast.33), calls=%async_computation.8 | async-start | bytes 32768 | tf_op jit(solution)/shard_map/all_to_all | solution.py:278
  24.9 0.1 pad_add_fusion.where
  25.0 2.2 %index.1 = (s32[8,128]{1,0:T(8,128)}, s32[128,128]{1,0:T(8,128)}) custom-call(s32[128,128]{1,0:T(8,128)} %bitcast.32), custom_call_target="tpu_custom_call" | custom-call | tf_op jit(solution)/shard_map/index/pallas_call | solution.py:303
  27.2 6.3 %all-to-all-done.8 = s32[32,1,128]{2,1,0:T(1,128)S(1)} async-done(((s32[32,1,128]{2,1,0:T(1,128)}), s32[32,1,128]{2,1,0:T(1,128)S(1)}, u32[]{:S(2)}, u32[]{:S(2)}) %all-to-all-start.8) | async-done | bytes 16416 | tf_op jit(solution)/shard_map/all_to_all | solution.py:278
  33.5 4.6 %fill.1.filled = f32[128,8,128]{2,1,0:T(8,128)} custom-call(s32[2]{0:T(128)S(1)} %pad_add_fusion.where, s32[32,128]{1,0:T(8,128)S(1)} %bitcast.19, s32[8,128]{1,0:T(8,128)} %get-tuple-element.88.start, s32[128,128]{1,0:T(8,128)} %get-tuple-element.89.index, f32[3,16384]{1,0:T(4,128)} %means.3, f32[3,16384]{1,0:T(4,128)} %scales.3, f32[4,16384]{1,0:T(4,128)} %quats.3, ...), custom_call_target="tpu_custom_call" | custom-call | tf_op jit(solution)/shard_map/fill/pallas_call | solution.py:313
  38.0 0.0 collective-permute-done.11.sq3
  38.1 0.0 collective-permute-done.10.sq2
  38.1 0.0 copy-start.15
  38.1 0.0 collective-permute-done.9.sq1
  38.1 0.6 copy-done.14
  38.7 0.1 copy-done.15
  38.8 0.6 copy-done.16
  39.4 2.3 %peaks.1 = (f32[128,8,128]{2,1,0:T(8,128)}, f32[2,16384]{1,0:T(2,128)}) custom-call(s32[2]{0:T(128)S(1)} %pad_add_fusion.where, s32[32,128]{1,0:T(8,128)S(1)} %bitcast.20, s32[8,128]{1,0:T(8,128)} %get-tuple-element.88.start, s32[128,128]{1,0:T(8,128)} %get-tuple-element.89.index, f32[2,128,128]{2,1,0:T(8,128)} %copy-done.11, f32[2,128,128]{2,1,0:T(8,128)} %copy-done.16, ...), custom_call_target="tpu_custom_call" | custom-call | tf_op jit(solution)/shard_map/peaks/pallas_call | solution.py:334
  41.7 3.9 %all-to-all-start.9 = ((f32[32,4,8,128]{3,2,1,0:T(8,128)}), f32[32,4,8,128]{3,2,1,0:T(8,128)S(1)}, u32[]{:S(2)}, u32[]{:S(2)}) async-start(f32[32,4,8,128]{3,2,1,0:T(8,128)} %bitcast.30), calls=%async_computation.9 | async-start | bytes 1048576 | tf_op jit(solution)/shard_map/all_to_all | solution.py:346
  45.6 0.6 slice_reduce_fusion
  46.9 11.3 %all-to-all-done.9 = f32[32,4,8,128]{3,2,1,0:T(8,128)S(1)} async-done(((f32[32,4,8,128]{3,2,1,0:T(8,128)}), f32[32,4,8,128]{3,2,1,0:T(8,128)S(1)}, u32[]{:S(2)}, u32[]{:S(2)}) %all-to-all-start.9) | async-done | bytes 524320 | tf_op jit(solution)/shard_map/all_to_all | solution.py:346
  58.2 33.3 %conditional.1 = (f32[61,16384]{1,0:T(8,128)}) conditional(s32[]{:T(128)} %clamp.3, (s32[2]{0:T(128)S(1)}, s32[32,128]{1,0:T(8,128)S(1)}, f32[128,8,128]{2,1,0:T(8,128)S(1)}) %tuple.51, (s32[2]{0:T(128)S(1)}, s32[32,128]{1,0:T(8,128)S(1)}, f32[128,8,128]{2,1,0:T(8,128)S(1)}) %tuple.52, (s32[2]{0:T(128)S(1)}, ...), branch_computations={%region_1.2_spmd, %region_2.3_spmd, %region_3.4_spmd, %region_4.5_... | conditional | bytes 20971596 | solution.py:383
  58.2 2.2 %place.11 = f32[4,64,8,128]{3,2,1,0:T(8,128)} custom-call(s32[2]{0:T(128)S(1)} %get-tuple-element.66.where, s32[32,128]{1,0:T(8,128)S(1)} %get-tuple-element.67.counts, f32[128,8,128]{2,1,0:T(8,128)S(1)} %get-tuple-element.68.arrived), custom_call_target="tpu_custom_call" | custom-call | tf_op jit(solution)/shard_map/cond/branch_3_fun/place/pallas_call | solution.py:355
  60.4 19.0 %all_to_all.51.own = f32[4,64,8,128]{3,2,1,0:T(8,128)S(1)} all-to-all(f32[4,64,8,128]{3,2,1,0:T(8,128)} %place.11), channel_id=1, replica_groups={{0,64,128,192},{32,96,160,224},{1,65,129,193},{33,97,161,225},{2,66,130..., dimensions={0} | all-to-all | bytes 2097152 | tf_op jit(solution)/shard_map/cond/branch_3_fun/all_to_all | solution.py:364
  79.4 4.1 %collective-permute-start.3 = (f32[4,64,8,128]{3,2,1,0:T(8,128)S(1)}, f32[4,64,8,128]{3,2,1,0:T(8,128)S(1)}, u32[]{:S(2)}, u32[]{:S(2)}) collective-permute-start(f32[4,64,8,128]{3,2,1,0:T(8,128)S(1)} %all_to_all.51.own), channel_id=1, source_target_pairs={{0,32},{32,0},{64,96},{96,64},{128,160},{160,128},{192,224},{224,1... | collective-permute-start | bytes 3145736 | tf_op jit(solution)/shard_map/cond/branch_3_fun/ppermute | solution.py:365
  83.5 2.3 %collective-permute-done.3.other = f32[4,64,8,128]{3,2,1,0:T(8,128)S(1)} collective-permute-done((f32[4,64,8,128]{3,2,1,0:T(8,128)S(1)}, f32[4,64,8,128]{3,2,1,0:T(8,128)S(1)}, u32[]{:S(2)}, u32[]{:S(2)}) %collective-permute-start.3) | collective-permute-done | bytes 1048608 | tf_op jit(solution)/shard_map/cond/branch_3_fun/ppermute | solution.py:365
  85.8 1.0 %copy-done.8 = f32[4,64,8,128]{3,2,1,0:T(8,128)} copy-done((f32[4,64,8,128]{3,2,1,0:T(8,128)}, f32[4,64,8,128]{3,2,1,0:T(8,128)S(1)}, u32[]{:S(2)}) %copy-start.8) | copy-done | bytes 1048600 | tf_op jit(solution)/shard_map/cond
  86.8 4.7 %join.11 = f32[61,16384]{1,0:T(8,128)} custom-call(s32[2]{0:T(128)S(1)} %get-tuple-element.66.where, f32[4,64,8,128]{3,2,1,0:T(8,128)} %copy-done.4, f32[4,64,8,128]{3,2,1,0:T(8,128)} %copy-done.8), custom_call_target="tpu_custom_call" | custom-call | tf_op jit(solution)/shard_map/cond/branch_3_fun/join/pallas_call | solution.py:366
  (6 shorter events, 0.0 us)
Async XLA Ops:
  4.8 4.4 %collective-permute-start.8 = (f32[2,128,128]{2,1,0:T(8,128)}, f32[2,128,128]{2,1,0:T(8,128)S(1)}, u32[]{:S(2)}, u32[]{:S(2)}) collective-permute-start(f32[2,128,128]{2,1,0:T(8,128)} %views.1), channel_id=1, source_target_pairs={{0,32},{32,0},{64,96},{96,64},{128,160},{160,128},{192,224},{224,1... | collective-permute-start | bytes 393224 | tf_op jit(solution)/shard_map/ppermute | solution.py:297
  10.1 27.9 %copy-start.11 = (f32[2,128,128]{2,1,0:T(8,128)}, f32[2,128,128]{2,1,0:T(8,128)S(1)}, u32[]{:S(2)}) copy-start(f32[2,128,128]{2,1,0:T(8,128)S(1)} %max.7.sq0) | copy-start | bytes 393220
  10.2 27.9 %collective-permute-start.11 = (f32[2,128,128]{2,1,0:T(8,128)S(1)}, f32[2,128,128]{2,1,0:T(8,128)S(1)}, u32[]{:S(2)}, u32[]{:S(2)}) collective-permute-start(f32[2,128,128]{2,1,0:T(8,128)S(1)} %max.7.sq0), channel_id=1, source_target_pairs={{0,192},{32,224},{64,0},{96,32},{128,64},{160,96},{192,128},{224,1... | collective-permute-start | bytes 393224 | tf_op jit(solution)/shard_map/ppermute | solution.py:301
  11.0 27.1 %collective-permute-start.10 = (f32[2,128,128]{2,1,0:T(8,128)S(1)}, f32[2,128,128]{2,1,0:T(8,128)S(1)}, u32[]{:S(2)}, u32[]{:S(2)}) collective-permute-start(f32[2,128,128]{2,1,0:T(8,128)S(1)} %max.7.sq0), channel_id=1, source_target_pairs={{0,128},{32,160},{64,192},{96,224},{128,0},{160,32},{192,64},{224,... | collective-permute-start | bytes 393224 | tf_op jit(solution)/shard_map/ppermute | solution.py:301
  11.5 26.6 %collective-permute-start.9 = (f32[2,128,128]{2,1,0:T(8,128)S(1)}, f32[2,128,128]{2,1,0:T(8,128)S(1)}, u32[]{:S(2)}, u32[]{:S(2)}) collective-permute-start(f32[2,128,128]{2,1,0:T(8,128)S(1)} %max.7.sq0), channel_id=1, source_target_pairs={{0,64},{32,96},{64,128},{96,160},{128,192},{160,224},{192,0},{224,... | collective-permute-start | bytes 393224 | tf_op jit(solution)/shard_map/ppermute | solution.py:301
  13.7 19.8 %all-to-all-start.8 = ((s32[32,1,128]{2,1,0:T(1,128)}), s32[32,1,128]{2,1,0:T(1,128)S(1)}, u32[]{:S(2)}, u32[]{:S(2)}) async-start(s32[32,1,128]{2,1,0:T(1,128)} %bitcast.33), calls=%async_computation.8 | async-start | bytes 32768 | tf_op jit(solution)/shard_map/all_to_all | solution.py:278
  38.0 0.6 copy-start.14
  38.1 0.7 copy-start.15
  38.8 0.6 copy-start.16
  41.7 16.5 %all-to-all-start.9 = ((f32[32,4,8,128]{3,2,1,0:T(8,128)}), f32[32,4,8,128]{3,2,1,0:T(8,128)S(1)}, u32[]{:S(2)}, u32[]{:S(2)}) async-start(f32[32,4,8,128]{3,2,1,0:T(8,128)} %bitcast.30), calls=%async_computation.9 | async-start | bytes 1048576 | tf_op jit(solution)/shard_map/all_to_all | solution.py:346
  79.4 6.4 %copy-start.4 = (f32[4,64,8,128]{3,2,1,0:T(8,128)}, f32[4,64,8,128]{3,2,1,0:T(8,128)S(1)}, u32[]{:S(2)}) copy-start(f32[4,64,8,128]{3,2,1,0:T(8,128)S(1)} %all_to_all.51.own) | copy-start | bytes 3145732 | tf_op jit(solution)/shard_map/cond
  79.4 6.4 %collective-permute-start.3 = (f32[4,64,8,128]{3,2,1,0:T(8,128)S(1)}, f32[4,64,8,128]{3,2,1,0:T(8,128)S(1)}, u32[]{:S(2)}, u32[]{:S(2)}) collective-permute-start(f32[4,64,8,128]{3,2,1,0:T(8,128)S(1)} %all_to_all.51.own), channel_id=1, source_target_pairs={{0,32},{32,0},{64,96},{96,64},{128,160},{160,128},{192,224},{224,1... | collective-permute-start | bytes 3145736 | tf_op jit(solution)/shard_map/cond/branch_3_fun/ppermute | solution.py:365
  85.8 1.0 %copy-start.8 = (f32[4,64,8,128]{3,2,1,0:T(8,128)}, f32[4,64,8,128]{3,2,1,0:T(8,128)S(1)}, u32[]{:S(2)}) copy-start(f32[4,64,8,128]{3,2,1,0:T(8,128)S(1)} %collective-permute-done.3.other) | copy-start | bytes 3145732 | tf_op jit(solution)/shard_map/cond

commit v4 on v3

--- a/solution.py
+++ b/solution.py
@@ -13,6 +13,7 @@
 VIEWS_DEV = 4
 STEP = 16
 ROWS = 61
+LIMIT = pltpu.CompilerParams(vmem_limit_bytes=16 * 2**20)
 SMEM = pltpu.MemorySpace.SMEM
 VMEM = pltpu.MemorySpace.VMEM
 
@@ -268,11 +269,19 @@
         return pl.BlockSpec(shape, lambda i, w: (0,) * len(shape))
 
     mask = clone_mask.reshape(BLOCKS, LANES)
+    rotation, focal = rotation.transpose(1, 0, 2), focal.reshape(1, VIEWS_DEV)
+    mask, means, scales, quats, attrs, grad_screen, visible, rotation, shift, focal = (
+        pltpu.with_memory_space_constraint(x, pltpu.MemorySpace.HBM)
+        for x in (
+            mask, means, scales, quats, attrs, grad_screen, visible, rotation, shift, focal
+        )
+    )
     count = pl.pallas_call(
         count_kernel,
         in_specs=[vmem()],
         out_specs=vmem(),
-        out_shape=jax.ShapeDtypeStruct((SHARDS, LANES), i32),
+        out_shape=VMEM((SHARDS, LANES), i32),
+        compiler_params=LIMIT,
         name="count",
     )(mask)
     counts = lax.all_to_all(count, "gauss", 0, 0, tiled=True)
@@ -281,13 +290,14 @@
         view_kernel,
         in_specs=[smem()] * 3 + [vmem()] * 5,
         out_specs=vmem(),
-        out_shape=jax.ShapeDtypeStruct((2, BLOCKS, LANES), f32),
+        out_shape=VMEM((2, BLOCKS, LANES), f32),
         scratch_shapes=[pltpu.VMEM((192, LANES), f32)],
+        compiler_params=LIMIT,
         name="views",
     )(
-        rotation.transpose(1, 0, 2),
+        rotation,
         shift,
-        focal.reshape(1, VIEWS_DEV),
+        focal,
         means,
         scales,
         quats,
@@ -305,9 +315,10 @@
         in_specs=[vmem()],
         out_specs=[vmem()] * 2,
         out_shape=[
-            jax.ShapeDtypeStruct((8, LANES), i32),
-            jax.ShapeDtypeStruct((BLOCKS, LANES), i32),
+            VMEM((8, LANES), i32),
+            VMEM((BLOCKS, LANES), i32),
         ],
+        compiler_params=LIMIT,
         name="index",
     )(mask)
     filled = pl.pallas_call(
@@ -328,7 +339,8 @@
             out_specs=whole(BLOCKS, 8, LANES),
             scratch_shapes=[pltpu.VMEM((8, G_DEV), f32)],
         ),
-        out_shape=jax.ShapeDtypeStruct((BLOCKS, 8, LANES), f32),
+        out_shape=VMEM((BLOCKS, 8, LANES), f32),
+        compiler_params=LIMIT,
         name="fill",
     )(where, counts, start, index, means, scales, quats, attrs, attrs)
     outgoing, peak = pl.pallas_call(
@@ -336,28 +348,30 @@
         in_specs=[smem()] * 3 + [vmem()] * 6,
         out_specs=[vmem()] * 2,
         out_shape=[
-            jax.ShapeDtypeStruct((BLOCKS, 8, LANES), f32),
+            VMEM((BLOCKS, 8, LANES), f32),
             jax.ShapeDtypeStruct((2, G_DEV), f32),
         ],
         scratch_shapes=[pltpu.VMEM((8, G_DEV), f32)],
+        compiler_params=LIMIT,
         name="peaks",
     )(where, counts, start, index, *squares, filled)
 
-    arrived = lax.all_to_all(
-        outgoing.reshape(SHARDS, PER, 8, LANES), "gauss", 0, 0, tiled=True
-    ).reshape(BLOCKS, 8, LANES)
-
     used = jnp.sum((counts[:, 0] + LANES - 1) >> 7)
     rounds = (used + SHARDS * STEP - 1) >> 9
+    branch = jnp.clip(rounds - 1, 0, BLOCKS // STEP - 1)
 
     def gather(cap):
-        def go(where, counts, arrived):
+        def go(where, counts, outgoing):
+            arrived = lax.all_to_all(
+                outgoing.reshape(SHARDS, PER, 8, LANES), "gauss", 0, 0, tiled=True
+            ).reshape(BLOCKS, 8, LANES)
             piece = pl.pallas_call(
                 place_kernel,
                 in_specs=[smem(), smem(), vmem()],
                 out_specs=vmem(),
-                out_shape=jax.ShapeDtypeStruct((4, cap, 8, LANES), f32),
+                out_shape=VMEM((4, cap, 8, LANES), f32),
                 scratch_shapes=[pltpu.VMEM((cap + 1, 8, LANES), f32)],
+                compiler_params=LIMIT,
                 name="place",
             )(where, counts, arrived)
             cores = [[0, 2, 4, 6], [1, 3, 5, 7]]
@@ -375,17 +389,18 @@
                     out_specs=pl.BlockSpec((16, G_DEV), lambda i, w: (i, 0)),
                 ),
                 out_shape=jax.ShapeDtypeStruct((ROWS, G_DEV), f32),
+                compiler_params=LIMIT,
                 name="join",
             )(where, own, other)
 
         return go
 
     clones = lax.switch(
-        jnp.clip(rounds - 1, 0, BLOCKS // STEP - 1),
+        branch,
         [gather(cap) for cap in range(STEP, BLOCKS + 1, STEP)],
         where,
         counts,
-        arrived,
+        outgoing,
     )
     return (peak, clones, jnp.sum(counts[:, 0]))
 

time: 92.2 us -> 83.8 us (0.909)
  blocking collectives: 19 us -> 39.1 us
  waiting for transfers between devices: 21.1 us -> 5.51 us
  Pallas kernels: 21.7 us -> 16.3 us
  starting transfers between devices: 24.4 us -> 19.7 us
  local copies, waits for them, and re-layouts: 2.3 us -> 0 us
    all_to_all x0 -> x1, blocking collectives: none -> 21.8 us  [go(): lax.all_to_all(outgoing.reshape(SHARDS, PER, 8, LANES), 'gauss', 0, 0, ti...]
    all_to_all x1 -> x0, waiting for transfers between devices: 11.3 us -> none  [body(): lax.all_to_all(outgoing.reshape(SHARDS, PER, 8, LANES), 'gauss', 0, 0, ti...]
    all_to_all x1 -> x0, starting transfers between devices: 3.89 us -> none  [body(): lax.all_to_all(outgoing.reshape(SHARDS, PER, 8, LANES), 'gauss', 0, 0, ti...]
    all_to_all x1, waiting for transfers between devices: 6.31 us -> 3.21 us  [body(): counts = lax.all_to_all(count, 'gauss', 0, 0, tiled=True)]
    pallas_call x1, Pallas kernels: 4.72 us -> 2.98 us  [go(): pl.pallas_call(join_kernel, grid_spec=pltpu.PrefetchScalarGridSpec(num_sc...]
    all_to_all x1, starting transfers between devices: 11.2 us -> 9.5 us  [body(): counts = lax.all_to_all(count, 'gauss', 0, 0, tiled=True)]
    ppermute x3, starting transfers between devices: 1.97 us -> 3.68 us  [body(): squares.append(lax.ppermute(squares[0], 'view', pairs))]
    all_to_all x1, blocking collectives: 19 us -> 17.3 us  [go(): lax.all_to_all(piece, 'view', 0, 0, axis_index_groups=cores, tiled=True)]
  transfers between devices with their start and end apart: 7 -> 6, of which waited for: 4 -> 2; matrix products, arithmetic and copies ran while one was open for 1% -> 1% of each run, Pallas kernels for 9% -> 8%
where the time goes in v4:
time: 83.8 us; the launch traced here: 82.7 us
  blocking collectives  39.1 us (47%)
  starting transfers between devices  19.7 us (24%)
  Pallas kernels  16.3 us (19%)
  waiting for transfers between devices  5.51 us (7%)
  between operations  1.35 us (2%)
    all_to_all x1, blocking collectives, go(): lax.all_to_all(outgoing.reshape(SHARDS, PER, 8, LANES), 'gauss', 0, 0, ti...  21.8 us
    all_to_all x1, blocking collectives, go(): lax.all_to_all(piece, 'view', 0, 0, axis_index_groups=cores, tiled=True)  17.3 us
    all_to_all x1, starting transfers between devices, body(): counts = lax.all_to_all(count, 'gauss', 0, 0, tiled=True)  9.5 us
    pallas_call x1, Pallas kernels, body(): pl.pallas_call(fill_kernel, grid_spec=pltpu.PrefetchScalarGridSpec(num_sc...  3.78 us
    ppermute x3, starting transfers between devices, body(): squares.append(lax.ppermute(squares[0], 'view', pairs))  3.68 us
    pallas_call x1, Pallas kernels, body(): pl.pallas_call(view_kernel, in_specs=[smem()] * 3 + [vmem()] * 5, out_spe...  3.53 us
    ppermute x1, starting transfers between devices, body(): other = lax.ppermute(squares, 'view', [(v, v ^ 1) for v in range(8)])  3.29 us
    ppermute x1, starting transfers between devices, go(): other = lax.ppermute(own, 'view', [(v, v ^ 1) for v in range(8)])  3.26 us
  transfers between devices with their start and end apart: 6, of which 2 were waited for; matrix products, arithmetic and copies ran while one was open for 1% of the time, Pallas kernels for 8%

profile of v4, /device:TPU:1, one launch (start us, length us, event | category | flops | bytes accessed | tf_op | source)
XLA Modules:
  0.0 82.7 jit_solution(6939646310572994988)
XLA Ops:
  0.6 3.5 %views.1 = f32[2,128,128]{2,1,0:T(8,128)S(1)} custom-call(f32[3,4,3]{2,1,0:T(4,128)} %bitcast.54, f32[4,3]{1,0:T(4,128)} %trans.1, f32[1,4]{1,0:T(1,128)} %bitcast.55, f32[3,16384]{1,0:T(4,128)} %means.3, f32[3,16384]{1,0:T(4,128)} %scales.3, f32[4,16384]{1,0:T(4,128)} %quats.3, f32[4,2,16384]{2,1,0:T(2,128)} %grad.1, s32[4,16384]{1,0:T(4,128)} %seen.1), custom_call_target="tpu_custom_call" | custom-call | tf_op jit(solution)/shard_map/views/pallas_call | solution.py:289
  4.2 3.3 %collective-permute-start.8 = (f32[2,128,128]{2,1,0:T(8,128)S(1)}, f32[2,128,128]{2,1,0:T(8,128)S(1)}, u32[]{:S(2)}, u32[]{:S(2)}) collective-permute-start(f32[2,128,128]{2,1,0:T(8,128)S(1)} %views.1), channel_id=1, source_target_pairs={{0,32},{32,0},{64,96},{96,64},{128,160},{160,128},{192,224},{224,1... | collective-permute-start | bytes 393224 | tf_op jit(solution)/shard_map/ppermute | solution.py:307
  7.5 1.5 %count.1 = s32[32,128]{1,0:T(8,128)} custom-call(s32[128,128]{1,0:T(8,128)} %bitcast.52), custom_call_target="tpu_custom_call" | custom-call | tf_op jit(solution)/shard_map/count/pallas_call | solution.py:279
  9.0 9.5 %all-to-all-start.16 = ((s32[32,1,128]{2,1,0:T(1,128)}), s32[32,1,128]{2,1,0:T(1,128)S(1)}, u32[]{:S(2)}, u32[]{:S(2)}) async-start(s32[32,1,128]{2,1,0:T(1,128)} %bitcast.20), calls=%async_computation.16 | async-start | bytes 32768 | tf_op jit(solution)/shard_map/all_to_all | solution.py:287
  18.5 0.0 collective-permute-done.8
  18.5 2.6 %collective-permute-start.11 = (f32[2,128,128]{2,1,0:T(8,128)S(1)}, f32[2,128,128]{2,1,0:T(8,128)S(1)}, u32[]{:S(2)}, u32[]{:S(2)}) collective-permute-start(f32[2,128,128]{2,1,0:T(8,128)S(1)} %max.7.sq0), channel_id=1, source_target_pairs={{0,192},{32,224},{64,0},{96,32},{128,64},{160,96},{192,128},{224,1... | collective-permute-start | bytes 393224 | tf_op jit(solution)/shard_map/ppermute | solution.py:311
  21.1 0.5 collective-permute-start.10
  21.6 0.6 collective-permute-start.9
  22.2 0.1 pad_add_fusion.where
  22.3 1.6 %index.1 = (s32[8,128]{1,0:T(8,128)S(1)}, s32[128,128]{1,0:T(8,128)S(1)}) custom-call(s32[128,128]{1,0:T(8,128)} %bitcast.53), custom_call_target="tpu_custom_call" | custom-call | tf_op jit(solution)/shard_map/index/pallas_call | solution.py:313
  23.9 3.2 %all-to-all-done.16 = s32[32,1,128]{2,1,0:T(1,128)S(1)} async-done(((s32[32,1,128]{2,1,0:T(1,128)}), s32[32,1,128]{2,1,0:T(1,128)S(1)}, u32[]{:S(2)}, u32[]{:S(2)}) %all-to-all-start.16) | async-done | bytes 16416 | tf_op jit(solution)/shard_map/all_to_all | solution.py:287
  27.1 0.6 slice_reduce_fusion
  28.4 3.8 %fill.1.filled = f32[128,8,128]{2,1,0:T(8,128)S(1)} custom-call(s32[2]{0:T(128)S(1)} %pad_add_fusion.where, s32[32,128]{1,0:T(8,128)S(1)} %bitcast.42, s32[8,128]{1,0:T(8,128)S(1)} %get-tuple-element.88.start, s32[128,128]{1,0:T(8,128)S(1)} %get-tuple-element.89.index, f32[3,16384]{1,0:T(4,128)} %means.3, f32[3,16384]{1,0:T(4,128)} %scales.3, ...), custom_call_target="tpu_custom_call" | custom-call | tf_op jit(solution)/shard_map/fill/pallas_call | solution.py:324
  32.2 0.0 collective-permute-done.11.sq3
  32.2 0.0 collective-permute-done.10.sq2
  32.2 0.0 collective-permute-done.9.sq1
  32.2 1.7 %peaks.1 = (f32[128,8,128]{2,1,0:T(8,128)S(1)}, f32[2,16384]{1,0:T(2,128)}) custom-call(s32[2]{0:T(128)S(1)} %pad_add_fusion.where, s32[32,128]{1,0:T(8,128)S(1)} %bitcast.43, s32[8,128]{1,0:T(8,128)S(1)} %get-tuple-element.88.start, s32[128,128]{1,0:T(8,128)S(1)} %get-tuple-element.89.index, f32[2,128,128]{2,1,0:T(8,128)S(1)} %max.7.sq0, ...), custom_call_target="tpu_custom_call" | custom-call | tf_op jit(solution)/shard_map/peaks/pallas_call | solution.py:346
  33.9 48.8 %conditional.1 = (f32[61,16384]{1,0:T(8,128)}) conditional(s32[]{:T(128)} %clamp.3, (f32[128,8,128]{2,1,0:T(8,128)S(1)}, s32[2]{0:T(128)S(1)}, s32[32,128]{1,0:T(8,128)S(1)}) %tuple.43, (f32[128,8,128]{2,1,0:T(8,128)S(1)}, s32[2]{0:T(128)S(1)}, s32[32,128]{1,0:T(8,128)S(1)}) %tuple.44, (f32[128,8,128]{2,1,0:T(8,128)S(1)}, ...), branch_computations={%region_1.2_spmd, %region_2.3_spmd, %region_3.4_spmd, %region_4.5_... | conditional | bytes 13631536 | solution.py:398
  33.9 21.8 %all_to_all.81 = f32[32,4,8,128]{3,2,1,0:T(8,128)S(1)} all-to-all(f32[32,4,8,128]{3,2,1,0:T(8,128)S(1)} %bitcast.28), channel_id=1, replica_groups=mesh['view'=8,'gauss'=32] {'gauss'}, dimensions={0} | all-to-all | bytes 1048576 | tf_op jit(solution)/shard_map/cond/branch_3_fun/all_to_all | solution.py:365
  55.7 1.2 %place.11 = f32[4,64,8,128]{3,2,1,0:T(8,128)S(1)} custom-call(s32[2]{0:T(128)S(1)} %get-tuple-element.66.where, s32[32,128]{1,0:T(8,128)S(1)} %get-tuple-element.67.counts, f32[128,8,128]{2,1,0:T(8,128)S(1)} %bitcast.37), custom_call_target="tpu_custom_call" | custom-call | tf_op jit(solution)/shard_map/cond/branch_3_fun/place/pallas_call | solution.py:368
  56.9 17.3 %all_to_all.82.own = f32[4,64,8,128]{3,2,1,0:T(8,128)S(1)} all-to-all(f32[4,64,8,128]{3,2,1,0:T(8,128)S(1)} %place.11), channel_id=1, replica_groups={{0,64,128,192},{32,96,160,224},{1,65,129,193},{33,97,161,225},{2,66,130..., dimensions={0} | all-to-all | bytes 2097152 | tf_op jit(solution)/shard_map/cond/branch_3_fun/all_to_all | solution.py:378
  74.2 3.3 %collective-permute-start.3 = (f32[4,64,8,128]{3,2,1,0:T(8,128)S(1)}, f32[4,64,8,128]{3,2,1,0:T(8,128)S(1)}, u32[]{:S(2)}, u32[]{:S(2)}) collective-permute-start(f32[4,64,8,128]{3,2,1,0:T(8,128)S(1)} %all_to_all.82.own), channel_id=1, source_target_pairs={{0,32},{32,0},{64,96},{96,64},{128,160},{160,128},{192,224},{224,1... | collective-permute-start | bytes 3145736 | tf_op jit(solution)/shard_map/cond/branch_3_fun/ppermute | solution.py:379
  77.4 2.3 %collective-permute-done.3.other = f32[4,64,8,128]{3,2,1,0:T(8,128)S(1)} collective-permute-done((f32[4,64,8,128]{3,2,1,0:T(8,128)S(1)}, f32[4,64,8,128]{3,2,1,0:T(8,128)S(1)}, u32[]{:S(2)}, u32[]{:S(2)}) %collective-permute-start.3) | collective-permute-done | bytes 1048608 | tf_op jit(solution)/shard_map/cond/branch_3_fun/ppermute | solution.py:379
  79.7 3.0 %join.11 = f32[61,16384]{1,0:T(8,128)} custom-call(s32[2]{0:T(128)S(1)} %get-tuple-element.66.where, f32[4,64,8,128]{3,2,1,0:T(8,128)S(1)} %all_to_all.82.own, f32[4,64,8,128]{3,2,1,0:T(8,128)S(1)} %collective-permute-done.3.other), custom_call_target="tpu_custom_call" | custom-call | tf_op jit(solution)/shard_map/cond/branch_3_fun/join/pallas_call | solution.py:380
  (1 shorter events, 0.0 us)
Async XLA Ops:
  4.2 14.3 %collective-permute-start.8 = (f32[2,128,128]{2,1,0:T(8,128)S(1)}, f32[2,128,128]{2,1,0:T(8,128)S(1)}, u32[]{:S(2)}, u32[]{:S(2)}) collective-permute-start(f32[2,128,128]{2,1,0:T(8,128)S(1)} %views.1), channel_id=1, source_target_pairs={{0,32},{32,0},{64,96},{96,64},{128,160},{160,128},{192,224},{224,1... | collective-permute-start | bytes 393224 | tf_op jit(solution)/shard_map/ppermute | solution.py:307
  9.0 18.1 %all-to-all-start.16 = ((s32[32,1,128]{2,1,0:T(1,128)}), s32[32,1,128]{2,1,0:T(1,128)S(1)}, u32[]{:S(2)}, u32[]{:S(2)}) async-start(s32[32,1,128]{2,1,0:T(1,128)} %bitcast.20), calls=%async_computation.16 | async-start | bytes 32768 | tf_op jit(solution)/shard_map/all_to_all | solution.py:287
  18.5 13.6 %collective-permute-start.11 = (f32[2,128,128]{2,1,0:T(8,128)S(1)}, f32[2,128,128]{2,1,0:T(8,128)S(1)}, u32[]{:S(2)}, u32[]{:S(2)}) collective-permute-start(f32[2,128,128]{2,1,0:T(8,128)S(1)} %max.7.sq0), channel_id=1, source_target_pairs={{0,192},{32,224},{64,0},{96,32},{128,64},{160,96},{192,128},{224,1... | collective-permute-start | bytes 393224 | tf_op jit(solution)/shard_map/ppermute | solution.py:311
  21.1 11.1 %collective-permute-start.10 = (f32[2,128,128]{2,1,0:T(8,128)S(1)}, f32[2,128,128]{2,1,0:T(8,128)S(1)}, u32[]{:S(2)}, u32[]{:S(2)}) collective-permute-start(f32[2,128,128]{2,1,0:T(8,128)S(1)} %max.7.sq0), channel_id=1, source_target_pairs={{0,128},{32,160},{64,192},{96,224},{128,0},{160,32},{192,64},{224,... | collective-permute-start | bytes 393224 | tf_op jit(solution)/shard_map/ppermute | solution.py:311
  21.6 10.6 %collective-permute-start.9 = (f32[2,128,128]{2,1,0:T(8,128)S(1)}, f32[2,128,128]{2,1,0:T(8,128)S(1)}, u32[]{:S(2)}, u32[]{:S(2)}) collective-permute-start(f32[2,128,128]{2,1,0:T(8,128)S(1)} %max.7.sq0), channel_id=1, source_target_pairs={{0,64},{32,96},{64,128},{96,160},{128,192},{160,224},{192,0},{224,... | collective-permute-start | bytes 393224 | tf_op jit(solution)/shard_map/ppermute | solution.py:311
  74.2 5.5 %collective-permute-start.3 = (f32[4,64,8,128]{3,2,1,0:T(8,128)S(1)}, f32[4,64,8,128]{3,2,1,0:T(8,128)S(1)}, u32[]{:S(2)}, u32[]{:S(2)}) collective-permute-start(f32[4,64,8,128]{3,2,1,0:T(8,128)S(1)} %all_to_all.82.own), channel_id=1, source_target_pairs={{0,32},{32,0},{64,96},{96,64},{128,160},{160,128},{192,224},{224,1... | collective-permute-start | bytes 3145736 | tf_op jit(solution)/shard_map/cond/branch_3_fun/ppermute | solution.py:379

commit v5 on v4

--- a/solution.py
+++ b/solution.py
@@ -119,7 +119,7 @@
         out_ref[1, rows, :] = lmax
         return carry
 
-    lax.fori_loop(0, G_DEV // 1024, group, 0)
+    lax.fori_loop(0, means.shape[1] // 1024, group, 0)
 
 
 def blocks_before(counts, upto):
@@ -152,7 +152,9 @@
     lax.fori_loop(0, BLOCKS // 8, eight, 0)
 
 
-def fill_kernel(where, counts, start, index, means, scales, quats, low, high, out_ref, rows):
+def fill_kernel(
+    where, counts, start, index, means, scales, quats, low, high, out_ref, sums_ref, pick_ref, rows
+):
     view = where[0]
 
     @pl.when(view == 0)
@@ -178,6 +180,13 @@
         rows[2:3, :] = high[0:1, :]
         rows[3:8, :] = jnp.zeros((5, G_DEV), jnp.float32)
 
+    total = jnp.int32(0)
+    for t in range(SHARDS):
+        total = total + counts[t, 0]
+    sums_ref[0] = total
+    used = blocks_before(counts, SHARDS)
+    pick_ref[0] = jnp.clip(((used + SHARDS * STEP - 1) >> 9) - 1, 0, BLOCKS // STEP - 1)
+
     zero = jnp.zeros((8, LANES), jnp.float32)
     for i in range(BLOCKS):
         out_ref[i] = zero
@@ -188,35 +197,51 @@
     each_block(where, counts, start, index, rows, store)
 
 
-def peak_kernel(where, counts, start, index, sq0, sq1, sq2, sq3, filled, out_ref, peak_ref, rows):
+def peak_kernel(where, counts, start, index, sq0, sq1, sq2, sq3, filled, out_ref, peak_ref, pairs):
+    last = where[0] == 7
     for i in range(BLOCKS):
         out_ref[i] = filled[i]
 
+    def top(k, at):
+        return jnp.maximum(
+            jnp.maximum(sq0[k, at, :], sq1[k, at, :]), jnp.maximum(sq2[k, at, :], sq3[k, at, :])
+        )
+
     for g in range(BLOCKS // 8):
         at = slice(8 * g, 8 * g + 8)
-
-        def top(k):
-            return jnp.maximum(
-                jnp.maximum(sq0[k, at, :], sq1[k, at, :]), jnp.maximum(sq2[k, at, :], sq3[k, at, :])
-            )
-
-        norm = jnp.sqrt(top(0))
-        radius = 3.0 * jnp.sqrt(top(1))
-        for j in range(8):
-            col = slice((8 * g + j) * LANES, (8 * g + j + 1) * LANES)
-            peak_ref[0:1, col] = norm[j : j + 1, :]
-            peak_ref[1:2, col] = radius[j : j + 1, :]
-
-    @pl.when(where[0] == 7)
-    def _():
-        rows[3:5, :] = peak_ref[...]
-        sub = lax.broadcasted_iota(jnp.int32, (8, LANES), 0)
-        ours = (sub == 3) | (sub == 4)
-
-        def store(at, packed, mask):
-            pltpu.store(out_ref.at[at], packed, mask=mask & ours)
-
-        each_block(where, counts, start, index, rows, store)
+        norm = jnp.sqrt(top(0, at))
+        radius = 3.0 * jnp.sqrt(top(1, at))
+        pairs[pl.ds(16 * g, 8, stride=2), :] = norm
+        pairs[pl.ds(16 * g + 1, 8, stride=2), :] = radius
+    for b in range(BLOCKS):
+        peak_ref[:, b * LANES : (b + 1) * LANES] = pairs[2 * b : 2 * b + 2, :]
+
+    @pl.when(last)
+    def _():
+        offset = blocks_before(counts, where[1])
+
+        def place_of(block):
+            return ((offset + block) & (SHARDS - 1)) * PER + (block >> 5)
+
+        def eight(g, carry):
+            at = pl.ds(pl.multiple_of(g * 8, 8), 8)
+            lanes = index[at, :] & (LANES - 1)
+            for k in range(2):
+                rows = pairs[pl.ds(16 * g + k, 8, stride=2), :]
+                pairs[pl.ds(2 * BLOCKS + k, 8, stride=2), :] = jnp.take_along_axis(
+                    rows, lanes, axis=1, mode="promise_in_bounds"
+                )
+            for j in range(8):
+                b = g * 8 + j
+                block = start[0, b] >> 7
+                after = jnp.minimum(block + 1, BLOCKS - 1)
+                code = jnp.broadcast_to(index[pl.ds(b, 1), :], (2, LANES))
+                two = pairs[2 * BLOCKS + 2 * j : 2 * BLOCKS + 2 * j + 2, :]
+                pltpu.store(out_ref.at[place_of(block), 3:5, :], two, mask=(code & 256) != 0)
+                pltpu.store(out_ref.at[place_of(after), 3:5, :], two, mask=(code & 512) != 0)
+            return carry
+
+        lax.fori_loop(0, BLOCKS // 8, eight, 0)
 
 
 def place_kernel(where, counts, arrived, out_ref, slots):
@@ -238,18 +263,30 @@
             out_ref[x, i] = tile
 
 
-def join_kernel(where, own, other, out_ref):
+def join_kernel(where, own, other, out_ref, buf, sems):
     cap = own.shape[1]
     core = where[0] & 1
-    mine = pl.ds(pl.multiple_of(8 * core, 8), 8)
-    theirs = pl.ds(pl.multiple_of(8 - 8 * core, 8), 8)
-    for i in range(BLOCKS):
-        col = slice(i * LANES, (i + 1) * LANES)
-        if i < cap:
-            out_ref[mine, col] = own[0, i]
-            out_ref[theirs, col] = other[0, i]
-        else:
-            out_ref[:, col] = jnp.zeros((16, LANES), jnp.float32)
+
+    def copy(r):
+        rows = min(8, ROWS - 8 * r)
+        return pltpu.make_async_copy(
+            buf.at[r, 0:rows, :], out_ref.at[8 * r : 8 * r + rows, :], sems.at[r]
+        )
+
+    for r in range(8):
+        for half in range(2):
+
+            @pl.when(core == half)
+            def _():
+                piece = own if r % 2 == half else other
+                for i in range(cap):
+                    buf[r, :, i * LANES : (i + 1) * LANES] = piece[r // 2, i]
+
+        for i in range(cap, BLOCKS):
+            buf[r, :, i * LANES : (i + 1) * LANES] = jnp.zeros((8, LANES), jnp.float32)
+        copy(r).start()
+    for r in range(8):
+        copy(r).wait()
 
 
 def smem():
@@ -286,24 +323,24 @@
     )(mask)
     counts = lax.all_to_all(count, "gauss", 0, 0, tiled=True)
 
+    chunk = G_DEV // 4
     squares = pl.pallas_call(
         view_kernel,
-        in_specs=[smem()] * 3 + [vmem()] * 5,
-        out_specs=vmem(),
+        grid=(4,),
+        in_specs=[smem()] * 3
+        + [
+            pl.BlockSpec((3, chunk), lambda i: (0, i)),
+            pl.BlockSpec((3, chunk), lambda i: (0, i)),
+            pl.BlockSpec((4, chunk), lambda i: (0, i)),
+            pl.BlockSpec((VIEWS_DEV, 2, chunk), lambda i: (0, 0, i)),
+            pl.BlockSpec((VIEWS_DEV, chunk), lambda i: (0, i)),
+        ],
+        out_specs=pl.BlockSpec((2, BLOCKS // 4, LANES), lambda i: (0, i, 0)),
         out_shape=VMEM((2, BLOCKS, LANES), f32),
-        scratch_shapes=[pltpu.VMEM((192, LANES), f32)],
+        scratch_shapes=[pltpu.VMEM((216, LANES), f32)],
         compiler_params=LIMIT,
         name="views",
-    )(
-        rotation,
-        shift,
-        focal,
-        means,
-        scales,
-        quats,
-        grad_screen,
-        visible,
-    )
+    )(rotation, shift, focal, means, scales, quats, grad_screen, visible)
     other = lax.ppermute(squares, "view", [(v, v ^ 1) for v in range(8)])
     squares = [jnp.maximum(squares, other)]
     for k in (1, 2, 3):
@@ -321,7 +358,7 @@
         compiler_params=LIMIT,
         name="index",
     )(mask)
-    filled = pl.pallas_call(
+    filled, total, branch = pl.pallas_call(
         fill_kernel,
         grid_spec=pltpu.PrefetchScalarGridSpec(
             num_scalar_prefetch=1,
@@ -336,10 +373,14 @@
                 pl.BlockSpec((8, G_DEV), lambda i, w: (jnp.maximum(w[0] - 2, 0), 0)),
                 pl.BlockSpec((8, G_DEV), lambda i, w: (jnp.maximum(w[0] - 1, 0), 0)),
             ],
-            out_specs=whole(BLOCKS, 8, LANES),
+            out_specs=[whole(BLOCKS, 8, LANES), smem(), smem()],
             scratch_shapes=[pltpu.VMEM((8, G_DEV), f32)],
         ),
-        out_shape=VMEM((BLOCKS, 8, LANES), f32),
+        out_shape=[
+            VMEM((BLOCKS, 8, LANES), f32),
+            jax.ShapeDtypeStruct((1,), i32),
+            jax.ShapeDtypeStruct((1,), i32),
+        ],
         compiler_params=LIMIT,
         name="fill",
     )(where, counts, start, index, means, scales, quats, attrs, attrs)
@@ -351,14 +392,10 @@
             VMEM((BLOCKS, 8, LANES), f32),
             jax.ShapeDtypeStruct((2, G_DEV), f32),
         ],
-        scratch_shapes=[pltpu.VMEM((8, G_DEV), f32)],
+        scratch_shapes=[pltpu.VMEM((2 * BLOCKS + 32, LANES), f32)],
         compiler_params=LIMIT,
         name="peaks",
     )(where, counts, start, index, *squares, filled)
-
-    used = jnp.sum((counts[:, 0] + LANES - 1) >> 7)
-    rounds = (used + SHARDS * STEP - 1) >> 9
-    branch = jnp.clip(rounds - 1, 0, BLOCKS // STEP - 1)
 
     def gather(cap):
         def go(where, counts, outgoing):
@@ -379,16 +416,10 @@
             other = lax.ppermute(own, "view", [(v, v ^ 1) for v in range(8)])
             return pl.pallas_call(
                 join_kernel,
-                grid_spec=pltpu.PrefetchScalarGridSpec(
-                    num_scalar_prefetch=1,
-                    grid=(4,),
-                    in_specs=[
-                        pl.BlockSpec((1, cap, 8, LANES), lambda i, w: (i, 0, 0, 0)),
-                        pl.BlockSpec((1, cap, 8, LANES), lambda i, w: (i, 0, 0, 0)),
-                    ],
-                    out_specs=pl.BlockSpec((16, G_DEV), lambda i, w: (i, 0)),
-                ),
+                in_specs=[smem(), vmem(), vmem()],
+                out_specs=pl.BlockSpec(memory_space=pl.ANY),
                 out_shape=jax.ShapeDtypeStruct((ROWS, G_DEV), f32),
+                scratch_shapes=[pltpu.VMEM((8, 8, G_DEV), f32), pltpu.SemaphoreType.DMA((8,))],
                 compiler_params=LIMIT,
                 name="join",
             )(where, own, other)
@@ -396,13 +427,13 @@
         return go
 
     clones = lax.switch(
-        branch,
+        branch[0],
         [gather(cap) for cap in range(STEP, BLOCKS + 1, STEP)],
         where,
         counts,
         outgoing,
     )
-    return (peak, clones, jnp.sum(counts[:, 0]))
+    return (peak, clones, total[0])
 
 
 def solution(mesh):

time: 83.8 us -> 86.9 us (1.037)
  waiting for transfers between devices: 5.51 us -> 10.2 us
    all_to_all x1, blocking collectives: 21.8 us -> 15.6 us  [go(): lax.all_to_all(outgoing.reshape(SHARDS, PER, 8, LANES), 'gauss', 0, 0, ti...]
    all_to_all x1, blocking collectives: 17.3 us -> 23.1 us  [go(): lax.all_to_all(piece, 'view', 0, 0, axis_index_groups=cores, tiled=True)]
    all_to_all x1, waiting for transfers between devices: 3.21 us -> 6.93 us  [body(): counts = lax.all_to_all(count, 'gauss', 0, 0, tiled=True)]
    ppermute x3, starting transfers between devices: 3.68 us -> 1.97 us  [body(): squares.append(lax.ppermute(squares[0], 'view', pairs))]
    all_to_all x1, starting transfers between devices: 9.5 us -> 11.2 us  [body(): counts = lax.all_to_all(count, 'gauss', 0, 0, tiled=True)]
    ppermute x1, waiting for transfers between devices: 0.01 us -> 0.99 us  [body(): other = lax.ppermute(squares, 'view', [(v, v ^ 1) for v in range(8)])]
  transfers between devices with their start and end apart: 6 -> 6, of which waited for: 2 -> 3; matrix products, arithmetic and copies ran while one was open for 1% -> 0% of each run, Pallas kernels for 8% -> 9%
where the time goes in v5:
time: 86.9 us; the launch traced here: 86.5 us
  blocking collectives  38.7 us (45%)
  starting transfers between devices  19 us (22%)
  Pallas kernels  16.8 us (19%)
  waiting for transfers between devices  10.2 us (12%)
  between operations  1.5 us (2%)
    all_to_all x1, blocking collectives, go(): lax.all_to_all(piece, 'view', 0, 0, axis_index_groups=cores, tiled=True)  23.1 us
    all_to_all x1, blocking collectives, go(): lax.all_to_all(outgoing.reshape(SHARDS, PER, 8, LANES), 'gauss', 0, 0, ti...  15.6 us
    all_to_all x1, starting transfers between devices, body(): counts = lax.all_to_all(count, 'gauss', 0, 0, tiled=True)  11.2 us
    all_to_all x1, waiting for transfers between devices, body(): counts = lax.all_to_all(count, 'gauss', 0, 0, tiled=True)  6.93 us
    pallas_call x1, Pallas kernels, body(): pl.pallas_call(fill_kernel, grid_spec=pltpu.PrefetchScalarGridSpec(num_sc...  4.48 us
    pallas_call x1, Pallas kernels, body(): pl.pallas_call(view_kernel, grid=(4,), in_specs=[smem()] * 3 + [pl.BlockS...  3.79 us
    ppermute x1, starting transfers between devices, body(): other = lax.ppermute(squares, 'view', [(v, v ^ 1) for v in range(8)])  3.29 us
    pallas_call x1, Pallas kernels, go(): pl.pallas_call(join_kernel, in_specs=[smem(), vmem(), vmem()], out_specs=...  2.58 us
  transfers between devices with their start and end apart: 6, of which 3 were waited for; matrix products, arithmetic and copies ran while one was open for 0% of the time, Pallas kernels for 9%

profile of v5, /device:TPU:1, one launch (start us, length us, event | category | flops | bytes accessed | tf_op | source)
XLA Modules:
  0.0 86.5 jit_solution(525363925801120852)
XLA Ops:
  0.6 3.8 %views.1 = f32[2,128,128]{2,1,0:T(8,128)S(1)} custom-call(f32[3,4,3]{2,1,0:T(4,128)} %bitcast.55, f32[4,3]{1,0:T(4,128)} %trans.1, f32[1,4]{1,0:T(1,128)} %bitcast.56, f32[3,16384]{1,0:T(4,128)} %means.3, f32[3,16384]{1,0:T(4,128)} %scales.3, f32[4,16384]{1,0:T(4,128)} %quats.3, f32[4,2,16384]{2,1,0:T(2,128)} %grad.1, s32[4,16384]{1,0:T(4,128)} %seen.1), custom_call_target="tpu_custom_call" | custom-call | tf_op jit(solution)/shard_map/views/pallas_call | solution.py:327
  4.4 3.3 %collective-permute-start.8 = (f32[2,128,128]{2,1,0:T(8,128)S(1)}, f32[2,128,128]{2,1,0:T(8,128)S(1)}, u32[]{:S(2)}, u32[]{:S(2)}) collective-permute-start(f32[2,128,128]{2,1,0:T(8,128)S(1)} %views.1), channel_id=1, source_target_pairs={{0,32},{32,0},{64,96},{96,64},{128,160},{160,128},{192,224},{224,1... | collective-permute-start | bytes 393224 | tf_op jit(solution)/shard_map/ppermute | solution.py:344
  7.7 1.0 %collective-permute-done.8 = f32[2,128,128]{2,1,0:T(8,128)S(1)} collective-permute-done((f32[2,128,128]{2,1,0:T(8,128)S(1)}, f32[2,128,128]{2,1,0:T(8,128)S(1)}, u32[]{:S(2)}, u32[]{:S(2)}) %collective-permute-start.8) | collective-permute-done | bytes 131104 | tf_op jit(solution)/shard_map/ppermute | solution.py:344
  8.7 0.8 collective-permute-start.11
  9.6 0.5 collective-permute-start.10
  10.1 0.6 collective-permute-start.9
  10.7 1.5 %count.1 = s32[32,128]{1,0:T(8,128)} custom-call(s32[128,128]{1,0:T(8,128)} %bitcast.53), custom_call_target="tpu_custom_call" | custom-call | tf_op jit(solution)/shard_map/count/pallas_call | solution.py:316
  12.2 11.2 %all-to-all-start.16 = ((s32[32,1,128]{2,1,0:T(1,128)}), s32[32,1,128]{2,1,0:T(1,128)S(1)}, u32[]{:S(2)}, u32[]{:S(2)}) async-start(s32[32,1,128]{2,1,0:T(1,128)} %bitcast.20), calls=%async_computation.16 | async-start | bytes 32768 | tf_op jit(solution)/shard_map/all_to_all | solution.py:324
  23.5 0.1 pad_add_fusion.where
  23.5 1.6 %index.1 = (s32[8,128]{1,0:T(8,128)S(1)}, s32[128,128]{1,0:T(8,128)S(1)}) custom-call(s32[128,128]{1,0:T(8,128)} %bitcast.54), custom_call_target="tpu_custom_call" | custom-call | tf_op jit(solution)/shard_map/index/pallas_call | solution.py:350
  25.1 6.9 %all-to-all-done.16 = s32[32,1,128]{2,1,0:T(1,128)S(1)} async-done(((s32[32,1,128]{2,1,0:T(1,128)}), s32[32,1,128]{2,1,0:T(1,128)S(1)}, u32[]{:S(2)}, u32[]{:S(2)}) %all-to-all-start.16) | async-done | bytes 16416 | tf_op jit(solution)/shard_map/all_to_all | solution.py:324
  32.0 4.5 %fill.1 = (f32[128,8,128]{2,1,0:T(8,128)S(1)}, s32[1]{0:T(128)}, s32[1]{0:T(128)}) custom-call(s32[2]{0:T(128)S(1)} %pad_add_fusion.where, s32[32,128]{1,0:T(8,128)S(1)} %bitcast.43, s32[8,128]{1,0:T(8,128)S(1)} %get-tuple-element.91.start, s32[128,128]{1,0:T(8,128)S(1)} %get-tuple-element.92.index, f32[3,16384]{1,0:T(4,128)} %means.3, f32[3,16384]{1,0:T(4,128)} %scales.3, ...), custom_call_target="tpu_custom_call" | custom-call | tf_op jit(solution)/shard_map/fill/pallas_call | solution.py:361
  37.2 0.0 collective-permute-done.11.sq3
  37.2 0.0 collective-permute-done.10.sq2
  37.2 0.0 collective-permute-done.9.sq1
  37.2 1.6 %peaks.1 = (f32[128,8,128]{2,1,0:T(8,128)S(1)}, f32[2,16384]{1,0:T(2,128)}) custom-call(s32[2]{0:T(128)S(1)} %pad_add_fusion.where, s32[32,128]{1,0:T(8,128)S(1)} %bitcast.44, s32[8,128]{1,0:T(8,128)S(1)} %get-tuple-element.91.start, s32[128,128]{1,0:T(8,128)S(1)} %get-tuple-element.92.index, f32[2,128,128]{2,1,0:T(8,128)S(1)} %max.3.sq0, ...), custom_call_target="tpu_custom_call" | custom-call | tf_op jit(solution)/shard_map/peaks/pallas_call | solution.py:387
  38.9 47.5 %conditional.1 = (f32[61,16384]{1,0:T(8,128)}) conditional(s32[]{:T(128)} %bitcast.24, (f32[128,8,128]{2,1,0:T(8,128)S(1)}, s32[2]{0:T(128)S(1)}, s32[32,128]{1,0:T(8,128)S(1)}) %tuple.42, (f32[128,8,128]{2,1,0:T(8,128)S(1)}, s32[2]{0:T(128)S(1)}, s32[32,128]{1,0:T(8,128)S(1)}) %tuple.43, ...), branch_computations={%region_0.0_spmd, %region_1.0_spmd, %region_2.0_spmd, %region_3.0_... | conditional | bytes 13631536 | solution.py:429
  38.9 15.6 %all_to_all.81 = f32[32,4,8,128]{3,2,1,0:T(8,128)S(1)} all-to-all(f32[32,4,8,128]{3,2,1,0:T(8,128)S(1)} %bitcast.30), channel_id=1, replica_groups=mesh['view'=8,'gauss'=32] {'gauss'}, dimensions={0} | all-to-all | bytes 1048576 | tf_op jit(solution)/shard_map/cond/branch_3_fun/all_to_all | solution.py:402
  54.4 1.2 %place.11 = f32[4,64,8,128]{3,2,1,0:T(8,128)S(1)} custom-call(s32[2]{0:T(128)S(1)} %get-tuple-element.66.where, s32[32,128]{1,0:T(8,128)S(1)} %get-tuple-element.67.counts, f32[128,8,128]{2,1,0:T(8,128)S(1)} %bitcast.39), custom_call_target="tpu_custom_call" | custom-call | tf_op jit(solution)/shard_map/cond/branch_3_fun/place/pallas_call | solution.py:405
  55.7 23.1 %all_to_all.82.own = f32[4,64,8,128]{3,2,1,0:T(8,128)S(1)} all-to-all(f32[4,64,8,128]{3,2,1,0:T(8,128)S(1)} %place.11), channel_id=1, replica_groups={{0,64,128,192},{32,96,160,224},{1,65,129,193},{33,97,161,225},{2,66,130..., dimensions={0} | all-to-all | bytes 2097152 | tf_op jit(solution)/shard_map/cond/branch_3_fun/all_to_all | solution.py:415
  78.8 2.5 %collective-permute-start.3 = (f32[4,64,8,128]{3,2,1,0:T(8,128)S(1)}, f32[4,64,8,128]{3,2,1,0:T(8,128)S(1)}, u32[]{:S(2)}, u32[]{:S(2)}) collective-permute-start(f32[4,64,8,128]{3,2,1,0:T(8,128)S(1)} %all_to_all.82.own), channel_id=1, source_target_pairs={{0,32},{32,0},{64,96},{96,64},{128,160},{160,128},{192,224},{224,1... | collective-permute-start | bytes 3145736 | tf_op jit(solution)/shard_map/cond/branch_3_fun/ppermute | solution.py:416
  81.3 2.3 %collective-permute-done.3.other = f32[4,64,8,128]{3,2,1,0:T(8,128)S(1)} collective-permute-done((f32[4,64,8,128]{3,2,1,0:T(8,128)S(1)}, f32[4,64,8,128]{3,2,1,0:T(8,128)S(1)}, u32[]{:S(2)}, u32[]{:S(2)}) %collective-permute-start.3) | collective-permute-done | bytes 1048608 | tf_op jit(solution)/shard_map/cond/branch_3_fun/ppermute | solution.py:416
  83.6 2.6 %join.11 = f32[61,16384]{1,0:T(8,128)} custom-call(s32[2]{0:T(128)S(1)} %get-tuple-element.66.where, f32[4,64,8,128]{3,2,1,0:T(8,128)S(1)} %all_to_all.82.own, f32[4,64,8,128]{3,2,1,0:T(8,128)S(1)} %collective-permute-done.3.other), custom_call_target="tpu_custom_call" | custom-call | tf_op jit(solution)/shard_map/cond/branch_3_fun/join/pallas_call | solution.py:417
  (1 shorter events, 0.0 us)
Async XLA Ops:
  4.4 4.3 %collective-permute-start.8 = (f32[2,128,128]{2,1,0:T(8,128)S(1)}, f32[2,128,128]{2,1,0:T(8,128)S(1)}, u32[]{:S(2)}, u32[]{:S(2)}) collective-permute-start(f32[2,128,128]{2,1,0:T(8,128)S(1)} %views.1), channel_id=1, source_target_pairs={{0,32},{32,0},{64,96},{96,64},{128,160},{160,128},{192,224},{224,1... | collective-permute-start | bytes 393224 | tf_op jit(solution)/shard_map/ppermute | solution.py:344
  8.7 28.5 %collective-permute-start.11 = (f32[2,128,128]{2,1,0:T(8,128)S(1)}, f32[2,128,128]{2,1,0:T(8,128)S(1)}, u32[]{:S(2)}, u32[]{:S(2)}) collective-permute-start(f32[2,128,128]{2,1,0:T(8,128)S(1)} %max.3.sq0), channel_id=1, source_target_pairs={{0,192},{32,224},{64,0},{96,32},{128,64},{160,96},{192,128},{224,1... | collective-permute-start | bytes 393224 | tf_op jit(solution)/shard_map/ppermute | solution.py:348
  9.6 27.6 %collective-permute-start.10 = (f32[2,128,128]{2,1,0:T(8,128)S(1)}, f32[2,128,128]{2,1,0:T(8,128)S(1)}, u32[]{:S(2)}, u32[]{:S(2)}) collective-permute-start(f32[2,128,128]{2,1,0:T(8,128)S(1)} %max.3.sq0), channel_id=1, source_target_pairs={{0,128},{32,160},{64,192},{96,224},{128,0},{160,32},{192,64},{224,... | collective-permute-start | bytes 393224 | tf_op jit(solution)/shard_map/ppermute | solution.py:348
  10.1 27.1 %collective-permute-start.9 = (f32[2,128,128]{2,1,0:T(8,128)S(1)}, f32[2,128,128]{2,1,0:T(8,128)S(1)}, u32[]{:S(2)}, u32[]{:S(2)}) collective-permute-start(f32[2,128,128]{2,1,0:T(8,128)S(1)} %max.3.sq0), channel_id=1, source_target_pairs={{0,64},{32,96},{64,128},{96,160},{128,192},{160,224},{192,0},{224,... | collective-permute-start | bytes 393224 | tf_op jit(solution)/shard_map/ppermute | solution.py:348
  12.2 19.8 %all-to-all-start.16 = ((s32[32,1,128]{2,1,0:T(1,128)}), s32[32,1,128]{2,1,0:T(1,128)S(1)}, u32[]{:S(2)}, u32[]{:S(2)}) async-start(s32[32,1,128]{2,1,0:T(1,128)} %bitcast.20), calls=%async_computation.16 | async-start | bytes 32768 | tf_op jit(solution)/shard_map/all_to_all | solution.py:324
  78.8 4.8 %collective-permute-start.3 = (f32[4,64,8,128]{3,2,1,0:T(8,128)S(1)}, f32[4,64,8,128]{3,2,1,0:T(8,128)S(1)}, u32[]{:S(2)}, u32[]{:S(2)}) collective-permute-start(f32[4,64,8,128]{3,2,1,0:T(8,128)S(1)} %all_to_all.82.own), channel_id=1, source_target_pairs={{0,32},{32,0},{64,96},{96,64},{128,160},{160,128},{192,224},{224,1... | collective-permute-start | bytes 3145736 | tf_op jit(solution)/shard_map/cond/branch_3_fun/ppermute | solution.py:416

commit v6 on v5

--- a/solution.py
+++ b/solution.py
@@ -11,7 +11,7 @@
 SHARDS = 32
 PER = BLOCKS // SHARDS
 VIEWS_DEV = 4
-STEP = 16
+CAPS = (16, 32, 40, 48, 56, 64, 80, 96, BLOCKS)
 ROWS = 61
 LIMIT = pltpu.CompilerParams(vmem_limit_bytes=16 * 2**20)
 SMEM = pltpu.MemorySpace.SMEM
@@ -185,7 +185,10 @@
         total = total + counts[t, 0]
     sums_ref[0] = total
     used = blocks_before(counts, SHARDS)
-    pick_ref[0] = jnp.clip(((used + SHARDS * STEP - 1) >> 9) - 1, 0, BLOCKS // STEP - 1)
+    pick = jnp.int32(0)
+    for cap in CAPS[:-1]:
+        pick = pick + jnp.where(used > cap * SHARDS, 1, 0)
+    pick_ref[0] = pick
 
     zero = jnp.zeros((8, LANES), jnp.float32)
     for i in range(BLOCKS):
@@ -197,51 +200,45 @@
     each_block(where, counts, start, index, rows, store)
 
 
-def peak_kernel(where, counts, start, index, sq0, sq1, sq2, sq3, filled, out_ref, peak_ref, pairs):
-    last = where[0] == 7
-    for i in range(BLOCKS):
-        out_ref[i] = filled[i]
-
-    def top(k, at):
-        return jnp.maximum(
-            jnp.maximum(sq0[k, at, :], sq1[k, at, :]), jnp.maximum(sq2[k, at, :], sq3[k, at, :])
-        )
-
+def top_of(squares, k, at):
+    a, b, c, d = (sq[k, at, :] for sq in squares)
+    return jnp.maximum(jnp.maximum(a, b), jnp.maximum(c, d))
+
+
+def add_kernel(where, counts, start, index, sq0, sq1, sq2, sq3, filled, out_ref, pairs):
+    @pl.when(where[0] == 7)
+    def _():
+        offset = blocks_before(counts, where[1])
+
+        def place_of(block):
+            return ((offset + block) & (SHARDS - 1)) * PER + (block >> 5)
+
+        for g in range(BLOCKS // 8):
+            at = slice(8 * g, 8 * g + 8)
+            lanes = index[at, :] & (LANES - 1)
+            for k in range(2):
+                root = jnp.sqrt(top_of((sq0, sq1, sq2, sq3), k, at))
+                pairs[pl.ds(16 * g + k, 8, stride=2), :] = jnp.take_along_axis(
+                    root if k == 0 else 3.0 * root, lanes, axis=1, mode="promise_in_bounds"
+                )
+        for b in range(BLOCKS):
+            block = start[0, b] >> 7
+            after = jnp.minimum(block + 1, BLOCKS - 1)
+            code = jnp.broadcast_to(index[b : b + 1, :], (2, LANES))
+            two = pairs[2 * b : 2 * b + 2, :]
+            pltpu.store(out_ref.at[place_of(block), 3:5, :], two, mask=(code & 256) != 0)
+            pltpu.store(out_ref.at[place_of(after), 3:5, :], two, mask=(code & 512) != 0)
+
+
+def peak_kernel(sq0, sq1, sq2, sq3, peak_ref, pairs):
     for g in range(BLOCKS // 8):
         at = slice(8 * g, 8 * g + 8)
-        norm = jnp.sqrt(top(0, at))
-        radius = 3.0 * jnp.sqrt(top(1, at))
+        norm = jnp.sqrt(top_of((sq0, sq1, sq2, sq3), 0, at))
+        radius = 3.0 * jnp.sqrt(top_of((sq0, sq1, sq2, sq3), 1, at))
         pairs[pl.ds(16 * g, 8, stride=2), :] = norm
         pairs[pl.ds(16 * g + 1, 8, stride=2), :] = radius
     for b in range(BLOCKS):
         peak_ref[:, b * LANES : (b + 1) * LANES] = pairs[2 * b : 2 * b + 2, :]
-
-    @pl.when(last)
-    def _():
-        offset = blocks_before(counts, where[1])
-
-        def place_of(block):
-            return ((offset + block) & (SHARDS - 1)) * PER + (block >> 5)
-
-        def eight(g, carry):
-            at = pl.ds(pl.multiple_of(g * 8, 8), 8)
-            lanes = index[at, :] & (LANES - 1)
-            for k in range(2):
-                rows = pairs[pl.ds(16 * g + k, 8, stride=2), :]
-                pairs[pl.ds(2 * BLOCKS + k, 8, stride=2), :] = jnp.take_along_axis(
-                    rows, lanes, axis=1, mode="promise_in_bounds"
-                )
-            for j in range(8):
-                b = g * 8 + j
-                block = start[0, b] >> 7
-                after = jnp.minimum(block + 1, BLOCKS - 1)
-                code = jnp.broadcast_to(index[pl.ds(b, 1), :], (2, LANES))
-                two = pairs[2 * BLOCKS + 2 * j : 2 * BLOCKS + 2 * j + 2, :]
-                pltpu.store(out_ref.at[place_of(block), 3:5, :], two, mask=(code & 256) != 0)
-                pltpu.store(out_ref.at[place_of(after), 3:5, :], two, mask=(code & 512) != 0)
-            return carry
-
-        lax.fori_loop(0, BLOCKS // 8, eight, 0)
 
 
 def place_kernel(where, counts, arrived, out_ref, slots):
@@ -263,30 +260,50 @@
             out_ref[x, i] = tile
 
 
-def join_kernel(where, own, other, out_ref, buf, sems):
+def row_copy(buf, out_ref, sems, r, columns):
+    rows = min(8, ROWS - 8 * r)
+    return pltpu.make_async_copy(
+        buf.at[r, 0:rows, columns], out_ref.at[8 * r : 8 * r + rows, columns], sems.at[r]
+    )
+
+
+def own_kernel(where, own, out_ref, buf, sems):
     cap = own.shape[1]
     core = where[0] & 1
-
-    def copy(r):
-        rows = min(8, ROWS - 8 * r)
-        return pltpu.make_async_copy(
-            buf.at[r, 0:rows, :], out_ref.at[8 * r : 8 * r + rows, :], sems.at[r]
-        )
-
-    for r in range(8):
-        for half in range(2):
-
-            @pl.when(core == half)
-            def _():
-                piece = own if r % 2 == half else other
+    empty = slice(cap * LANES, G_DEV)
+    for half in range(2):
+
+        @pl.when(core == half)
+        def _():
+            for r in range(8):
+                for i in range(cap, BLOCKS):
+                    buf[r, :, i * LANES : (i + 1) * LANES] = jnp.zeros((8, LANES), jnp.float32)
+                if r % 2 == half:
+                    for i in range(cap):
+                        buf[r, :, i * LANES : (i + 1) * LANES] = own[r // 2, i]
+                    row_copy(buf, out_ref, sems, r, slice(0, G_DEV)).start()
+                elif cap < BLOCKS:
+                    row_copy(buf, out_ref, sems, r, empty).start()
+            for r in range(8):
+                if r % 2 == half:
+                    row_copy(buf, out_ref, sems, r, slice(0, G_DEV)).wait()
+                elif cap < BLOCKS:
+                    row_copy(buf, out_ref, sems, r, empty).wait()
+
+
+def other_kernel(where, other, begun, out_ref, buf, sems):
+    cap = other.shape[1]
+    core = where[0] & 1
+    for half in range(2):
+
+        @pl.when(core == half)
+        def _():
+            for r in range(1 - half, 8, 2):
                 for i in range(cap):
-                    buf[r, :, i * LANES : (i + 1) * LANES] = piece[r // 2, i]
-
-        for i in range(cap, BLOCKS):
-            buf[r, :, i * LANES : (i + 1) * LANES] = jnp.zeros((8, LANES), jnp.float32)
-        copy(r).start()
-    for r in range(8):
-        copy(r).wait()
+                    buf[r, :, i * LANES : (i + 1) * LANES] = other[r // 2, i]
+                row_copy(buf, out_ref, sems, r, slice(0, cap * LANES)).start()
+            for r in range(1 - half, 8, 2):
+                row_copy(buf, out_ref, sems, r, slice(0, cap * LANES)).wait()
 
 
 def smem():
@@ -323,19 +340,10 @@
     )(mask)
     counts = lax.all_to_all(count, "gauss", 0, 0, tiled=True)
 
-    chunk = G_DEV // 4
     squares = pl.pallas_call(
         view_kernel,
-        grid=(4,),
-        in_specs=[smem()] * 3
-        + [
-            pl.BlockSpec((3, chunk), lambda i: (0, i)),
-            pl.BlockSpec((3, chunk), lambda i: (0, i)),
-            pl.BlockSpec((4, chunk), lambda i: (0, i)),
-            pl.BlockSpec((VIEWS_DEV, 2, chunk), lambda i: (0, 0, i)),
-            pl.BlockSpec((VIEWS_DEV, chunk), lambda i: (0, i)),
-        ],
-        out_specs=pl.BlockSpec((2, BLOCKS // 4, LANES), lambda i: (0, i, 0)),
+        in_specs=[smem()] * 3 + [vmem()] * 5,
+        out_specs=vmem(),
         out_shape=VMEM((2, BLOCKS, LANES), f32),
         scratch_shapes=[pltpu.VMEM((216, LANES), f32)],
         compiler_params=LIMIT,
@@ -384,21 +392,19 @@
         compiler_params=LIMIT,
         name="fill",
     )(where, counts, start, index, means, scales, quats, attrs, attrs)
-    outgoing, peak = pl.pallas_call(
-        peak_kernel,
+    outgoing = pl.pallas_call(
+        add_kernel,
         in_specs=[smem()] * 3 + [vmem()] * 6,
-        out_specs=[vmem()] * 2,
-        out_shape=[
-            VMEM((BLOCKS, 8, LANES), f32),
-            jax.ShapeDtypeStruct((2, G_DEV), f32),
-        ],
+        out_specs=vmem(),
+        out_shape=VMEM((BLOCKS, 8, LANES), f32),
+        input_output_aliases={8: 0},
         scratch_shapes=[pltpu.VMEM((2 * BLOCKS + 32, LANES), f32)],
         compiler_params=LIMIT,
-        name="peaks",
+        name="add",
     )(where, counts, start, index, *squares, filled)
 
     def gather(cap):
-        def go(where, counts, outgoing):
+        def go(where, counts, outgoing, *squares):
             arrived = lax.all_to_all(
                 outgoing.reshape(SHARDS, PER, 8, LANES), "gauss", 0, 0, tiled=True
             ).reshape(BLOCKS, 8, LANES)
@@ -414,24 +420,40 @@
             cores = [[0, 2, 4, 6], [1, 3, 5, 7]]
             own = lax.all_to_all(piece, "view", 0, 0, axis_index_groups=cores, tiled=True)
             other = lax.ppermute(own, "view", [(v, v ^ 1) for v in range(8)])
-            return pl.pallas_call(
-                join_kernel,
-                in_specs=[smem(), vmem(), vmem()],
+            peak = pl.pallas_call(
+                peak_kernel,
+                in_specs=[vmem()] * 4,
+                out_specs=vmem(),
+                out_shape=pltpu.MemorySpace.HBM((2, G_DEV), f32),
+                scratch_shapes=[pltpu.VMEM((2 * BLOCKS + 32, LANES), f32)],
+                compiler_params=LIMIT,
+                name="peaks",
+            )(*squares)
+            begun = pl.pallas_call(
+                own_kernel,
+                in_specs=[smem(), vmem()],
                 out_specs=pl.BlockSpec(memory_space=pl.ANY),
                 out_shape=jax.ShapeDtypeStruct((ROWS, G_DEV), f32),
                 scratch_shapes=[pltpu.VMEM((8, 8, G_DEV), f32), pltpu.SemaphoreType.DMA((8,))],
                 compiler_params=LIMIT,
-                name="join",
-            )(where, own, other)
+                name="own",
+            )(where, own)
+            clones = pl.pallas_call(
+                other_kernel,
+                in_specs=[smem(), vmem(), pl.BlockSpec(memory_space=pl.ANY)],
+                out_specs=pl.BlockSpec(memory_space=pl.ANY),
+                out_shape=jax.ShapeDtypeStruct((ROWS, G_DEV), f32),
+                input_output_aliases={2: 0},
+                scratch_shapes=[pltpu.VMEM((8, 8, G_DEV), f32), pltpu.SemaphoreType.DMA((8,))],
+                compiler_params=LIMIT,
+                name="other",
+            )(where, other, begun)
+            return peak, clones
 
         return go
 
-    clones = lax.switch(
-        branch[0],
-        [gather(cap) for cap in range(STEP, BLOCKS + 1, STEP)],
-        where,
-        counts,
-        outgoing,
+    peak, clones = lax.switch(
+        branch[0], [gather(cap) for cap in CAPS], where, counts, outgoing, *squares
     )
     return (peak, clones, total[0])
 

time: 86.9 us -> 79.8 us (0.918)
  blocking collectives: 38.7 us -> 28.1 us
  starting transfers between devices: 19 us -> 23.1 us
  waiting for transfers between devices: 10.2 us -> 7.93 us
  Pallas kernels: 16.8 us -> 17.8 us
    all_to_all x1, blocking collectives: 23.1 us -> 12.5 us  [go(): lax.all_to_all(piece, 'view', 0, 0, axis_index_groups=cores, tiled=True)]
    ppermute x1, starting transfers between devices: 2.52 us -> 5.47 us  [go(): other = lax.ppermute(own, 'view', [(v, v ^ 1) for v in range(8)])]
    ppermute x1, waiting for transfers between devices: 2.29 us -> 0.01 us  [go(): other = lax.ppermute(own, 'view', [(v, v ^ 1) for v in range(8)])]
    ppermute x3, starting transfers between devices: 1.97 us -> 3.18 us  [body(): squares.append(lax.ppermute(squares[0], 'view', pairs))]
    pallas_call x3 -> x5, Pallas kernels: 8 us -> 8.96 us  [the longest x1 3.53 us: body(): pl.pallas_call(view_kernel, in_specs=[smem()] * 3 + [vmem()] * 5, out_spe...]
  transfers between devices with their start and end apart: 6 -> 6, of which waited for: 3 -> 2; matrix products, arithmetic and copies ran while one was open for 0% -> 0% of each run, Pallas kernels for 9% -> 13%
where the time goes in v6:
time: 79.8 us; the launch traced here: 78.8 us
  blocking collectives  28.1 us (35%)
  starting transfers between devices  23.1 us (29%)
  Pallas kernels  17.8 us (22%)
  waiting for transfers between devices  7.93 us (10%)
  between operations  1.51 us (2%)
    all_to_all x1, blocking collectives, go(): lax.all_to_all(outgoing.reshape(SHARDS, PER, 8, LANES), 'gauss', 0, 0, ti...  15.6 us
    all_to_all x1, blocking collectives, go(): lax.all_to_all(piece, 'view', 0, 0, axis_index_groups=cores, tiled=True)  12.5 us
    all_to_all x1, starting transfers between devices, body(): counts = lax.all_to_all(count, 'gauss', 0, 0, tiled=True)  11.2 us
    all_to_all x1, waiting for transfers between devices, body(): counts = lax.all_to_all(count, 'gauss', 0, 0, tiled=True)  6.93 us
    ppermute x1, starting transfers between devices, go(): other = lax.ppermute(own, 'view', [(v, v ^ 1) for v in range(8)])  5.47 us
    pallas_call x1, Pallas kernels, body(): pl.pallas_call(fill_kernel, grid_spec=pltpu.PrefetchScalarGridSpec(num_sc...  4.5 us
    pallas_call x1, Pallas kernels, body(): pl.pallas_call(view_kernel, in_specs=[smem()] * 3 + [vmem()] * 5, out_spe...  3.53 us
    ppermute x1, starting transfers between devices, body(): other = lax.ppermute(squares, 'view', [(v, v ^ 1) for v in range(8)])  3.29 us
  transfers between devices with their start and end apart: 6, of which 2 were waited for; matrix products, arithmetic and copies ran while one was open for 0% of the time, Pallas kernels for 13%

profile of v6, /device:TPU:1, one launch (start us, length us, event | category | flops | bytes accessed | tf_op | source)
XLA Modules:
  0.0 78.8 jit_solution(14364709808210453408)
XLA Ops:
  0.6 3.5 %views.1 = f32[2,128,128]{2,1,0:T(8,128)S(1)} custom-call(f32[3,4,3]{2,1,0:T(4,128)} %bitcast.60, f32[4,3]{1,0:T(4,128)} %trans.1, f32[1,4]{1,0:T(1,128)} %bitcast.61, f32[3,16384]{1,0:T(4,128)} %means.3, f32[3,16384]{1,0:T(4,128)} %scales.3, f32[4,16384]{1,0:T(4,128)} %quats.3, f32[4,2,16384]{2,1,0:T(2,128)} %grad.1, s32[4,16384]{1,0:T(4,128)} %seen.1), custom_call_target="tpu_custom_call" | custom-call | tf_op jit(solution)/shard_map/views/pallas_call | solution.py:343
  4.2 3.3 %collective-permute-start.9 = (f32[2,128,128]{2,1,0:T(8,128)S(1)}, f32[2,128,128]{2,1,0:T(8,128)S(1)}, u32[]{:S(2)}, u32[]{:S(2)}) collective-permute-start(f32[2,128,128]{2,1,0:T(8,128)S(1)} %views.1), channel_id=1, source_target_pairs={{0,32},{32,0},{64,96},{96,64},{128,160},{160,128},{192,224},{224,1... | collective-permute-start | bytes 393224 | tf_op jit(solution)/shard_map/ppermute | solution.py:352
  7.5 1.0 %collective-permute-done.9 = f32[2,128,128]{2,1,0:T(8,128)S(1)} collective-permute-done((f32[2,128,128]{2,1,0:T(8,128)S(1)}, f32[2,128,128]{2,1,0:T(8,128)S(1)}, u32[]{:S(2)}, u32[]{:S(2)}) %collective-permute-start.9) | collective-permute-done | bytes 131104 | tf_op jit(solution)/shard_map/ppermute | solution.py:352
  8.5 0.1 collective-permute-start.10
  8.5 1.9 %collective-permute-start.11 = (f32[2,128,128]{2,1,0:T(8,128)S(1)}, f32[2,128,128]{2,1,0:T(8,128)S(1)}, u32[]{:S(2)}, u32[]{:S(2)}) collective-permute-start(f32[2,128,128]{2,1,0:T(8,128)S(1)} %max.3.sq0), channel_id=1, source_target_pairs={{0,128},{32,160},{64,192},{96,224},{128,0},{160,32},{192,64},{224,... | collective-permute-start | bytes 393224 | tf_op jit(solution)/shard_map/ppermute | solution.py:356
  10.5 1.2 %collective-permute-start.12 = (f32[2,128,128]{2,1,0:T(8,128)S(1)}, f32[2,128,128]{2,1,0:T(8,128)S(1)}, u32[]{:S(2)}, u32[]{:S(2)}) collective-permute-start(f32[2,128,128]{2,1,0:T(8,128)S(1)} %max.3.sq0), channel_id=1, source_target_pairs={{0,192},{32,224},{64,0},{96,32},{128,64},{160,96},{192,128},{224,1... | collective-permute-start | bytes 393224 | tf_op jit(solution)/shard_map/ppermute | solution.py:356
  11.6 1.5 %count.1 = s32[32,128]{1,0:T(8,128)} custom-call(s32[128,128]{1,0:T(8,128)} %bitcast.58), custom_call_target="tpu_custom_call" | custom-call | tf_op jit(solution)/shard_map/count/pallas_call | solution.py:333
  13.2 11.2 %all-to-all-start.18 = ((s32[32,1,128]{2,1,0:T(1,128)}), s32[32,1,128]{2,1,0:T(1,128)S(1)}, u32[]{:S(2)}, u32[]{:S(2)}) async-start(s32[32,1,128]{2,1,0:T(1,128)} %bitcast.22), calls=%async_computation.18 | async-start | bytes 32768 | tf_op jit(solution)/shard_map/all_to_all | solution.py:341
  24.4 0.1 pad_add_fusion.where
  24.5 1.6 %index.1 = (s32[8,128]{1,0:T(8,128)S(1)}, s32[128,128]{1,0:T(8,128)S(1)}) custom-call(s32[128,128]{1,0:T(8,128)} %bitcast.59), custom_call_target="tpu_custom_call" | custom-call | tf_op jit(solution)/shard_map/index/pallas_call | solution.py:358
  26.1 6.9 %all-to-all-done.18 = s32[32,1,128]{2,1,0:T(1,128)S(1)} async-done(((s32[32,1,128]{2,1,0:T(1,128)}), s32[32,1,128]{2,1,0:T(1,128)S(1)}, u32[]{:S(2)}, u32[]{:S(2)}) %all-to-all-start.18) | async-done | bytes 16416 | tf_op jit(solution)/shard_map/all_to_all | solution.py:341
  33.0 4.5 %fill.1 = (f32[128,8,128]{2,1,0:T(8,128)S(1)}, s32[1]{0:T(128)}, s32[1]{0:T(128)}) custom-call(s32[2]{0:T(128)S(1)} %pad_add_fusion.where, s32[32,128]{1,0:T(8,128)S(1)} %bitcast.47, s32[8,128]{1,0:T(8,128)S(1)} %get-tuple-element.199.start, s32[128,128]{1,0:T(8,128)S(1)} %get-tuple-element.200.index, f32[3,16384]{1,0:T(4,128)} %means.3, f32[3,16384]{1,0:T(4,128)} %scales.3, ...), custom_call_target="tpu_custom_call" | custom-call | tf_op jit(solution)/shard_map/fill/pallas_call | solution.py:369
  38.1 0.0 collective-permute-done.10.sq1
  38.2 0.0 collective-permute-done.11.sq2
  38.2 0.0 collective-permute-done.12.sq3
  38.2 0.9 %add.3 = f32[128,8,128]{2,1,0:T(8,128)S(1)} custom-call(s32[2]{0:T(128)S(1)} %pad_add_fusion.where, s32[32,128]{1,0:T(8,128)S(1)} %bitcast.48, s32[8,128]{1,0:T(8,128)S(1)} %get-tuple-element.199.start, s32[128,128]{1,0:T(8,128)S(1)} %get-tuple-element.200.index, f32[2,128,128]{2,1,0:T(8,128)S(1)} %max.3.sq0, ...), custom_call_target="tpu_custom_call", output_to_operand_aliasing={{}: (8, {})} | custom-call | tf_op jit(solution)/shard_map/add/pallas_call | solution.py:395
  39.1 39.6 %conditional.1 = (f32[2,16384]{1,0:T(2,128)}, f32[61,16384]{1,0:T(8,128)}) conditional(s32[]{:T(128)} %bitcast.24, (f32[2,128,128]{2,1,0:T(8,128)S(1)}, f32[2,128,128]{2,1,0:T(8,128)S(1)}, f32[2,128,128]{2,1,0:T(8,128)S(1)}, f32[2,128,128]{2,1,0:T(8,128)S(1)}, f32[128,8,128]{2,1,0:T(8,128)S(1)}, ...), branch_computations={%region_0.0_spmd, %region_1.0_spmd, %region_2.0_spmd, %region_3.0_... | conditional | bytes 13631544 | solution.py:455
  39.3 15.6 %all_to_all.91 = f32[32,4,8,128]{3,2,1,0:T(8,128)S(1)} all-to-all(f32[32,4,8,128]{3,2,1,0:T(8,128)S(1)} %bitcast.33), channel_id=1, replica_groups=mesh['view'=8,'gauss'=32] {'gauss'}, dimensions={0} | all-to-all | bytes 1048576 | tf_op jit(solution)/shard_map/cond/branch_4_fun/all_to_all | solution.py:408
  54.9 1.2 %place.13 = f32[4,56,8,128]{3,2,1,0:T(8,128)S(1)} custom-call(s32[2]{0:T(128)S(1)} %get-tuple-element.158.where, s32[32,128]{1,0:T(8,128)S(1)} %get-tuple-element.159.counts, f32[128,8,128]{2,1,0:T(8,128)S(1)} %bitcast.43), custom_call_target="tpu_custom_call" | custom-call | tf_op jit(solution)/shard_map/cond/branch_4_fun/place/pallas_call | solution.py:411
  56.1 12.5 %all_to_all.92.own = f32[4,56,8,128]{3,2,1,0:T(8,128)S(1)} all-to-all(f32[4,56,8,128]{3,2,1,0:T(8,128)S(1)} %place.13), channel_id=1, replica_groups={{0,64,128,192},{32,96,160,224},{1,65,129,193},{33,97,161,225},{2,66,130..., dimensions={0} | all-to-all | bytes 1835008 | tf_op jit(solution)/shard_map/cond/branch_4_fun/all_to_all | solution.py:421
  68.6 5.5 %collective-permute-start.4 = (f32[4,56,8,128]{3,2,1,0:T(8,128)S(1)}, f32[4,56,8,128]{3,2,1,0:T(8,128)S(1)}, u32[]{:S(2)}, u32[]{:S(2)}) collective-permute-start(f32[4,56,8,128]{3,2,1,0:T(8,128)S(1)} %all_to_all.92.own), channel_id=1, source_target_pairs={{0,32},{32,0},{64,96},{96,64},{128,160},{160,128},{192,224},{224,1... | collective-permute-start | bytes 2752520 | tf_op jit(solution)/shard_map/cond/branch_4_fun/ppermute | solution.py:422
  74.1 0.7 peaks.13
  74.8 2.3 %own.13.begun = f32[61,16384]{1,0:T(8,128)} custom-call(s32[2]{0:T(128)S(1)} %get-tuple-element.158.where, f32[4,56,8,128]{3,2,1,0:T(8,128)S(1)} %all_to_all.92.own), custom_call_target="tpu_custom_call" | custom-call | tf_op jit(solution)/shard_map/cond/branch_4_fun/own/pallas_call | solution.py:432
  77.1 0.0 collective-permute-done.4.other
  77.1 1.6 %other.13 = f32[61,16384]{1,0:T(8,128)} custom-call(s32[2]{0:T(128)S(1)} %get-tuple-element.158.where, f32[4,56,8,128]{3,2,1,0:T(8,128)S(1)} %collective-permute-done.4.other, f32[61,16384]{1,0:T(8,128)} %own.13.begun), custom_call_target="tpu_custom_call", output_to_operand_aliasing={{}: (2, {})} | custom-call | tf_op jit(solution)/shard_map/cond/branch_4_fun/other/pallas_call | solution.py:441
  (1 shorter events, 0.0 us)
Async XLA Ops:
  4.2 4.3 %collective-permute-start.9 = (f32[2,128,128]{2,1,0:T(8,128)S(1)}, f32[2,128,128]{2,1,0:T(8,128)S(1)}, u32[]{:S(2)}, u32[]{:S(2)}) collective-permute-start(f32[2,128,128]{2,1,0:T(8,128)S(1)} %views.1), channel_id=1, source_target_pairs={{0,32},{32,0},{64,96},{96,64},{128,160},{160,128},{192,224},{224,1... | collective-permute-start | bytes 393224 | tf_op jit(solution)/shard_map/ppermute | solution.py:352
  8.5 29.7 %collective-permute-start.10 = (f32[2,128,128]{2,1,0:T(8,128)S(1)}, f32[2,128,128]{2,1,0:T(8,128)S(1)}, u32[]{:S(2)}, u32[]{:S(2)}) collective-permute-start(f32[2,128,128]{2,1,0:T(8,128)S(1)} %max.3.sq0), channel_id=1, source_target_pairs={{0,64},{32,96},{64,128},{96,160},{128,192},{160,224},{192,0},{224,... | collective-permute-start | bytes 393224 | tf_op jit(solution)/shard_map/ppermute | solution.py:356
  8.5 29.6 %collective-permute-start.11 = (f32[2,128,128]{2,1,0:T(8,128)S(1)}, f32[2,128,128]{2,1,0:T(8,128)S(1)}, u32[]{:S(2)}, u32[]{:S(2)}) collective-permute-start(f32[2,128,128]{2,1,0:T(8,128)S(1)} %max.3.sq0), channel_id=1, source_target_pairs={{0,128},{32,160},{64,192},{96,224},{128,0},{160,32},{192,64},{224,... | collective-permute-start | bytes 393224 | tf_op jit(solution)/shard_map/ppermute | solution.py:356
  10.5 27.7 %collective-permute-start.12 = (f32[2,128,128]{2,1,0:T(8,128)S(1)}, f32[2,128,128]{2,1,0:T(8,128)S(1)}, u32[]{:S(2)}, u32[]{:S(2)}) collective-permute-start(f32[2,128,128]{2,1,0:T(8,128)S(1)} %max.3.sq0), channel_id=1, source_target_pairs={{0,192},{32,224},{64,0},{96,32},{128,64},{160,96},{192,128},{224,1... | collective-permute-start | bytes 393224 | tf_op jit(solution)/shard_map/ppermute | solution.py:356
  13.2 19.8 %all-to-all-start.18 = ((s32[32,1,128]{2,1,0:T(1,128)}), s32[32,1,128]{2,1,0:T(1,128)S(1)}, u32[]{:S(2)}, u32[]{:S(2)}) async-start(s32[32,1,128]{2,1,0:T(1,128)} %bitcast.22), calls=%async_computation.18 | async-start | bytes 32768 | tf_op jit(solution)/shard_map/all_to_all | solution.py:341
  68.6 8.5 %collective-permute-start.4 = (f32[4,56,8,128]{3,2,1,0:T(8,128)S(1)}, f32[4,56,8,128]{3,2,1,0:T(8,128)S(1)}, u32[]{:S(2)}, u32[]{:S(2)}) collective-permute-start(f32[4,56,8,128]{3,2,1,0:T(8,128)S(1)} %all_to_all.92.own), channel_id=1, source_target_pairs={{0,32},{32,0},{64,96},{96,64},{128,160},{160,128},{192,224},{224,1... | collective-permute-start | bytes 2752520 | tf_op jit(solution)/shard_map/cond/branch_4_fun/ppermute | solution.py:422

commit v7 on v6

--- a/solution.py
+++ b/solution.py
@@ -122,15 +122,56 @@
     lax.fori_loop(0, means.shape[1] // 1024, group, 0)
 
 
-def blocks_before(counts, upto):
-    total = jnp.int32(0)
-    for t in range(SHARDS):
-        total = total + jnp.where(t < upto, (counts[t, 0] + LANES - 1) // LANES, 0)
-    return total
-
-
-def each_block(where, counts, start, index, rows, store):
-    offset = blocks_before(counts, where[1])
+def fill_kernel(
+    where, counts, start, index, means, scales, quats, low, high,
+    out_ref, sums_ref, pick_ref, table, rows
+):
+    view = where[0]
+
+    @pl.when(view == 0)
+    def _():
+        rows[0:3, :] = means[...]
+        rows[3:6, :] = scales[...]
+        rows[6:8, :] = quats[0:2, :]
+
+    @pl.when(view == 1)
+    def _():
+        rows[0:2, :] = quats[2:4, :]
+
+    @pl.when(view > 1)
+    def _():
+        rows[0:2, :] = low[6:8, :]
+
+    @pl.when((view > 0) & (view < 7))
+    def _():
+        rows[2:8, :] = high[0:6, :]
+
+    @pl.when(view == 7)
+    def _():
+        rows[2:3, :] = high[0:1, :]
+        rows[3:8, :] = jnp.zeros((5, G_DEV), jnp.float32)
+
+    zero = jnp.zeros((8, LANES), jnp.float32)
+    for i in range(BLOCKS):
+        out_ref[i] = zero
+
+    mine = where[1]
+    total = offset = used = jnp.int32(0)
+    for s in range(SHARDS):
+        offset = jnp.where(s == mine, used, offset)
+        local = (mine - used) & (SHARDS - 1)
+        first = (used + local) >> 5
+        for w in range(PER):
+            table[BLOCKS + s * PER + w] = first + w
+        count = counts[s, 0]
+        total = total + count
+        used = used + ((count + LANES - 1) >> 7)
+    sums_ref[0] = total
+    pick = jnp.int32(0)
+    for cap in CAPS[:-1]:
+        pick = pick + jnp.where(used > cap * SHARDS, 1, 0)
+    pick_ref[0] = pick
+    table[2 * BLOCKS] = view
 
     def place_of(block):
         return ((offset + block) & (SHARDS - 1)) * PER + (block >> 5)
@@ -139,65 +180,19 @@
         for j in range(8):
             b = i * 8 + j
             block = start[0, b] >> 7
+            here = place_of(block)
+            after = place_of(jnp.minimum(block + 1, BLOCKS - 1))
+            table[b] = here + (after << 8)
             code = jnp.broadcast_to(index[pl.ds(b, 1), :], (8, LANES))
             tile = rows[:, pl.ds(pl.multiple_of(b * LANES, LANES), LANES)]
             packed = jnp.take_along_axis(
                 tile, code & (LANES - 1), axis=1, mode="promise_in_bounds"
             )
-            store(place_of(block), packed, (code & 256) != 0)
-            after = jnp.minimum(block + 1, BLOCKS - 1)
-            store(place_of(after), packed, (code & 512) != 0)
+            pltpu.store(out_ref.at[here], packed, mask=(code & 256) != 0)
+            pltpu.store(out_ref.at[after], packed, mask=(code & 512) != 0)
         return carry
 
     lax.fori_loop(0, BLOCKS // 8, eight, 0)
-
-
-def fill_kernel(
-    where, counts, start, index, means, scales, quats, low, high, out_ref, sums_ref, pick_ref, rows
-):
-    view = where[0]
-
-    @pl.when(view == 0)
-    def _():
-        rows[0:3, :] = means[...]
-        rows[3:6, :] = scales[...]
-        rows[6:8, :] = quats[0:2, :]
-
-    @pl.when(view == 1)
-    def _():
-        rows[0:2, :] = quats[2:4, :]
-
-    @pl.when(view > 1)
-    def _():
-        rows[0:2, :] = low[6:8, :]
-
-    @pl.when((view > 0) & (view < 7))
-    def _():
-        rows[2:8, :] = high[0:6, :]
-
-    @pl.when(view == 7)
-    def _():
-        rows[2:3, :] = high[0:1, :]
-        rows[3:8, :] = jnp.zeros((5, G_DEV), jnp.float32)
-
-    total = jnp.int32(0)
-    for t in range(SHARDS):
-        total = total + counts[t, 0]
-    sums_ref[0] = total
-    used = blocks_before(counts, SHARDS)
-    pick = jnp.int32(0)
-    for cap in CAPS[:-1]:
-        pick = pick + jnp.where(used > cap * SHARDS, 1, 0)
-    pick_ref[0] = pick
-
-    zero = jnp.zeros((8, LANES), jnp.float32)
-    for i in range(BLOCKS):
-        out_ref[i] = zero
-
-    def store(at, packed, mask):
-        pltpu.store(out_ref.at[at], packed, mask=mask)
-
-    each_block(where, counts, start, index, rows, store)
 
 
 def top_of(squares, k, at):
@@ -205,14 +200,9 @@
     return jnp.maximum(jnp.maximum(a, b), jnp.maximum(c, d))
 
 
-def add_kernel(where, counts, start, index, sq0, sq1, sq2, sq3, filled, out_ref, pairs):
-    @pl.when(where[0] == 7)
-    def _():
-        offset = blocks_before(counts, where[1])
-
-        def place_of(block):
-            return ((offset + block) & (SHARDS - 1)) * PER + (block >> 5)
-
+def add_kernel(table, index, sq0, sq1, sq2, sq3, filled, out_ref, pairs):
+    @pl.when(table[2 * BLOCKS] == 7)
+    def _():
         for g in range(BLOCKS // 8):
             at = slice(8 * g, 8 * g + 8)
             lanes = index[at, :] & (LANES - 1)
@@ -222,12 +212,11 @@
                     root if k == 0 else 3.0 * root, lanes, axis=1, mode="promise_in_bounds"
                 )
         for b in range(BLOCKS):
-            block = start[0, b] >> 7
-            after = jnp.minimum(block + 1, BLOCKS - 1)
+            both = table[b]
             code = jnp.broadcast_to(index[b : b + 1, :], (2, LANES))
             two = pairs[2 * b : 2 * b + 2, :]
-            pltpu.store(out_ref.at[place_of(block), 3:5, :], two, mask=(code & 256) != 0)
-            pltpu.store(out_ref.at[place_of(after), 3:5, :], two, mask=(code & 512) != 0)
+            pltpu.store(out_ref.at[both & 255, 3:5, :], two, mask=(code & 256) != 0)
+            pltpu.store(out_ref.at[both >> 8, 3:5, :], two, mask=(code & 512) != 0)
 
 
 def peak_kernel(sq0, sq1, sq2, sq3, peak_ref, pairs):
@@ -241,19 +230,13 @@
         peak_ref[:, b * LANES : (b + 1) * LANES] = pairs[2 * b : 2 * b + 2, :]
 
 
-def place_kernel(where, counts, arrived, out_ref, slots):
+def place_kernel(table, arrived, out_ref, slots):
     cap = out_ref.shape[1]
-    mine = where[1]
     zero = jnp.zeros((8, LANES), jnp.float32)
     for i in range(cap):
         slots[i] = zero
-    before = jnp.int32(0)
-    for s in range(SHARDS):
-        local = (mine - before) & (SHARDS - 1)
-        first = (before + local) >> 5
-        for w in range(PER):
-            slots[jnp.minimum(first + w, cap)] = arrived[s * PER + w]
-        before = before + (counts[s, 0] + LANES - 1) // LANES
+    for i in range(BLOCKS):
+        slots[jnp.minimum(table[BLOCKS + i], cap)] = arrived[i]
     for i in range(cap):
         tile = slots[i]
         for x in range(4):
@@ -267,28 +250,37 @@
     )
 
 
-def own_kernel(where, own, out_ref, buf, sems):
+def own_kernel(where, own, out_ref, buf, zeros, sems):
     cap = own.shape[1]
     core = where[0] & 1
-    empty = slice(cap * LANES, G_DEV)
+
+    def clear(r):
+        rows = min(8, ROWS - 8 * r)
+        return pltpu.make_async_copy(
+            zeros.at[0:rows, :],
+            out_ref.at[8 * r : 8 * r + rows, cap * LANES : G_DEV],
+            sems.at[8 + r],
+        )
+
+    if cap < BLOCKS:
+        for i in range(BLOCKS - cap):
+            zeros[:, i * LANES : (i + 1) * LANES] = jnp.zeros((8, LANES), jnp.float32)
+        for r in range(8):
+            clear(r).start()
     for half in range(2):
 
         @pl.when(core == half)
         def _():
-            for r in range(8):
-                for i in range(cap, BLOCKS):
-                    buf[r, :, i * LANES : (i + 1) * LANES] = jnp.zeros((8, LANES), jnp.float32)
-                if r % 2 == half:
-                    for i in range(cap):
-                        buf[r, :, i * LANES : (i + 1) * LANES] = own[r // 2, i]
-                    row_copy(buf, out_ref, sems, r, slice(0, G_DEV)).start()
-                elif cap < BLOCKS:
-                    row_copy(buf, out_ref, sems, r, empty).start()
-            for r in range(8):
-                if r % 2 == half:
-                    row_copy(buf, out_ref, sems, r, slice(0, G_DEV)).wait()
-                elif cap < BLOCKS:
-                    row_copy(buf, out_ref, sems, r, empty).wait()
+            for r in range(half, 8, 2):
+                for i in range(cap):
+                    buf[r, :, i * LANES : (i + 1) * LANES] = own[r // 2, i]
+                row_copy(buf, out_ref, sems, r, slice(0, cap * LANES)).start()
+            for r in range(half, 8, 2):
+                row_copy(buf, out_ref, sems, r, slice(0, cap * LANES)).wait()
+
+    if cap < BLOCKS:
+        for r in range(8):
+            clear(r).wait()
 
 
 def other_kernel(where, other, begun, out_ref, buf, sems):
@@ -366,7 +358,7 @@
         compiler_params=LIMIT,
         name="index",
     )(mask)
-    filled, total, branch = pl.pallas_call(
+    filled, total, branch, table = pl.pallas_call(
         fill_kernel,
         grid_spec=pltpu.PrefetchScalarGridSpec(
             num_scalar_prefetch=1,
@@ -381,42 +373,43 @@
                 pl.BlockSpec((8, G_DEV), lambda i, w: (jnp.maximum(w[0] - 2, 0), 0)),
                 pl.BlockSpec((8, G_DEV), lambda i, w: (jnp.maximum(w[0] - 1, 0), 0)),
             ],
-            out_specs=[whole(BLOCKS, 8, LANES), smem(), smem()],
+            out_specs=[whole(BLOCKS, 8, LANES), smem(), smem(), smem()],
             scratch_shapes=[pltpu.VMEM((8, G_DEV), f32)],
         ),
         out_shape=[
             VMEM((BLOCKS, 8, LANES), f32),
             jax.ShapeDtypeStruct((1,), i32),
             jax.ShapeDtypeStruct((1,), i32),
+            VMEM((3 * BLOCKS,), i32),
         ],
         compiler_params=LIMIT,
         name="fill",
     )(where, counts, start, index, means, scales, quats, attrs, attrs)
     outgoing = pl.pallas_call(
         add_kernel,
-        in_specs=[smem()] * 3 + [vmem()] * 6,
+        in_specs=[smem()] + [vmem()] * 6,
         out_specs=vmem(),
         out_shape=VMEM((BLOCKS, 8, LANES), f32),
-        input_output_aliases={8: 0},
+        input_output_aliases={6: 0},
         scratch_shapes=[pltpu.VMEM((2 * BLOCKS + 32, LANES), f32)],
         compiler_params=LIMIT,
         name="add",
-    )(where, counts, start, index, *squares, filled)
+    )(table, index, *squares, filled)
 
     def gather(cap):
-        def go(where, counts, outgoing, *squares):
+        def go(where, table, outgoing, *squares):
             arrived = lax.all_to_all(
                 outgoing.reshape(SHARDS, PER, 8, LANES), "gauss", 0, 0, tiled=True
             ).reshape(BLOCKS, 8, LANES)
             piece = pl.pallas_call(
                 place_kernel,
-                in_specs=[smem(), smem(), vmem()],
+                in_specs=[smem(), vmem()],
                 out_specs=vmem(),
                 out_shape=VMEM((4, cap, 8, LANES), f32),
                 scratch_shapes=[pltpu.VMEM((cap + 1, 8, LANES), f32)],
                 compiler_params=LIMIT,
                 name="place",
-            )(where, counts, arrived)
+            )(table, arrived)
             cores = [[0, 2, 4, 6], [1, 3, 5, 7]]
             own = lax.all_to_all(piece, "view", 0, 0, axis_index_groups=cores, tiled=True)
             other = lax.ppermute(own, "view", [(v, v ^ 1) for v in range(8)])
@@ -434,7 +427,11 @@
                 in_specs=[smem(), vmem()],
                 out_specs=pl.BlockSpec(memory_space=pl.ANY),
                 out_shape=jax.ShapeDtypeStruct((ROWS, G_DEV), f32),
-                scratch_shapes=[pltpu.VMEM((8, 8, G_DEV), f32), pltpu.SemaphoreType.DMA((8,))],
+                scratch_shapes=[
+                    pltpu.VMEM((8, 8, cap * LANES), f32),
+                    pltpu.VMEM((8, max(BLOCKS - cap, 1) * LANES), f32),
+                    pltpu.SemaphoreType.DMA((16,)),
+                ],
                 compiler_params=LIMIT,
                 name="own",
             )(where, own)
@@ -444,7 +441,10 @@
                 out_specs=pl.BlockSpec(memory_space=pl.ANY),
                 out_shape=jax.ShapeDtypeStruct((ROWS, G_DEV), f32),
                 input_output_aliases={2: 0},
-                scratch_shapes=[pltpu.VMEM((8, 8, G_DEV), f32), pltpu.SemaphoreType.DMA((8,))],
+                scratch_shapes=[
+                    pltpu.VMEM((8, 8, cap * LANES), f32),
+                    pltpu.SemaphoreType.DMA((8,)),
+                ],
                 compiler_params=LIMIT,
                 name="other",
             )(where, other, begun)
@@ -453,7 +453,7 @@
         return go
 
     peak, clones = lax.switch(
-        branch[0], [gather(cap) for cap in CAPS], where, counts, outgoing, *squares
+        branch[0], [gather(cap) for cap in CAPS], where, table, outgoing, *squares
     )
     return (peak, clones, total[0])
 

time: 79.8 us -> 79.1 us (level)
  blocking collectives: 28.1 us -> 27 us
  Pallas kernels: 17.8 us -> 17 us
  starting transfers between devices: 23.1 us -> 23.9 us
    all_to_all x1, blocking collectives: 12.5 us -> 11.5 us  [go(): lax.all_to_all(piece, 'view', 0, 0, axis_index_groups=cores, tiled=True)]
  transfers between devices with their start and end apart: 6 -> 6, of which waited for: 2 -> 2; matrix products, arithmetic and copies ran while one was open for 0% -> 0% of each run, Pallas kernels for 13% -> 14%
where the time goes in v7:
time: 79.1 us; the launch traced here: 77.9 us
  blocking collectives  27 us (34%)
  starting transfers between devices  23.9 us (30%)
  Pallas kernels  17 us (21%)
  waiting for transfers between devices  7.93 us (10%)
  between operations  1.53 us (2%)
    all_to_all x1, blocking collectives, go(): lax.all_to_all(outgoing.reshape(SHARDS, PER, 8, LANES), 'gauss', 0, 0, ti...  15.6 us
    all_to_all x1, blocking collectives, go(): lax.all_to_all(piece, 'view', 0, 0, axis_index_groups=cores, tiled=True)  11.5 us
    all_to_all x1, starting transfers between devices, body(): counts = lax.all_to_all(count, 'gauss', 0, 0, tiled=True)  11.2 us
    all_to_all x1, waiting for transfers between devices, body(): counts = lax.all_to_all(count, 'gauss', 0, 0, tiled=True)  6.93 us
    ppermute x1, starting transfers between devices, go(): other = lax.ppermute(own, 'view', [(v, v ^ 1) for v in range(8)])  6.18 us
    pallas_call x1, Pallas kernels, body(): pl.pallas_call(fill_kernel, grid_spec=pltpu.PrefetchScalarGridSpec(num_sc...  4.36 us
    pallas_call x1, Pallas kernels, body(): pl.pallas_call(view_kernel, in_specs=[smem()] * 3 + [vmem()] * 5, out_spe...  3.53 us
    ppermute x1, starting transfers between devices, body(): other = lax.ppermute(squares, 'view', [(v, v ^ 1) for v in range(8)])  3.29 us
  transfers between devices with their start and end apart: 6, of which 2 were waited for; matrix products, arithmetic and copies ran while one was open for 0% of the time, Pallas kernels for 14%

profile of v7, /device:TPU:1, one launch (start us, length us, event | category | flops | bytes accessed | tf_op | source)
XLA Modules:
  0.0 77.9 jit_solution(14176679278722123373)
XLA Ops:
  0.6 3.5 %views.1 = f32[2,128,128]{2,1,0:T(8,128)S(1)} custom-call(f32[3,4,3]{2,1,0:T(4,128)} %bitcast.50, f32[4,3]{1,0:T(4,128)} %trans.1, f32[1,4]{1,0:T(1,128)} %bitcast.51, f32[3,16384]{1,0:T(4,128)} %means.3, f32[3,16384]{1,0:T(4,128)} %scales.3, f32[4,16384]{1,0:T(4,128)} %quats.3, f32[4,2,16384]{2,1,0:T(2,128)} %grad.1, s32[4,16384]{1,0:T(4,128)} %seen.1), custom_call_target="tpu_custom_call" | custom-call | tf_op jit(solution)/shard_map/views/pallas_call | solution.py:335
  4.2 3.3 %collective-permute-start.9 = (f32[2,128,128]{2,1,0:T(8,128)S(1)}, f32[2,128,128]{2,1,0:T(8,128)S(1)}, u32[]{:S(2)}, u32[]{:S(2)}) collective-permute-start(f32[2,128,128]{2,1,0:T(8,128)S(1)} %views.1), channel_id=1, source_target_pairs={{0,32},{32,0},{64,96},{96,64},{128,160},{160,128},{192,224},{224,1... | collective-permute-start | bytes 393224 | tf_op jit(solution)/shard_map/ppermute | solution.py:344
  7.5 1.0 %collective-permute-done.9 = f32[2,128,128]{2,1,0:T(8,128)S(1)} collective-permute-done((f32[2,128,128]{2,1,0:T(8,128)S(1)}, f32[2,128,128]{2,1,0:T(8,128)S(1)}, u32[]{:S(2)}, u32[]{:S(2)}) %collective-permute-start.9) | collective-permute-done | bytes 131104 | tf_op jit(solution)/shard_map/ppermute | solution.py:344
  8.5 0.1 collective-permute-start.10
  8.5 1.9 %collective-permute-start.11 = (f32[2,128,128]{2,1,0:T(8,128)S(1)}, f32[2,128,128]{2,1,0:T(8,128)S(1)}, u32[]{:S(2)}, u32[]{:S(2)}) collective-permute-start(f32[2,128,128]{2,1,0:T(8,128)S(1)} %max.3.sq0), channel_id=1, source_target_pairs={{0,128},{32,160},{64,192},{96,224},{128,0},{160,32},{192,64},{224,... | collective-permute-start | bytes 393224 | tf_op jit(solution)/shard_map/ppermute | solution.py:348
  10.5 1.2 %collective-permute-start.12 = (f32[2,128,128]{2,1,0:T(8,128)S(1)}, f32[2,128,128]{2,1,0:T(8,128)S(1)}, u32[]{:S(2)}, u32[]{:S(2)}) collective-permute-start(f32[2,128,128]{2,1,0:T(8,128)S(1)} %max.3.sq0), channel_id=1, source_target_pairs={{0,192},{32,224},{64,0},{96,32},{128,64},{160,96},{192,128},{224,1... | collective-permute-start | bytes 393224 | tf_op jit(solution)/shard_map/ppermute | solution.py:348
  11.6 1.5 %count.1 = s32[32,128]{1,0:T(8,128)} custom-call(s32[128,128]{1,0:T(8,128)} %bitcast.48), custom_call_target="tpu_custom_call" | custom-call | tf_op jit(solution)/shard_map/count/pallas_call | solution.py:325
  13.2 11.2 %all-to-all-start.18 = ((s32[32,1,128]{2,1,0:T(1,128)}), s32[32,1,128]{2,1,0:T(1,128)S(1)}, u32[]{:S(2)}, u32[]{:S(2)}) async-start(s32[32,1,128]{2,1,0:T(1,128)} %bitcast.22), calls=%async_computation.18 | async-start | bytes 32768 | tf_op jit(solution)/shard_map/all_to_all | solution.py:333
  24.4 0.1 pad_add_fusion.where
  24.5 1.6 %index.1 = (s32[8,128]{1,0:T(8,128)S(1)}, s32[128,128]{1,0:T(8,128)S(1)}) custom-call(s32[128,128]{1,0:T(8,128)} %bitcast.49), custom_call_target="tpu_custom_call" | custom-call | tf_op jit(solution)/shard_map/index/pallas_call | solution.py:350
  26.1 6.9 %all-to-all-done.18 = s32[32,1,128]{2,1,0:T(1,128)S(1)} async-done(((s32[32,1,128]{2,1,0:T(1,128)}), s32[32,1,128]{2,1,0:T(1,128)S(1)}, u32[]{:S(2)}, u32[]{:S(2)}) %all-to-all-start.18) | async-done | bytes 16416 | tf_op jit(solution)/shard_map/all_to_all | solution.py:333
  33.0 4.4 %fill.1 = (f32[128,8,128]{2,1,0:T(8,128)S(1)}, s32[1]{0:T(128)}, s32[1]{0:T(128)}, s32[384]{0:T(512)S(1)}) custom-call(s32[2]{0:T(128)S(1)} %pad_add_fusion.where, s32[32,128]{1,0:T(8,128)S(1)} %bitcast.47, s32[8,128]{1,0:T(8,128)S(1)} %get-tuple-element.200.start, s32[128,128]{1,0:T(8,128)S(1)} %get-tuple-element.201.index, f32[3,16384]{1,0:T(4,128)} %means.3, ...), custom_call_target="tpu_custom_call" | custom-call | tf_op jit(solution)/shard_map/fill/pallas_call | solution.py:361
  38.0 0.0 collective-permute-done.10.sq1
  38.0 0.0 collective-permute-done.11.sq2
  38.0 0.0 collective-permute-done.12.sq3
  38.0 0.6 add.3
  38.6 39.1 %conditional.1 = (f32[2,16384]{1,0:T(2,128)}, f32[61,16384]{1,0:T(8,128)}) conditional(s32[]{:T(128)} %bitcast.24, (f32[2,128,128]{2,1,0:T(8,128)S(1)}, f32[2,128,128]{2,1,0:T(8,128)S(1)}, f32[2,128,128]{2,1,0:T(8,128)S(1)}, f32[2,128,128]{2,1,0:T(8,128)S(1)}, f32[128,8,128]{2,1,0:T(8,128)S(1)}, ...), branch_computations={%region_0.0_spmd, %region_1.0_spmd, %region_2.0_spmd, %region_3.0_... | conditional | bytes 13631544 | solution.py:455
  38.6 15.6 %all_to_all.91 = f32[32,4,8,128]{3,2,1,0:T(8,128)S(1)} all-to-all(f32[32,4,8,128]{3,2,1,0:T(8,128)S(1)} %bitcast.33), channel_id=1, replica_groups=mesh['view'=8,'gauss'=32] {'gauss'}, dimensions={0} | all-to-all | bytes 1048576 | tf_op jit(solution)/shard_map/cond/branch_4_fun/all_to_all | solution.py:401
  54.2 0.8 %place.13 = f32[4,56,8,128]{3,2,1,0:T(8,128)S(1)} custom-call(s32[384]{0:T(512)S(1)} %get-tuple-element.159.table, f32[128,8,128]{2,1,0:T(8,128)S(1)} %bitcast.43), custom_call_target="tpu_custom_call" | custom-call | tf_op jit(solution)/shard_map/cond/branch_4_fun/place/pallas_call | solution.py:404
  55.0 11.5 %all_to_all.92.own = f32[4,56,8,128]{3,2,1,0:T(8,128)S(1)} all-to-all(f32[4,56,8,128]{3,2,1,0:T(8,128)S(1)} %place.13), channel_id=1, replica_groups={{0,64,128,192},{32,96,160,224},{1,65,129,193},{33,97,161,225},{2,66,130..., dimensions={0} | all-to-all | bytes 1835008 | tf_op jit(solution)/shard_map/cond/branch_4_fun/all_to_all | solution.py:414
  66.5 6.2 %collective-permute-start.4 = (f32[4,56,8,128]{3,2,1,0:T(8,128)S(1)}, f32[4,56,8,128]{3,2,1,0:T(8,128)S(1)}, u32[]{:S(2)}, u32[]{:S(2)}) collective-permute-start(f32[4,56,8,128]{3,2,1,0:T(8,128)S(1)} %all_to_all.92.own), channel_id=1, source_target_pairs={{0,32},{32,0},{64,96},{96,64},{128,160},{160,128},{192,224},{224,1... | collective-permute-start | bytes 2752520 | tf_op jit(solution)/shard_map/cond/branch_4_fun/ppermute | solution.py:415
  72.7 0.7 peaks.13
  73.4 2.3 %own.13.begun = f32[61,16384]{1,0:T(8,128)} custom-call(s32[2]{0:T(128)S(1)} %get-tuple-element.158.where, f32[4,56,8,128]{3,2,1,0:T(8,128)S(1)} %all_to_all.92.own), custom_call_target="tpu_custom_call" | custom-call | tf_op jit(solution)/shard_map/cond/branch_4_fun/own/pallas_call | solution.py:425
  75.7 0.0 collective-permute-done.4.other
  75.8 1.6 %other.13 = f32[61,16384]{1,0:T(8,128)} custom-call(s32[2]{0:T(128)S(1)} %get-tuple-element.158.where, f32[4,56,8,128]{3,2,1,0:T(8,128)S(1)} %collective-permute-done.4.other, f32[61,16384]{1,0:T(8,128)} %own.13.begun), custom_call_target="tpu_custom_call", output_to_operand_aliasing={{}: (2, {})} | custom-call | tf_op jit(solution)/shard_map/cond/branch_4_fun/other/pallas_call | solution.py:438
  (1 shorter events, 0.0 us)
Async XLA Ops:
  4.2 4.3 %collective-permute-start.9 = (f32[2,128,128]{2,1,0:T(8,128)S(1)}, f32[2,128,128]{2,1,0:T(8,128)S(1)}, u32[]{:S(2)}, u32[]{:S(2)}) collective-permute-start(f32[2,128,128]{2,1,0:T(8,128)S(1)} %views.1), channel_id=1, source_target_pairs={{0,32},{32,0},{64,96},{96,64},{128,160},{160,128},{192,224},{224,1... | collective-permute-start | bytes 393224 | tf_op jit(solution)/shard_map/ppermute | solution.py:344
  8.5 29.6 %collective-permute-start.10 = (f32[2,128,128]{2,1,0:T(8,128)S(1)}, f32[2,128,128]{2,1,0:T(8,128)S(1)}, u32[]{:S(2)}, u32[]{:S(2)}) collective-permute-start(f32[2,128,128]{2,1,0:T(8,128)S(1)} %max.3.sq0), channel_id=1, source_target_pairs={{0,64},{32,96},{64,128},{96,160},{128,192},{160,224},{192,0},{224,... | collective-permute-start | bytes 393224 | tf_op jit(solution)/shard_map/ppermute | solution.py:348
  8.5 29.5 %collective-permute-start.11 = (f32[2,128,128]{2,1,0:T(8,128)S(1)}, f32[2,128,128]{2,1,0:T(8,128)S(1)}, u32[]{:S(2)}, u32[]{:S(2)}) collective-permute-start(f32[2,128,128]{2,1,0:T(8,128)S(1)} %max.3.sq0), channel_id=1, source_target_pairs={{0,128},{32,160},{64,192},{96,224},{128,0},{160,32},{192,64},{224,... | collective-permute-start | bytes 393224 | tf_op jit(solution)/shard_map/ppermute | solution.py:348
  10.5 27.5 %collective-permute-start.12 = (f32[2,128,128]{2,1,0:T(8,128)S(1)}, f32[2,128,128]{2,1,0:T(8,128)S(1)}, u32[]{:S(2)}, u32[]{:S(2)}) collective-permute-start(f32[2,128,128]{2,1,0:T(8,128)S(1)} %max.3.sq0), channel_id=1, source_target_pairs={{0,192},{32,224},{64,0},{96,32},{128,64},{160,96},{192,128},{224,1... | collective-permute-start | bytes 393224 | tf_op jit(solution)/shard_map/ppermute | solution.py:348
  13.2 19.8 %all-to-all-start.18 = ((s32[32,1,128]{2,1,0:T(1,128)}), s32[32,1,128]{2,1,0:T(1,128)S(1)}, u32[]{:S(2)}, u32[]{:S(2)}) async-start(s32[32,1,128]{2,1,0:T(1,128)} %bitcast.22), calls=%async_computation.18 | async-start | bytes 32768 | tf_op jit(solution)/shard_map/all_to_all | solution.py:333
  66.5 9.3 %collective-permute-start.4 = (f32[4,56,8,128]{3,2,1,0:T(8,128)S(1)}, f32[4,56,8,128]{3,2,1,0:T(8,128)S(1)}, u32[]{:S(2)}, u32[]{:S(2)}) collective-permute-start(f32[4,56,8,128]{3,2,1,0:T(8,128)S(1)} %all_to_all.92.own), channel_id=1, source_target_pairs={{0,32},{32,0},{64,96},{96,64},{128,160},{160,128},{192,224},{224,1... | collective-permute-start | bytes 2752520 | tf_op jit(solution)/shard_map/cond/branch_4_fun/ppermute | solution.py:415

commit v8 on v7

--- a/solution.py
+++ b/solution.py
@@ -176,9 +176,9 @@
     def place_of(block):
         return ((offset + block) & (SHARDS - 1)) * PER + (block >> 5)
 
-    def eight(i, carry):
-        for j in range(8):
-            b = i * 8 + j
+    def some(i, carry):
+        for j in range(32):
+            b = i * 32 + j
             block = start[0, b] >> 7
             here = place_of(block)
             after = place_of(jnp.minimum(block + 1, BLOCKS - 1))
@@ -192,7 +192,7 @@
             pltpu.store(out_ref.at[after], packed, mask=(code & 512) != 0)
         return carry
 
-    lax.fori_loop(0, BLOCKS // 8, eight, 0)
+    lax.fori_loop(0, BLOCKS // 32, some, 0)
 
 
 def top_of(squares, k, at):
@@ -219,17 +219,6 @@
             pltpu.store(out_ref.at[both >> 8, 3:5, :], two, mask=(code & 512) != 0)
 
 
-def peak_kernel(sq0, sq1, sq2, sq3, peak_ref, pairs):
-    for g in range(BLOCKS // 8):
-        at = slice(8 * g, 8 * g + 8)
-        norm = jnp.sqrt(top_of((sq0, sq1, sq2, sq3), 0, at))
-        radius = 3.0 * jnp.sqrt(top_of((sq0, sq1, sq2, sq3), 1, at))
-        pairs[pl.ds(16 * g, 8, stride=2), :] = norm
-        pairs[pl.ds(16 * g + 1, 8, stride=2), :] = radius
-    for b in range(BLOCKS):
-        peak_ref[:, b * LANES : (b + 1) * LANES] = pairs[2 * b : 2 * b + 2, :]
-
-
 def place_kernel(table, arrived, out_ref, slots):
     cap = out_ref.shape[1]
     zero = jnp.zeros((8, LANES), jnp.float32)
@@ -250,7 +239,9 @@
     )
 
 
-def own_kernel(where, own, out_ref, buf, zeros, sems):
+def own_kernel(
+    where, own, sq0, sq1, sq2, sq3, out_ref, peak_ref, buf, zeros, pairs, peaks, sems
+):
     cap = own.shape[1]
     core = where[0] & 1
 
@@ -275,12 +266,29 @@
                 for i in range(cap):
                     buf[r, :, i * LANES : (i + 1) * LANES] = own[r // 2, i]
                 row_copy(buf, out_ref, sems, r, slice(0, cap * LANES)).start()
+
+    for g in range(BLOCKS // 8):
+        at = slice(8 * g, 8 * g + 8)
+        norm = jnp.sqrt(top_of((sq0, sq1, sq2, sq3), 0, at))
+        radius = 3.0 * jnp.sqrt(top_of((sq0, sq1, sq2, sq3), 1, at))
+        pairs[pl.ds(16 * g, 8, stride=2), :] = norm
+        pairs[pl.ds(16 * g + 1, 8, stride=2), :] = radius
+    for b in range(BLOCKS):
+        peaks[:, b * LANES : (b + 1) * LANES] = pairs[2 * b : 2 * b + 2, :]
+    peak_copy = pltpu.make_async_copy(peaks, peak_ref, sems.at[16])
+    peak_copy.start()
+
+    for half in range(2):
+
+        @pl.when(core == half)
+        def _():
             for r in range(half, 8, 2):
                 row_copy(buf, out_ref, sems, r, slice(0, cap * LANES)).wait()
 
     if cap < BLOCKS:
         for r in range(8):
             clear(r).wait()
+    peak_copy.wait()
 
 
 def other_kernel(where, other, begun, out_ref, buf, sems):
@@ -413,28 +421,24 @@
             cores = [[0, 2, 4, 6], [1, 3, 5, 7]]
             own = lax.all_to_all(piece, "view", 0, 0, axis_index_groups=cores, tiled=True)
             other = lax.ppermute(own, "view", [(v, v ^ 1) for v in range(8)])
-            peak = pl.pallas_call(
-                peak_kernel,
-                in_specs=[vmem()] * 4,
-                out_specs=vmem(),
-                out_shape=pltpu.MemorySpace.HBM((2, G_DEV), f32),
-                scratch_shapes=[pltpu.VMEM((2 * BLOCKS + 32, LANES), f32)],
-                compiler_params=LIMIT,
-                name="peaks",
-            )(*squares)
-            begun = pl.pallas_call(
+            begun, peak = pl.pallas_call(
                 own_kernel,
-                in_specs=[smem(), vmem()],
-                out_specs=pl.BlockSpec(memory_space=pl.ANY),
-                out_shape=jax.ShapeDtypeStruct((ROWS, G_DEV), f32),
+                in_specs=[smem()] + [vmem()] * 5,
+                out_specs=[pl.BlockSpec(memory_space=pl.ANY)] * 2,
+                out_shape=[
+                    jax.ShapeDtypeStruct((ROWS, G_DEV), f32),
+                    pltpu.MemorySpace.HBM((2, G_DEV), f32),
+                ],
                 scratch_shapes=[
                     pltpu.VMEM((8, 8, cap * LANES), f32),
                     pltpu.VMEM((8, max(BLOCKS - cap, 1) * LANES), f32),
-                    pltpu.SemaphoreType.DMA((16,)),
+                    pltpu.VMEM((2 * BLOCKS + 32, LANES), f32),
+                    pltpu.VMEM((2, G_DEV), f32),
+                    pltpu.SemaphoreType.DMA((17,)),
                 ],
                 compiler_params=LIMIT,
                 name="own",
-            )(where, own)
+            )(where, own, *squares)
             clones = pl.pallas_call(
                 other_kernel,
                 in_specs=[smem(), vmem(), pl.BlockSpec(memory_space=pl.ANY)],

time: 79.1 us -> 78.1 us (0.987)
  blocking collectives: 27 us -> 28.4 us
  Pallas kernels: 17 us -> 15.9 us
  starting transfers between devices: 23.9 us -> 22.9 us
    all_to_all x1, blocking collectives: 11.5 us -> 12.8 us  [go(): lax.all_to_all(piece, 'view', 0, 0, axis_index_groups=cores, tiled=True)]
    ppermute x3, starting transfers between devices: 3.18 us -> 1.97 us  [body(): squares.append(lax.ppermute(squares[0], 'view', pairs))]
    pallas_call x2 -> x1, Pallas kernels: 3.06 us -> 2.38 us  [go(): pl.pallas_call(own_kernel, in_specs=[smem()] + [vmem()] * 5, out_specs=[p...]
  transfers between devices with their start and end apart: 6 -> 6, of which waited for: 2 -> 2; matrix products, arithmetic and copies ran while one was open for 0% -> 0% of each run, Pallas kernels for 14% -> 12%
where the time goes in v8:
time: 78.1 us; the launch traced here: 77.2 us
  blocking collectives  28.4 us (36%)
  starting transfers between devices  22.9 us (29%)
  Pallas kernels  15.9 us (20%)
  waiting for transfers between devices  7.93 us (10%)
  between operations  1.53 us (2%)
    all_to_all x1, blocking collectives, go(): lax.all_to_all(outgoing.reshape(SHARDS, PER, 8, LANES), 'gauss', 0, 0, ti...  15.6 us
    all_to_all x1, blocking collectives, go(): lax.all_to_all(piece, 'view', 0, 0, axis_index_groups=cores, tiled=True)  12.8 us
    all_to_all x1, starting transfers between devices, body(): counts = lax.all_to_all(count, 'gauss', 0, 0, tiled=True)  11.2 us
    all_to_all x1, waiting for transfers between devices, body(): counts = lax.all_to_all(count, 'gauss', 0, 0, tiled=True)  6.93 us
    ppermute x1, starting transfers between devices, go(): other = lax.ppermute(own, 'view', [(v, v ^ 1) for v in range(8)])  6.45 us
    pallas_call x1, Pallas kernels, body(): pl.pallas_call(fill_kernel, grid_spec=pltpu.PrefetchScalarGridSpec(num_sc...  3.99 us
    pallas_call x1, Pallas kernels, body(): pl.pallas_call(view_kernel, in_specs=[smem()] * 3 + [vmem()] * 5, out_spe...  3.53 us
    ppermute x1, starting transfers between devices, body(): other = lax.ppermute(squares, 'view', [(v, v ^ 1) for v in range(8)])  3.29 us
  transfers between devices with their start and end apart: 6, of which 2 were waited for; matrix products, arithmetic and copies ran while one was open for 0% of the time, Pallas kernels for 12%

profile of v8, /device:TPU:1, one launch (start us, length us, event | category | flops | bytes accessed | tf_op | source)
XLA Modules:
  0.0 77.2 jit_solution(2535974837584573911)
XLA Ops:
  0.6 3.5 %views.1 = f32[2,128,128]{2,1,0:T(8,128)S(1)} custom-call(f32[3,4,3]{2,1,0:T(4,128)} %bitcast.50, f32[4,3]{1,0:T(4,128)} %trans.1, f32[1,4]{1,0:T(1,128)} %bitcast.51, f32[3,16384]{1,0:T(4,128)} %means.3, f32[3,16384]{1,0:T(4,128)} %scales.3, f32[4,16384]{1,0:T(4,128)} %quats.3, f32[4,2,16384]{2,1,0:T(2,128)} %grad.1, s32[4,16384]{1,0:T(4,128)} %seen.1), custom_call_target="tpu_custom_call" | custom-call | tf_op jit(solution)/shard_map/views/pallas_call | solution.py:343
  4.2 3.3 %collective-permute-start.9 = (f32[2,128,128]{2,1,0:T(8,128)S(1)}, f32[2,128,128]{2,1,0:T(8,128)S(1)}, u32[]{:S(2)}, u32[]{:S(2)}) collective-permute-start(f32[2,128,128]{2,1,0:T(8,128)S(1)} %views.1), channel_id=1, source_target_pairs={{0,32},{32,0},{64,96},{96,64},{128,160},{160,128},{192,224},{224,1... | collective-permute-start | bytes 393224 | tf_op jit(solution)/shard_map/ppermute | solution.py:352
  7.5 1.0 %collective-permute-done.9 = f32[2,128,128]{2,1,0:T(8,128)S(1)} collective-permute-done((f32[2,128,128]{2,1,0:T(8,128)S(1)}, f32[2,128,128]{2,1,0:T(8,128)S(1)}, u32[]{:S(2)}, u32[]{:S(2)}) %collective-permute-start.9) | collective-permute-done | bytes 131104 | tf_op jit(solution)/shard_map/ppermute | solution.py:352
  8.5 0.8 %collective-permute-start.12 = (f32[2,128,128]{2,1,0:T(8,128)S(1)}, f32[2,128,128]{2,1,0:T(8,128)S(1)}, u32[]{:S(2)}, u32[]{:S(2)}) collective-permute-start(f32[2,128,128]{2,1,0:T(8,128)S(1)} %max.3.sq0), channel_id=1, source_target_pairs={{0,192},{32,224},{64,0},{96,32},{128,64},{160,96},{192,128},{224,1... | collective-permute-start | bytes 393224 | tf_op jit(solution)/shard_map/ppermute | solution.py:356
  9.3 0.5 collective-permute-start.11
  9.8 0.6 collective-permute-start.10
  10.4 1.5 %count.1 = s32[32,128]{1,0:T(8,128)} custom-call(s32[128,128]{1,0:T(8,128)} %bitcast.48), custom_call_target="tpu_custom_call" | custom-call | tf_op jit(solution)/shard_map/count/pallas_call | solution.py:333
  12.0 11.2 %all-to-all-start.18 = ((s32[32,1,128]{2,1,0:T(1,128)}), s32[32,1,128]{2,1,0:T(1,128)S(1)}, u32[]{:S(2)}, u32[]{:S(2)}) async-start(s32[32,1,128]{2,1,0:T(1,128)} %bitcast.22), calls=%async_computation.18 | async-start | bytes 32768 | tf_op jit(solution)/shard_map/all_to_all | solution.py:341
  23.2 0.1 pad_add_fusion.where
  23.3 1.6 %index.1 = (s32[8,128]{1,0:T(8,128)S(1)}, s32[128,128]{1,0:T(8,128)S(1)}) custom-call(s32[128,128]{1,0:T(8,128)} %bitcast.49), custom_call_target="tpu_custom_call" | custom-call | tf_op jit(solution)/shard_map/index/pallas_call | solution.py:358
  24.8 6.9 %all-to-all-done.18 = s32[32,1,128]{2,1,0:T(1,128)S(1)} async-done(((s32[32,1,128]{2,1,0:T(1,128)}), s32[32,1,128]{2,1,0:T(1,128)S(1)}, u32[]{:S(2)}, u32[]{:S(2)}) %all-to-all-start.18) | async-done | bytes 16416 | tf_op jit(solution)/shard_map/all_to_all | solution.py:341
  31.8 4.0 %fill.1 = (f32[128,8,128]{2,1,0:T(8,128)S(1)}, s32[1]{0:T(128)}, s32[1]{0:T(128)}, s32[384]{0:T(512)S(1)}) custom-call(s32[2]{0:T(128)S(1)} %pad_add_fusion.where, s32[32,128]{1,0:T(8,128)S(1)} %bitcast.47, s32[8,128]{1,0:T(8,128)S(1)} %get-tuple-element.218.start, s32[128,128]{1,0:T(8,128)S(1)} %get-tuple-element.219.index, f32[3,16384]{1,0:T(4,128)} %means.3, ...), custom_call_target="tpu_custom_call" | custom-call | tf_op jit(solution)/shard_map/fill/pallas_call | solution.py:369
  36.4 0.0 collective-permute-done.12.sq3
  36.4 0.0 collective-permute-done.11.sq2
  36.4 0.0 collective-permute-done.10.sq1
  36.5 0.6 add.3
  37.0 40.0 %conditional.1 = (f32[2,16384]{1,0:T(2,128)}, f32[61,16384]{1,0:T(8,128)}) conditional(s32[]{:T(128)} %bitcast.24, (f32[128,8,128]{2,1,0:T(8,128)S(1)}, s32[384]{0:T(512)S(1)}, s32[2]{0:T(128)S(1)}, f32[2,128,128]{2,1,0:T(8,128)S(1)}, f32[2,128,128]{2,1,0:T(8,128)S(1)}, /*index=5*/f32[2,128,128]{2,1,0:T(8,128)S(1)}, ...), branch_computations={%region_0.0_spmd, %region_1.0_spmd, %region_2.0_spmd, %region_3.0_... | conditional | bytes 13631544 | solution.py:459
  37.1 15.6 %all_to_all.91 = f32[32,4,8,128]{3,2,1,0:T(8,128)S(1)} all-to-all(f32[32,4,8,128]{3,2,1,0:T(8,128)S(1)} %bitcast.33), channel_id=1, replica_groups=mesh['view'=8,'gauss'=32] {'gauss'}, dimensions={0} | all-to-all | bytes 1048576 | tf_op jit(solution)/shard_map/cond/branch_4_fun/all_to_all | solution.py:409
  52.7 0.8 %place.13 = f32[4,56,8,128]{3,2,1,0:T(8,128)S(1)} custom-call(s32[384]{0:T(512)S(1)} %get-tuple-element.163.table, f32[128,8,128]{2,1,0:T(8,128)S(1)} %bitcast.43), custom_call_target="tpu_custom_call" | custom-call | tf_op jit(solution)/shard_map/cond/branch_4_fun/place/pallas_call | solution.py:412
  53.4 12.8 %all_to_all.92.own = f32[4,56,8,128]{3,2,1,0:T(8,128)S(1)} all-to-all(f32[4,56,8,128]{3,2,1,0:T(8,128)S(1)} %place.13), channel_id=1, replica_groups={{0,64,128,192},{32,96,160,224},{1,65,129,193},{33,97,161,225},{2,66,130..., dimensions={0} | all-to-all | bytes 1835008 | tf_op jit(solution)/shard_map/cond/branch_4_fun/all_to_all | solution.py:422
  66.2 6.4 %collective-permute-start.4 = (f32[4,56,8,128]{3,2,1,0:T(8,128)S(1)}, f32[4,56,8,128]{3,2,1,0:T(8,128)S(1)}, u32[]{:S(2)}, u32[]{:S(2)}) collective-permute-start(f32[4,56,8,128]{3,2,1,0:T(8,128)S(1)} %all_to_all.92.own), channel_id=1, source_target_pairs={{0,32},{32,0},{64,96},{96,64},{128,160},{160,128},{192,224},{224,1... | collective-permute-start | bytes 2752520 | tf_op jit(solution)/shard_map/cond/branch_4_fun/ppermute | solution.py:423
  72.7 2.4 %own.13 = (f32[61,16384]{1,0:T(8,128)}, f32[2,16384]{1,0:T(2,128)}) custom-call(s32[2]{0:T(128)S(1)} %get-tuple-element.162.where, f32[4,56,8,128]{3,2,1,0:T(8,128)S(1)} %all_to_all.92.own, f32[2,128,128]{2,1,0:T(8,128)S(1)} %get-tuple-element.165.sq0, f32[2,128,128]{2,1,0:T(8,128)S(1)} %get-tuple-element.166.sq1, ...), custom_call_target="tpu_custom_call" | custom-call | tf_op jit(solution)/shard_map/cond/branch_4_fun/own/pallas_call | solution.py:424
  75.1 0.0 collective-permute-done.4.other
  75.1 1.6 %other.13 = f32[61,16384]{1,0:T(8,128)} custom-call(s32[2]{0:T(128)S(1)} %get-tuple-element.162.where, f32[4,56,8,128]{3,2,1,0:T(8,128)S(1)} %collective-permute-done.4.other, f32[61,16384]{1,0:T(8,128)} %get-tuple-element.170.begun), custom_call_target="tpu_custom_call", output_to_operand_aliasing={{}: (2, {})} | custom-call | tf_op jit(solution)/shard_map/cond/branch_4_fun/other/pallas_call | solution.py:442
  (1 shorter events, 0.0 us)
Async XLA Ops:
  4.2 4.3 %collective-permute-start.9 = (f32[2,128,128]{2,1,0:T(8,128)S(1)}, f32[2,128,128]{2,1,0:T(8,128)S(1)}, u32[]{:S(2)}, u32[]{:S(2)}) collective-permute-start(f32[2,128,128]{2,1,0:T(8,128)S(1)} %views.1), channel_id=1, source_target_pairs={{0,32},{32,0},{64,96},{96,64},{128,160},{160,128},{192,224},{224,1... | collective-permute-start | bytes 393224 | tf_op jit(solution)/shard_map/ppermute | solution.py:352
  8.5 28.0 %collective-permute-start.12 = (f32[2,128,128]{2,1,0:T(8,128)S(1)}, f32[2,128,128]{2,1,0:T(8,128)S(1)}, u32[]{:S(2)}, u32[]{:S(2)}) collective-permute-start(f32[2,128,128]{2,1,0:T(8,128)S(1)} %max.3.sq0), channel_id=1, source_target_pairs={{0,192},{32,224},{64,0},{96,32},{128,64},{160,96},{192,128},{224,1... | collective-permute-start | bytes 393224 | tf_op jit(solution)/shard_map/ppermute | solution.py:356
  9.3 27.1 %collective-permute-start.11 = (f32[2,128,128]{2,1,0:T(8,128)S(1)}, f32[2,128,128]{2,1,0:T(8,128)S(1)}, u32[]{:S(2)}, u32[]{:S(2)}) collective-permute-start(f32[2,128,128]{2,1,0:T(8,128)S(1)} %max.3.sq0), channel_id=1, source_target_pairs={{0,128},{32,160},{64,192},{96,224},{128,0},{160,32},{192,64},{224,... | collective-permute-start | bytes 393224 | tf_op jit(solution)/shard_map/ppermute | solution.py:356
  9.8 26.6 %collective-permute-start.10 = (f32[2,128,128]{2,1,0:T(8,128)S(1)}, f32[2,128,128]{2,1,0:T(8,128)S(1)}, u32[]{:S(2)}, u32[]{:S(2)}) collective-permute-start(f32[2,128,128]{2,1,0:T(8,128)S(1)} %max.3.sq0), channel_id=1, source_target_pairs={{0,64},{32,96},{64,128},{96,160},{128,192},{160,224},{192,0},{224,... | collective-permute-start | bytes 393224 | tf_op jit(solution)/shard_map/ppermute | solution.py:356
  12.0 19.8 %all-to-all-start.18 = ((s32[32,1,128]{2,1,0:T(1,128)}), s32[32,1,128]{2,1,0:T(1,128)S(1)}, u32[]{:S(2)}, u32[]{:S(2)}) async-start(s32[32,1,128]{2,1,0:T(1,128)} %bitcast.22), calls=%async_computation.18 | async-start | bytes 32768 | tf_op jit(solution)/shard_map/all_to_all | solution.py:341
  66.2 8.8 %collective-permute-start.4 = (f32[4,56,8,128]{3,2,1,0:T(8,128)S(1)}, f32[4,56,8,128]{3,2,1,0:T(8,128)S(1)}, u32[]{:S(2)}, u32[]{:S(2)}) collective-permute-start(f32[4,56,8,128]{3,2,1,0:T(8,128)S(1)} %all_to_all.92.own), channel_id=1, source_target_pairs={{0,32},{32,0},{64,96},{96,64},{128,160},{160,128},{192,224},{224,1... | collective-permute-start | bytes 2752520 | tf_op jit(solution)/shard_map/cond/branch_4_fun/ppermute | solution.py:423

commit v9 on v8

--- a/solution.py
+++ b/solution.py
@@ -124,7 +124,7 @@
 
 def fill_kernel(
     where, counts, start, index, means, scales, quats, low, high,
-    out_ref, sums_ref, pick_ref, table, rows
+    out_ref, pick_ref, table, rows
 ):
     view = where[0]
 
@@ -166,7 +166,7 @@
         count = counts[s, 0]
         total = total + count
         used = used + ((count + LANES - 1) >> 7)
-    sums_ref[0] = total
+    table[2 * BLOCKS + 1] = total
     pick = jnp.int32(0)
     for cap in CAPS[:-1]:
         pick = pick + jnp.where(used > cap * SHARDS, 1, 0)
@@ -240,10 +240,12 @@
 
 
 def own_kernel(
-    where, own, sq0, sq1, sq2, sq3, out_ref, peak_ref, buf, zeros, pairs, peaks, sems
+    table, own, sq0, sq1, sq2, sq3,
+    out_ref, peak_ref, total_ref, buf, zeros, pairs, peaks, sems
 ):
     cap = own.shape[1]
-    core = where[0] & 1
+    core = table[2 * BLOCKS] & 1
+    total_ref[0] = table[2 * BLOCKS + 1]
 
     def clear(r):
         rows = min(8, ROWS - 8 * r)
@@ -291,9 +293,9 @@
     peak_copy.wait()
 
 
-def other_kernel(where, other, begun, out_ref, buf, sems):
+def other_kernel(table, other, begun, out_ref, buf, sems):
     cap = other.shape[1]
-    core = where[0] & 1
+    core = table[2 * BLOCKS] & 1
     for half in range(2):
 
         @pl.when(core == half)
@@ -366,7 +368,7 @@
         compiler_params=LIMIT,
         name="index",
     )(mask)
-    filled, total, branch, table = pl.pallas_call(
+    filled, branch, table = pl.pallas_call(
         fill_kernel,
         grid_spec=pltpu.PrefetchScalarGridSpec(
             num_scalar_prefetch=1,
@@ -381,14 +383,13 @@
                 pl.BlockSpec((8, G_DEV), lambda i, w: (jnp.maximum(w[0] - 2, 0), 0)),
                 pl.BlockSpec((8, G_DEV), lambda i, w: (jnp.maximum(w[0] - 1, 0), 0)),
             ],
-            out_specs=[whole(BLOCKS, 8, LANES), smem(), smem(), smem()],
+            out_specs=[whole(BLOCKS, 8, LANES), smem(), smem()],
             scratch_shapes=[pltpu.VMEM((8, G_DEV), f32)],
         ),
         out_shape=[
             VMEM((BLOCKS, 8, LANES), f32),
-            jax.ShapeDtypeStruct((1,), i32),
-            jax.ShapeDtypeStruct((1,), i32),
-            VMEM((3 * BLOCKS,), i32),
+            SMEM((1,), i32),
+            SMEM((3 * BLOCKS,), i32),
         ],
         compiler_params=LIMIT,
         name="fill",
@@ -405,7 +406,7 @@
     )(table, index, *squares, filled)
 
     def gather(cap):
-        def go(where, table, outgoing, *squares):
+        def go(table, outgoing, *squares):
             arrived = lax.all_to_all(
                 outgoing.reshape(SHARDS, PER, 8, LANES), "gauss", 0, 0, tiled=True
             ).reshape(BLOCKS, 8, LANES)
@@ -421,13 +422,14 @@
             cores = [[0, 2, 4, 6], [1, 3, 5, 7]]
             own = lax.all_to_all(piece, "view", 0, 0, axis_index_groups=cores, tiled=True)
             other = lax.ppermute(own, "view", [(v, v ^ 1) for v in range(8)])
-            begun, peak = pl.pallas_call(
+            begun, peak, total = pl.pallas_call(
                 own_kernel,
                 in_specs=[smem()] + [vmem()] * 5,
-                out_specs=[pl.BlockSpec(memory_space=pl.ANY)] * 2,
+                out_specs=[pl.BlockSpec(memory_space=pl.ANY)] * 2 + [smem()],
                 out_shape=[
                     jax.ShapeDtypeStruct((ROWS, G_DEV), f32),
                     pltpu.MemorySpace.HBM((2, G_DEV), f32),
+                    pltpu.MemorySpace.HBM((1,), i32),
                 ],
                 scratch_shapes=[
                     pltpu.VMEM((8, 8, cap * LANES), f32),
@@ -438,7 +440,7 @@
                 ],
                 compiler_params=LIMIT,
                 name="own",
-            )(where, own, *squares)
+            )(table, own, *squares)
             clones = pl.pallas_call(
                 other_kernel,
                 in_specs=[smem(), vmem(), pl.BlockSpec(memory_space=pl.ANY)],
@@ -451,13 +453,13 @@
                 ],
                 compiler_params=LIMIT,
                 name="other",
-            )(where, other, begun)
-            return peak, clones
+            )(table, other, begun)
+            return peak, clones, total
 
         return go
 
-    peak, clones = lax.switch(
-        branch[0], [gather(cap) for cap in CAPS], where, table, outgoing, *squares
+    peak, clones, total = lax.switch(
+        branch[0], [gather(cap) for cap in CAPS], table, outgoing, *squares
     )
     return (peak, clones, total[0])
 

time: 78.1 us -> 75.2 us (0.963)
  Pallas kernels: 15.9 us -> 13.7 us
where the time goes in v9:
time: 75.2 us; the launch traced here: 74.4 us
  blocking collectives  28.4 us (38%)
  starting transfers between devices  22.9 us (30%)
  Pallas kernels  13.7 us (18%)
  waiting for transfers between devices  7.93 us (11%)
  between operations  0.88 us (1%)
    all_to_all x1, blocking collectives, go(): lax.all_to_all(outgoing.reshape(SHARDS, PER, 8, LANES), 'gauss', 0, 0, ti...  15.6 us
    all_to_all x1, blocking collectives, go(): lax.all_to_all(piece, 'view', 0, 0, axis_index_groups=cores, tiled=True)  12.8 us
    all_to_all x1, starting transfers between devices, body(): counts = lax.all_to_all(count, 'gauss', 0, 0, tiled=True)  11.2 us
    all_to_all x1, waiting for transfers between devices, body(): counts = lax.all_to_all(count, 'gauss', 0, 0, tiled=True)  6.93 us
    ppermute x1, starting transfers between devices, go(): other = lax.ppermute(own, 'view', [(v, v ^ 1) for v in range(8)])  6.45 us
    pallas_call x1, Pallas kernels, body(): pl.pallas_call(view_kernel, in_specs=[smem()] * 3 + [vmem()] * 5, out_spe...  3.53 us
    pallas_call x1, Pallas kernels, body(): pl.pallas_call(fill_kernel, grid_spec=pltpu.PrefetchScalarGridSpec(num_sc...  3.4 us
    ppermute x1, starting transfers between devices, body(): other = lax.ppermute(squares, 'view', [(v, v ^ 1) for v in range(8)])  3.29 us
  transfers between devices with their start and end apart: 6, of which 2 were waited for; matrix products, arithmetic and copies ran while one was open for 0% of the time, Pallas kernels for 12%

profile of v9, /device:TPU:1, one launch (start us, length us, event | category | flops | bytes accessed | tf_op | source)
XLA Modules:
  0.0 74.4 jit_solution(3544829203049230762)
XLA Ops:
  0.6 3.5 %views.1 = f32[2,128,128]{2,1,0:T(8,128)S(1)} custom-call(f32[3,4,3]{2,1,0:T(4,128)} %bitcast.50, f32[4,3]{1,0:T(4,128)} %trans.1, f32[1,4]{1,0:T(1,128)} %bitcast.51, f32[3,16384]{1,0:T(4,128)} %means.3, f32[3,16384]{1,0:T(4,128)} %scales.3, f32[4,16384]{1,0:T(4,128)} %quats.3, f32[4,2,16384]{2,1,0:T(2,128)} %grad.1, s32[4,16384]{1,0:T(4,128)} %seen.1), custom_call_target="tpu_custom_call" | custom-call | tf_op jit(solution)/shard_map/views/pallas_call | solution.py:345
  4.2 3.3 %collective-permute-start.9 = (f32[2,128,128]{2,1,0:T(8,128)S(1)}, f32[2,128,128]{2,1,0:T(8,128)S(1)}, u32[]{:S(2)}, u32[]{:S(2)}) collective-permute-start(f32[2,128,128]{2,1,0:T(8,128)S(1)} %views.1), channel_id=1, source_target_pairs={{0,32},{32,0},{64,96},{96,64},{128,160},{160,128},{192,224},{224,1... | collective-permute-start | bytes 393224 | tf_op jit(solution)/shard_map/ppermute | solution.py:354
  7.5 1.0 %collective-permute-done.9 = f32[2,128,128]{2,1,0:T(8,128)S(1)} collective-permute-done((f32[2,128,128]{2,1,0:T(8,128)S(1)}, f32[2,128,128]{2,1,0:T(8,128)S(1)}, u32[]{:S(2)}, u32[]{:S(2)}) %collective-permute-start.9) | collective-permute-done | bytes 131104 | tf_op jit(solution)/shard_map/ppermute | solution.py:354
  8.5 0.8 %collective-permute-start.12 = (f32[2,128,128]{2,1,0:T(8,128)S(1)}, f32[2,128,128]{2,1,0:T(8,128)S(1)}, u32[]{:S(2)}, u32[]{:S(2)}) collective-permute-start(f32[2,128,128]{2,1,0:T(8,128)S(1)} %max.3.sq0), channel_id=1, source_target_pairs={{0,192},{32,224},{64,0},{96,32},{128,64},{160,96},{192,128},{224,1... | collective-permute-start | bytes 393224 | tf_op jit(solution)/shard_map/ppermute | solution.py:358
  9.3 0.5 collective-permute-start.11
  9.8 0.6 collective-permute-start.10
  10.4 1.5 %count.1 = s32[32,128]{1,0:T(8,128)} custom-call(s32[128,128]{1,0:T(8,128)} %bitcast.48), custom_call_target="tpu_custom_call" | custom-call | tf_op jit(solution)/shard_map/count/pallas_call | solution.py:335
  12.0 11.2 %all-to-all-start.18 = ((s32[32,1,128]{2,1,0:T(1,128)}), s32[32,1,128]{2,1,0:T(1,128)S(1)}, u32[]{:S(2)}, u32[]{:S(2)}) async-start(s32[32,1,128]{2,1,0:T(1,128)} %bitcast.22), calls=%async_computation.18 | async-start | bytes 32768 | tf_op jit(solution)/shard_map/all_to_all | solution.py:343
  23.2 0.1 pad_add_fusion.where
  23.3 1.6 %index.1 = (s32[8,128]{1,0:T(8,128)S(1)}, s32[128,128]{1,0:T(8,128)S(1)}) custom-call(s32[128,128]{1,0:T(8,128)} %bitcast.49), custom_call_target="tpu_custom_call" | custom-call | tf_op jit(solution)/shard_map/index/pallas_call | solution.py:360
  24.8 6.9 %all-to-all-done.18 = s32[32,1,128]{2,1,0:T(1,128)S(1)} async-done(((s32[32,1,128]{2,1,0:T(1,128)}), s32[32,1,128]{2,1,0:T(1,128)S(1)}, u32[]{:S(2)}, u32[]{:S(2)}) %all-to-all-start.18) | async-done | bytes 16416 | tf_op jit(solution)/shard_map/all_to_all | solution.py:343
  31.8 3.4 %fill.1 = (f32[128,8,128]{2,1,0:T(8,128)S(1)}, s32[1]{0:T(128)S(4)}, s32[384]{0:T(512)S(4)}) custom-call(s32[2]{0:T(128)S(1)} %pad_add_fusion.where, s32[32,128]{1,0:T(8,128)S(1)} %bitcast.47, s32[8,128]{1,0:T(8,128)S(1)} %get-tuple-element.200.start, s32[128,128]{1,0:T(8,128)S(1)} %get-tuple-element.201.index, f32[3,16384]{1,0:T(4,128)} %means.3, ...), custom_call_target="tpu_custom_call" | custom-call | tf_op jit(solution)/shard_map/fill/pallas_call | solution.py:371
  35.2 0.0 collective-permute-done.12.sq3
  35.2 0.0 collective-permute-done.11.sq2
  35.2 0.0 collective-permute-done.10.sq1
  35.2 38.9 %conditional.1 = (f32[2,16384]{1,0:T(2,128)}, f32[61,16384]{1,0:T(8,128)}, s32[1]{0:T(128)}) conditional(s32[]{:T(128)} %bitcast.24, (f32[128,8,128]{2,1,0:T(8,128)S(1)}, s32[384]{0:T(512)S(4)}, f32[2,128,128]{2,1,0:T(8,128)S(1)}, f32[2,128,128]{2,1,0:T(8,128)S(1)}, f32[2,128,128]{2,1,0:T(8,128)S(1)}, ...), branch_computations={%region_0.0_spmd, %region_1.0_spmd, %region_2.0_spmd, %region_3.0_... | conditional | bytes 13631552 | solution.py:461
  35.3 15.6 %all_to_all.91 = f32[32,4,8,128]{3,2,1,0:T(8,128)S(1)} all-to-all(f32[32,4,8,128]{3,2,1,0:T(8,128)S(1)} %bitcast.33), channel_id=1, replica_groups=mesh['view'=8,'gauss'=32] {'gauss'}, dimensions={0} | all-to-all | bytes 1048576 | tf_op jit(solution)/shard_map/cond/branch_4_fun/all_to_all | solution.py:410
  50.9 0.3 place.13
  51.1 12.8 %all_to_all.92.own = f32[4,56,8,128]{3,2,1,0:T(8,128)S(1)} all-to-all(f32[4,56,8,128]{3,2,1,0:T(8,128)S(1)} %place.13), channel_id=1, replica_groups={{0,64,128,192},{32,96,160,224},{1,65,129,193},{33,97,161,225},{2,66,130..., dimensions={0} | all-to-all | bytes 1835008 | tf_op jit(solution)/shard_map/cond/branch_4_fun/all_to_all | solution.py:423
  63.9 6.4 %collective-permute-start.4 = (f32[4,56,8,128]{3,2,1,0:T(8,128)S(1)}, f32[4,56,8,128]{3,2,1,0:T(8,128)S(1)}, u32[]{:S(2)}, u32[]{:S(2)}) collective-permute-start(f32[4,56,8,128]{3,2,1,0:T(8,128)S(1)} %all_to_all.92.own), channel_id=1, source_target_pairs={{0,32},{32,0},{64,96},{96,64},{128,160},{160,128},{192,224},{224,1... | collective-permute-start | bytes 2752520 | tf_op jit(solution)/shard_map/cond/branch_4_fun/ppermute | solution.py:424
  70.4 2.4 %own.13 = (f32[61,16384]{1,0:T(8,128)}, f32[2,16384]{1,0:T(2,128)}, s32[1]{0:T(128)}) custom-call(s32[384]{0:T(512)S(4)} %get-tuple-element.144.table, f32[4,56,8,128]{3,2,1,0:T(8,128)S(1)} %all_to_all.92.own, f32[2,128,128]{2,1,0:T(8,128)S(1)} %get-tuple-element.146.sq0, f32[2,128,128]{2,1,0:T(8,128)S(1)} %get-tuple-element.147.sq1, ...), custom_call_target="tpu_custom_call" | custom-call | tf_op jit(solution)/shard_map/cond/branch_4_fun/own/pallas_call | solution.py:425
  72.7 0.0 collective-permute-done.4.other
  72.8 1.0 %other.13 = f32[61,16384]{1,0:T(8,128)} custom-call(s32[384]{0:T(512)S(4)} %get-tuple-element.144.table, f32[4,56,8,128]{3,2,1,0:T(8,128)S(1)} %collective-permute-done.4.other, f32[61,16384]{1,0:T(8,128)} %get-tuple-element.151.begun), custom_call_target="tpu_custom_call", output_to_operand_aliasing={{}: (2, {})} | custom-call | tf_op jit(solution)/shard_map/cond/branch_4_fun/other/pallas_call | solution.py:444
  (2 shorter events, 0.0 us)
Async XLA Ops:
  4.2 4.3 %collective-permute-start.9 = (f32[2,128,128]{2,1,0:T(8,128)S(1)}, f32[2,128,128]{2,1,0:T(8,128)S(1)}, u32[]{:S(2)}, u32[]{:S(2)}) collective-permute-start(f32[2,128,128]{2,1,0:T(8,128)S(1)} %views.1), channel_id=1, source_target_pairs={{0,32},{32,0},{64,96},{96,64},{128,160},{160,128},{192,224},{224,1... | collective-permute-start | bytes 393224 | tf_op jit(solution)/shard_map/ppermute | solution.py:354
  8.5 26.7 %collective-permute-start.12 = (f32[2,128,128]{2,1,0:T(8,128)S(1)}, f32[2,128,128]{2,1,0:T(8,128)S(1)}, u32[]{:S(2)}, u32[]{:S(2)}) collective-permute-start(f32[2,128,128]{2,1,0:T(8,128)S(1)} %max.3.sq0), channel_id=1, source_target_pairs={{0,192},{32,224},{64,0},{96,32},{128,64},{160,96},{192,128},{224,1... | collective-permute-start | bytes 393224 | tf_op jit(solution)/shard_map/ppermute | solution.py:358
  9.3 25.9 %collective-permute-start.11 = (f32[2,128,128]{2,1,0:T(8,128)S(1)}, f32[2,128,128]{2,1,0:T(8,128)S(1)}, u32[]{:S(2)}, u32[]{:S(2)}) collective-permute-start(f32[2,128,128]{2,1,0:T(8,128)S(1)} %max.3.sq0), channel_id=1, source_target_pairs={{0,128},{32,160},{64,192},{96,224},{128,0},{160,32},{192,64},{224,... | collective-permute-start | bytes 393224 | tf_op jit(solution)/shard_map/ppermute | solution.py:358
  9.8 25.4 %collective-permute-start.10 = (f32[2,128,128]{2,1,0:T(8,128)S(1)}, f32[2,128,128]{2,1,0:T(8,128)S(1)}, u32[]{:S(2)}, u32[]{:S(2)}) collective-permute-start(f32[2,128,128]{2,1,0:T(8,128)S(1)} %max.3.sq0), channel_id=1, source_target_pairs={{0,64},{32,96},{64,128},{96,160},{128,192},{160,224},{192,0},{224,... | collective-permute-start | bytes 393224 | tf_op jit(solution)/shard_map/ppermute | solution.py:358
  12.0 19.8 %all-to-all-start.18 = ((s32[32,1,128]{2,1,0:T(1,128)}), s32[32,1,128]{2,1,0:T(1,128)S(1)}, u32[]{:S(2)}, u32[]{:S(2)}) async-start(s32[32,1,128]{2,1,0:T(1,128)} %bitcast.22), calls=%async_computation.18 | async-start | bytes 32768 | tf_op jit(solution)/shard_map/all_to_all | solution.py:343
  63.9 8.8 %collective-permute-start.4 = (f32[4,56,8,128]{3,2,1,0:T(8,128)S(1)}, f32[4,56,8,128]{3,2,1,0:T(8,128)S(1)}, u32[]{:S(2)}, u32[]{:S(2)}) collective-permute-start(f32[4,56,8,128]{3,2,1,0:T(8,128)S(1)} %all_to_all.92.own), channel_id=1, source_target_pairs={{0,32},{32,0},{64,96},{96,64},{128,160},{160,128},{192,224},{224,1... | collective-permute-start | bytes 2752520 | tf_op jit(solution)/shard_map/cond/branch_4_fun/ppermute | solution.py:424

commit v10 on v9

--- a/solution.py
+++ b/solution.py
@@ -200,14 +200,19 @@
     return jnp.maximum(jnp.maximum(a, b), jnp.maximum(c, d))
 
 
-def add_kernel(table, index, sq0, sq1, sq2, sq3, filled, out_ref, pairs):
+def add_kernel(table, index, sq0, sq1, sq2, sq3, filled, out_ref, top_ref, pairs):
+    for g in range(BLOCKS // 8):
+        at = slice(8 * g, 8 * g + 8)
+        for k in range(2):
+            top_ref[k, at, :] = top_of((sq0, sq1, sq2, sq3), k, at)
+
     @pl.when(table[2 * BLOCKS] == 7)
     def _():
         for g in range(BLOCKS // 8):
             at = slice(8 * g, 8 * g + 8)
             lanes = index[at, :] & (LANES - 1)
             for k in range(2):
-                root = jnp.sqrt(top_of((sq0, sq1, sq2, sq3), k, at))
+                root = jnp.sqrt(top_ref[k, at, :])
                 pairs[pl.ds(16 * g + k, 8, stride=2), :] = jnp.take_along_axis(
                     root if k == 0 else 3.0 * root, lanes, axis=1, mode="promise_in_bounds"
                 )
@@ -239,10 +244,7 @@
     )
 
 
-def own_kernel(
-    table, own, sq0, sq1, sq2, sq3,
-    out_ref, peak_ref, total_ref, buf, zeros, pairs, peaks, sems
-):
+def own_kernel(table, own, out_ref, total_ref, buf, zeros, sems):
     cap = own.shape[1]
     core = table[2 * BLOCKS] & 1
     total_ref[0] = table[2 * BLOCKS + 1]
@@ -269,17 +271,6 @@
                     buf[r, :, i * LANES : (i + 1) * LANES] = own[r // 2, i]
                 row_copy(buf, out_ref, sems, r, slice(0, cap * LANES)).start()
 
-    for g in range(BLOCKS // 8):
-        at = slice(8 * g, 8 * g + 8)
-        norm = jnp.sqrt(top_of((sq0, sq1, sq2, sq3), 0, at))
-        radius = 3.0 * jnp.sqrt(top_of((sq0, sq1, sq2, sq3), 1, at))
-        pairs[pl.ds(16 * g, 8, stride=2), :] = norm
-        pairs[pl.ds(16 * g + 1, 8, stride=2), :] = radius
-    for b in range(BLOCKS):
-        peaks[:, b * LANES : (b + 1) * LANES] = pairs[2 * b : 2 * b + 2, :]
-    peak_copy = pltpu.make_async_copy(peaks, peak_ref, sems.at[16])
-    peak_copy.start()
-
     for half in range(2):
 
         @pl.when(core == half)
@@ -290,10 +281,11 @@
     if cap < BLOCKS:
         for r in range(8):
             clear(r).wait()
-    peak_copy.wait()
-
-
-def other_kernel(table, other, begun, out_ref, buf, sems):
+
+
+def other_kernel(
+    table, other, top, mate, begun, out_ref, peak_ref, buf, pairs, peaks, sems
+):
     cap = other.shape[1]
     core = table[2 * BLOCKS] & 1
     for half in range(2):
@@ -304,8 +296,26 @@
                 for i in range(cap):
                     buf[r, :, i * LANES : (i + 1) * LANES] = other[r // 2, i]
                 row_copy(buf, out_ref, sems, r, slice(0, cap * LANES)).start()
+
+    for g in range(BLOCKS // 8):
+        at = slice(8 * g, 8 * g + 8)
+        norm = jnp.sqrt(jnp.maximum(top[0, at, :], mate[0, at, :]))
+        radius = 3.0 * jnp.sqrt(jnp.maximum(top[1, at, :], mate[1, at, :]))
+        pairs[pl.ds(16 * g, 8, stride=2), :] = norm
+        pairs[pl.ds(16 * g + 1, 8, stride=2), :] = radius
+    for b in range(BLOCKS):
+        peaks[:, b * LANES : (b + 1) * LANES] = pairs[2 * b : 2 * b + 2, :]
+    peak_copy = pltpu.make_async_copy(peaks, peak_ref, sems.at[8])
+    peak_copy.start()
+
+    for half in range(2):
+
+        @pl.when(core == half)
+        def _():
             for r in range(1 - half, 8, 2):
                 row_copy(buf, out_ref, sems, r, slice(0, cap * LANES)).wait()
+
+    peak_copy.wait()
 
 
 def smem():
@@ -354,7 +364,7 @@
     other = lax.ppermute(squares, "view", [(v, v ^ 1) for v in range(8)])
     squares = [jnp.maximum(squares, other)]
     for k in (1, 2, 3):
-        pairs = [(v, (v + 2 * k) % 8) for v in range(8)]
+        pairs = [(v, (v + 2 * k) % 8) for v in (1, 3, 5, 7)]
         squares.append(lax.ppermute(squares[0], "view", pairs))
 
     start, index = pl.pallas_call(
@@ -394,11 +404,11 @@
         compiler_params=LIMIT,
         name="fill",
     )(where, counts, start, index, means, scales, quats, attrs, attrs)
-    outgoing = pl.pallas_call(
+    outgoing, top = pl.pallas_call(
         add_kernel,
         in_specs=[smem()] + [vmem()] * 6,
-        out_specs=vmem(),
-        out_shape=VMEM((BLOCKS, 8, LANES), f32),
+        out_specs=[vmem()] * 2,
+        out_shape=[VMEM((BLOCKS, 8, LANES), f32), VMEM((2, BLOCKS, LANES), f32)],
         input_output_aliases={6: 0},
         scratch_shapes=[pltpu.VMEM((2 * BLOCKS + 32, LANES), f32)],
         compiler_params=LIMIT,
@@ -406,7 +416,7 @@
     )(table, index, *squares, filled)
 
     def gather(cap):
-        def go(table, outgoing, *squares):
+        def go(table, outgoing, top):
             arrived = lax.all_to_all(
                 outgoing.reshape(SHARDS, PER, 8, LANES), "gauss", 0, 0, tiled=True
             ).reshape(BLOCKS, 8, LANES)
@@ -421,45 +431,49 @@
             )(table, arrived)
             cores = [[0, 2, 4, 6], [1, 3, 5, 7]]
             own = lax.all_to_all(piece, "view", 0, 0, axis_index_groups=cores, tiled=True)
+            mate = lax.ppermute(top, "view", [(1, 0), (3, 2), (5, 4), (7, 6)])
+            own, mate = lax.optimization_barrier((own, mate))
             other = lax.ppermute(own, "view", [(v, v ^ 1) for v in range(8)])
-            begun, peak, total = pl.pallas_call(
+            begun, total = pl.pallas_call(
                 own_kernel,
-                in_specs=[smem()] + [vmem()] * 5,
-                out_specs=[pl.BlockSpec(memory_space=pl.ANY)] * 2 + [smem()],
+                in_specs=[smem(), vmem()],
+                out_specs=[pl.BlockSpec(memory_space=pl.ANY), smem()],
                 out_shape=[
                     jax.ShapeDtypeStruct((ROWS, G_DEV), f32),
-                    pltpu.MemorySpace.HBM((2, G_DEV), f32),
                     pltpu.MemorySpace.HBM((1,), i32),
                 ],
                 scratch_shapes=[
                     pltpu.VMEM((8, 8, cap * LANES), f32),
                     pltpu.VMEM((8, max(BLOCKS - cap, 1) * LANES), f32),
-                    pltpu.VMEM((2 * BLOCKS + 32, LANES), f32),
-                    pltpu.VMEM((2, G_DEV), f32),
-                    pltpu.SemaphoreType.DMA((17,)),
+                    pltpu.SemaphoreType.DMA((16,)),
                 ],
                 compiler_params=LIMIT,
                 name="own",
-            )(table, own, *squares)
-            clones = pl.pallas_call(
+            )(table, own)
+            clones, peak = pl.pallas_call(
                 other_kernel,
-                in_specs=[smem(), vmem(), pl.BlockSpec(memory_space=pl.ANY)],
-                out_specs=pl.BlockSpec(memory_space=pl.ANY),
-                out_shape=jax.ShapeDtypeStruct((ROWS, G_DEV), f32),
-                input_output_aliases={2: 0},
+                in_specs=[smem(), vmem(), vmem(), vmem(), pl.BlockSpec(memory_space=pl.ANY)],
+                out_specs=[pl.BlockSpec(memory_space=pl.ANY)] * 2,
+                out_shape=[
+                    jax.ShapeDtypeStruct((ROWS, G_DEV), f32),
+                    pltpu.MemorySpace.HBM((2, G_DEV), f32),
+                ],
+                input_output_aliases={4: 0},
                 scratch_shapes=[
                     pltpu.VMEM((8, 8, cap * LANES), f32),
-                    pltpu.SemaphoreType.DMA((8,)),
+                    pltpu.VMEM((2 * BLOCKS + 32, LANES), f32),
+                    pltpu.VMEM((2, G_DEV), f32),
+                    pltpu.SemaphoreType.DMA((9,)),
                 ],
                 compiler_params=LIMIT,
                 name="other",
-            )(table, other, begun)
+            )(table, other, top, mate, begun)
             return peak, clones, total
 
         return go
 
     peak, clones, total = lax.switch(
-        branch[0], [gather(cap) for cap in CAPS], table, outgoing, *squares
+        branch[0], [gather(cap) for cap in CAPS], table, outgoing, top
     )
     return (peak, clones, total[0])
 

time: 75.2 us -> 76.7 us (1.020)
  blocking collectives: 28.4 us -> 15.6 us
  waiting for transfers between devices: 7.93 us -> 16.5 us
  starting transfers between devices: 22.9 us -> 27.2 us
  Pallas kernels: 13.7 us -> 14.6 us
    all_to_all x1 -> x0, blocking collectives: 12.8 us -> none  [go(): lax.all_to_all(piece, 'view', 0, 0, axis_index_groups=cores, tiled=True)]
    all_to_all x0 -> x1, waiting for transfers between devices: none -> 7.43 us  [go(): lax.all_to_all(piece, 'view', 0, 0, axis_index_groups=cores, tiled=True)]
    ppermute x1, starting transfers between devices: 6.45 us -> 0.01 us  [go(): other = lax.ppermute(own, 'view', [(v, v ^ 1) for v in range(8)])]
    ppermute x3, starting transfers between devices: 1.97 us -> 7.62 us  [body(): squares.append(lax.ppermute(squares[0], 'view', pairs))]
    all_to_all x0 -> x1, starting transfers between devices: none -> 3.75 us  [go(): lax.all_to_all(piece, 'view', 0, 0, axis_index_groups=cores, tiled=True)]
    ppermute x0 -> x1, starting transfers between devices: none -> 1.29 us  [go(): mate = lax.ppermute(top, 'view', [(1, 0), (3, 2), (5, 4), (7, 6)])]
    ppermute x0 -> x1, waiting for transfers between devices: none -> 0.96 us  [go(): mate = lax.ppermute(top, 'view', [(1, 0), (3, 2), (5, 4), (7, 6)])]
    pallas_call x1, Pallas kernels: 0.26 us -> 1.18 us  [go(): pl.pallas_call(place_kernel, in_specs=[smem(), vmem()], out_specs=vmem(),...]
  transfers between devices with their start and end apart: 6 -> 8, of which waited for: 2 -> 5; matrix products, arithmetic and copies ran while one was open for 0% -> 0% of each run, Pallas kernels for 12% -> 12%
where the time goes in v10:
time: 76.7 us; the launch traced here: 75.3 us
  starting transfers between devices  27.2 us (35%)
  waiting for transfers between devices  16.5 us (22%)
  blocking collectives  15.6 us (20%)
  Pallas kernels  14.6 us (19%)
  between operations  0.91 us (1%)
    all_to_all x1, blocking collectives, go(): lax.all_to_all(outgoing.reshape(SHARDS, PER, 8, LANES), 'gauss', 0, 0, ti...  15.6 us
    all_to_all x1, starting transfers between devices, body(): counts = lax.all_to_all(count, 'gauss', 0, 0, tiled=True)  11.2 us
    ppermute x3, starting transfers between devices, body(): squares.append(lax.ppermute(squares[0], 'view', pairs))  7.62 us
    all_to_all x1, waiting for transfers between devices, go(): lax.all_to_all(piece, 'view', 0, 0, axis_index_groups=cores, tiled=True)  7.43 us
    all_to_all x1, waiting for transfers between devices, body(): counts = lax.all_to_all(count, 'gauss', 0, 0, tiled=True)  6.93 us
    all_to_all x1, starting transfers between devices, go(): lax.all_to_all(piece, 'view', 0, 0, axis_index_groups=cores, tiled=True)  3.75 us
    pallas_call x1, Pallas kernels, body(): pl.pallas_call(view_kernel, in_specs=[smem()] * 3 + [vmem()] * 5, out_spe...  3.53 us
    pallas_call x1, Pallas kernels, body(): pl.pallas_call(fill_kernel, grid_spec=pltpu.PrefetchScalarGridSpec(num_sc...  3.4 us
  transfers between devices with their start and end apart: 8, of which 5 were waited for; matrix products, arithmetic and copies ran while one was open for 0% of the time, Pallas kernels for 12%

profile of v10, /device:TPU:1, one launch (start us, length us, event | category | flops | bytes accessed | tf_op | source)
XLA Modules:
  0.0 75.3 jit_solution(2621365104332100334)
XLA Ops:
  0.6 3.5 %views.1 = f32[2,128,128]{2,1,0:T(8,128)S(1)} custom-call(f32[3,4,3]{2,1,0:T(4,128)} %bitcast.50, f32[4,3]{1,0:T(4,128)} %trans.1, f32[1,4]{1,0:T(1,128)} %bitcast.51, f32[3,16384]{1,0:T(4,128)} %means.3, f32[3,16384]{1,0:T(4,128)} %scales.3, f32[4,16384]{1,0:T(4,128)} %quats.3, f32[4,2,16384]{2,1,0:T(2,128)} %grad.1, s32[4,16384]{1,0:T(4,128)} %seen.1), custom_call_target="tpu_custom_call" | custom-call | tf_op jit(solution)/shard_map/views/pallas_call | solution.py:355
  4.2 3.3 %collective-permute-start.18 = (f32[2,128,128]{2,1,0:T(8,128)S(1)}, f32[2,128,128]{2,1,0:T(8,128)S(1)}, u32[]{:S(2)}, u32[]{:S(2)}) collective-permute-start(f32[2,128,128]{2,1,0:T(8,128)S(1)} %views.1), channel_id=1, source_target_pairs={{0,32},{32,0},{64,96},{96,64},{128,160},{160,128},{192,224},{224,1... | collective-permute-start | bytes 393224 | tf_op jit(solution)/shard_map/ppermute | solution.py:364
  7.5 1.0 %collective-permute-done.18 = f32[2,128,128]{2,1,0:T(8,128)S(1)} collective-permute-done((f32[2,128,128]{2,1,0:T(8,128)S(1)}, f32[2,128,128]{2,1,0:T(8,128)S(1)}, u32[]{:S(2)}, u32[]{:S(2)}) %collective-permute-start.18) | collective-permute-done | bytes 131104 | tf_op jit(solution)/shard_map/ppermute | solution.py:364
  8.5 2.7 %collective-permute-start.21 = (f32[2,128,128]{2,1,0:T(8,128)S(1)}, f32[2,128,128]{2,1,0:T(8,128)S(1)}, u32[]{:S(2)}, u32[]{:S(2)}) collective-permute-start(f32[2,128,128]{2,1,0:T(8,128)S(1)} %max.3.sq0), channel_id=1, source_target_pairs={{32,224},{96,32},{160,96},{224,160},{33,225},{97,33},{161,97},{225... | collective-permute-start | bytes 393224 | tf_op jit(solution)/shard_map/ppermute | solution.py:368
  11.1 2.4 %collective-permute-start.20 = (f32[2,128,128]{2,1,0:T(8,128)S(1)}, f32[2,128,128]{2,1,0:T(8,128)S(1)}, u32[]{:S(2)}, u32[]{:S(2)}) collective-permute-start(f32[2,128,128]{2,1,0:T(8,128)S(1)} %max.3.sq0), channel_id=1, source_target_pairs={{32,160},{96,224},{160,32},{224,96},{33,161},{97,225},{161,33},{22... | collective-permute-start | bytes 393224 | tf_op jit(solution)/shard_map/ppermute | solution.py:368
  13.6 2.5 %collective-permute-start.19 = (f32[2,128,128]{2,1,0:T(8,128)S(1)}, f32[2,128,128]{2,1,0:T(8,128)S(1)}, u32[]{:S(2)}, u32[]{:S(2)}) collective-permute-start(f32[2,128,128]{2,1,0:T(8,128)S(1)} %max.3.sq0), channel_id=1, source_target_pairs={{32,96},{96,160},{160,224},{224,32},{33,97},{97,161},{161,225},{22... | collective-permute-start | bytes 393224 | tf_op jit(solution)/shard_map/ppermute | solution.py:368
  16.1 1.5 %count.1 = s32[32,128]{1,0:T(8,128)} custom-call(s32[128,128]{1,0:T(8,128)} %bitcast.48), custom_call_target="tpu_custom_call" | custom-call | tf_op jit(solution)/shard_map/count/pallas_call | solution.py:345
  17.6 11.2 %all-to-all-start.18 = ((s32[32,1,128]{2,1,0:T(1,128)}), s32[32,1,128]{2,1,0:T(1,128)S(1)}, u32[]{:S(2)}, u32[]{:S(2)}) async-start(s32[32,1,128]{2,1,0:T(1,128)} %bitcast.22), calls=%async_computation.18 | async-start | bytes 32768 | tf_op jit(solution)/shard_map/all_to_all | solution.py:353
  28.9 0.1 pad_add_fusion.where
  28.9 1.6 %index.1 = (s32[8,128]{1,0:T(8,128)S(1)}, s32[128,128]{1,0:T(8,128)S(1)}) custom-call(s32[128,128]{1,0:T(8,128)} %bitcast.49), custom_call_target="tpu_custom_call" | custom-call | tf_op jit(solution)/shard_map/index/pallas_call | solution.py:370
  30.5 6.9 %all-to-all-done.18 = s32[32,1,128]{2,1,0:T(1,128)S(1)} async-done(((s32[32,1,128]{2,1,0:T(1,128)}), s32[32,1,128]{2,1,0:T(1,128)S(1)}, u32[]{:S(2)}, u32[]{:S(2)}) %all-to-all-start.18) | async-done | bytes 16416 | tf_op jit(solution)/shard_map/all_to_all | solution.py:353
  37.4 3.4 %fill.1 = (f32[128,8,128]{2,1,0:T(8,128)S(1)}, s32[1]{0:T(128)S(4)}, s32[384]{0:T(512)S(4)}) custom-call(s32[2]{0:T(128)S(1)} %pad_add_fusion.where, s32[32,128]{1,0:T(8,128)S(1)} %bitcast.47, s32[8,128]{1,0:T(8,128)S(1)} %get-tuple-element.148.start, s32[128,128]{1,0:T(8,128)S(1)} %get-tuple-element.149.index, f32[3,16384]{1,0:T(4,128)} %means.3, ...), custom_call_target="tpu_custom_call" | custom-call | tf_op jit(solution)/shard_map/fill/pallas_call | solution.py:381
  40.9 0.0 collective-permute-done.21.sq3
  40.9 0.0 collective-permute-done.20.sq2
  40.9 0.0 collective-permute-done.19.sq1
  40.9 34.2 %conditional.1 = (f32[2,16384]{1,0:T(2,128)}, f32[61,16384]{1,0:T(8,128)}, s32[1]{0:T(128)}) conditional(s32[]{:T(128)} %bitcast.24, (f32[128,8,128]{2,1,0:T(8,128)S(1)}, s32[384]{0:T(512)S(4)}, f32[2,128,128]{2,1,0:T(8,128)S(1)}) %tuple.53, (f32[128,8,128]{2,1,0:T(8,128)S(1)}, s32[384]{0:T(512)S(4)}, ...), branch_computations={%region_0.0_spmd, %region_1.0_spmd, %region_2.0_spmd, %region_3.0_... | conditional | bytes 24641700 | solution.py:475
  41.0 15.6 %all_to_all.87 = f32[32,4,8,128]{3,2,1,0:T(8,128)S(1)} all-to-all(f32[32,4,8,128]{3,2,1,0:T(8,128)S(1)} %bitcast.33), channel_id=1, replica_groups=mesh['view'=8,'gauss'=32] {'gauss'}, dimensions={0} | all-to-all | bytes 1048576 | tf_op jit(solution)/shard_map/cond/branch_4_fun/all_to_all | solution.py:420
  56.6 1.2 %place.13 = f32[4,56,8,128]{3,2,1,0:T(8,128)} custom-call(s32[384]{0:T(512)S(4)} %get-tuple-element.90.table, f32[128,8,128]{2,1,0:T(8,128)S(1)} %bitcast.43), custom_call_target="tpu_custom_call" | custom-call | tf_op jit(solution)/shard_map/cond/branch_4_fun/place/pallas_call | solution.py:423
  57.8 3.8 %all-to-all-start.9 = ((f32[4,56,8,128]{3,2,1,0:T(8,128)}), f32[4,56,8,128]{3,2,1,0:T(8,128)S(1)}, u32[]{:S(2)}, u32[]{:S(2)}) async-start(f32[4,56,8,128]{3,2,1,0:T(8,128)} %place.13), calls=%async_computation.9 | async-start | bytes 1835008 | tf_op jit(solution)/shard_map/cond/branch_4_fun/all_to_all | solution.py:433
  61.5 1.3 %collective-permute-start.8 = (f32[2,128,128]{2,1,0:T(8,128)S(1)}, f32[2,128,128]{2,1,0:T(8,128)S(1)}, u32[]{:S(2)}, u32[]{:S(2)}) collective-permute-start(f32[2,128,128]{2,1,0:T(8,128)S(1)} %get-tuple-element.92.top), channel_id=1, source_target_pairs={{32,0},{96,64},{160,128},{224,192},{33,1},{97,65},{161,129},{225,1... | collective-permute-start | bytes 393224 | tf_op jit(solution)/shard_map/cond/branch_4_fun/ppermute | solution.py:434
  62.8 1.0 %collective-permute-done.8.mate = f32[2,128,128]{2,1,0:T(8,128)S(1)} collective-permute-done((f32[2,128,128]{2,1,0:T(8,128)S(1)}, f32[2,128,128]{2,1,0:T(8,128)S(1)}, u32[]{:S(2)}, u32[]{:S(2)}) %collective-permute-start.8) | collective-permute-done | bytes 131104 | tf_op jit(solution)/shard_map/cond/branch_4_fun/ppermute | solution.py:434
  63.8 7.4 %all-to-all-done.9.own = f32[4,56,8,128]{3,2,1,0:T(8,128)S(1)} async-done(((f32[4,56,8,128]{3,2,1,0:T(8,128)}), f32[4,56,8,128]{3,2,1,0:T(8,128)S(1)}, u32[]{:S(2)}, u32[]{:S(2)}) %all-to-all-start.9) | async-done | bytes 917536 | tf_op jit(solution)/shard_map/cond/branch_4_fun/all_to_all | solution.py:433
  71.2 0.0 collective-permute-start.9
  71.2 2.3 %own.13 = (f32[61,16384]{1,0:T(8,128)}, s32[1]{0:T(128)}) custom-call(s32[384]{0:T(512)S(4)} %get-tuple-element.90.table, f32[4,56,8,128]{3,2,1,0:T(8,128)S(1)} %all-to-all-done.9.own), custom_call_target="tpu_custom_call" | custom-call | tf_op jit(solution)/shard_map/cond/branch_4_fun/own/pallas_call | solution.py:437
  73.5 0.1 collective-permute-done.9.other
  73.7 1.1 %other.13 = (f32[61,16384]{1,0:T(8,128)}, f32[2,16384]{1,0:T(2,128)}) custom-call(s32[384]{0:T(512)S(4)} %get-tuple-element.90.table, f32[4,56,8,128]{3,2,1,0:T(8,128)S(1)} %collective-permute-done.9.other, f32[2,128,128]{2,1,0:T(8,128)S(1)} %get-tuple-element.92.top, ...), custom_call_target="tpu_custom_call", output_to_operand_aliasing={{0}: (4, {})} | custom-call | tf_op jit(solution)/shard_map/cond/branch_4_fun/other/pallas_call | solution.py:453
  (2 shorter events, 0.0 us)
Async XLA Ops:
  4.2 4.3 %collective-permute-start.18 = (f32[2,128,128]{2,1,0:T(8,128)S(1)}, f32[2,128,128]{2,1,0:T(8,128)S(1)}, u32[]{:S(2)}, u32[]{:S(2)}) collective-permute-start(f32[2,128,128]{2,1,0:T(8,128)S(1)} %views.1), channel_id=1, source_target_pairs={{0,32},{32,0},{64,96},{96,64},{128,160},{160,128},{192,224},{224,1... | collective-permute-start | bytes 393224 | tf_op jit(solution)/shard_map/ppermute | solution.py:364
  8.5 32.4 %collective-permute-start.21 = (f32[2,128,128]{2,1,0:T(8,128)S(1)}, f32[2,128,128]{2,1,0:T(8,128)S(1)}, u32[]{:S(2)}, u32[]{:S(2)}) collective-permute-start(f32[2,128,128]{2,1,0:T(8,128)S(1)} %max.3.sq0), channel_id=1, source_target_pairs={{32,224},{96,32},{160,96},{224,160},{33,225},{97,33},{161,97},{225... | collective-permute-start | bytes 393224 | tf_op jit(solution)/shard_map/ppermute | solution.py:368
  11.1 29.7 %collective-permute-start.20 = (f32[2,128,128]{2,1,0:T(8,128)S(1)}, f32[2,128,128]{2,1,0:T(8,128)S(1)}, u32[]{:S(2)}, u32[]{:S(2)}) collective-permute-start(f32[2,128,128]{2,1,0:T(8,128)S(1)} %max.3.sq0), channel_id=1, source_target_pairs={{32,160},{96,224},{160,32},{224,96},{33,161},{97,225},{161,33},{22... | collective-permute-start | bytes 393224 | tf_op jit(solution)/shard_map/ppermute | solution.py:368
  13.6 27.3 %collective-permute-start.19 = (f32[2,128,128]{2,1,0:T(8,128)S(1)}, f32[2,128,128]{2,1,0:T(8,128)S(1)}, u32[]{:S(2)}, u32[]{:S(2)}) collective-permute-start(f32[2,128,128]{2,1,0:T(8,128)S(1)} %max.3.sq0), channel_id=1, source_target_pairs={{32,96},{96,160},{160,224},{224,32},{33,97},{97,161},{161,225},{22... | collective-permute-start | bytes 393224 | tf_op jit(solution)/shard_map/ppermute | solution.py:368
  17.6 19.8 %all-to-all-start.18 = ((s32[32,1,128]{2,1,0:T(1,128)}), s32[32,1,128]{2,1,0:T(1,128)S(1)}, u32[]{:S(2)}, u32[]{:S(2)}) async-start(s32[32,1,128]{2,1,0:T(1,128)} %bitcast.22), calls=%async_computation.18 | async-start | bytes 32768 | tf_op jit(solution)/shard_map/all_to_all | solution.py:353
  57.8 13.4 %all-to-all-start.9 = ((f32[4,56,8,128]{3,2,1,0:T(8,128)}), f32[4,56,8,128]{3,2,1,0:T(8,128)S(1)}, u32[]{:S(2)}, u32[]{:S(2)}) async-start(f32[4,56,8,128]{3,2,1,0:T(8,128)} %place.13), calls=%async_computation.9 | async-start | bytes 1835008 | tf_op jit(solution)/shard_map/cond/branch_4_fun/all_to_all | solution.py:433
  61.5 2.3 %collective-permute-start.8 = (f32[2,128,128]{2,1,0:T(8,128)S(1)}, f32[2,128,128]{2,1,0:T(8,128)S(1)}, u32[]{:S(2)}, u32[]{:S(2)}) collective-permute-start(f32[2,128,128]{2,1,0:T(8,128)S(1)} %get-tuple-element.92.top), channel_id=1, source_target_pairs={{32,0},{96,64},{160,128},{224,192},{33,1},{97,65},{161,129},{225,1... | collective-permute-start | bytes 393224 | tf_op jit(solution)/shard_map/cond/branch_4_fun/ppermute | solution.py:434
  71.2 2.5 %collective-permute-start.9 = (f32[4,56,8,128]{3,2,1,0:T(8,128)S(1)}, f32[4,56,8,128]{3,2,1,0:T(8,128)S(1)}, u32[]{:S(2)}, u32[]{:S(2)}) collective-permute-start(f32[4,56,8,128]{3,2,1,0:T(8,128)S(1)} %all-to-all-done.9.own), channel_id=1, source_target_pairs={{0,32},{32,0},{64,96},{96,64},{128,160},{160,128},{192,224},{224,1... | collective-permute-start | bytes 2752520 | tf_op jit(solution)/shard_map/cond/branch_4_fun/ppermute | solution.py:436
